TPU v7x, 16 devices: a whole 2x2x2 slice. The times are simulated.
16 devices in a mesh: cp: 16 (over z, y, x, core).
Axes of the slice: x: 2, y: 2, z: 2, core: 2. Of those that a mesh axis runs over, the one named last changes fastest.
Arguments:
- query: bfloat16 [8, 1024, 16, 128], P(None, 'cp')
- key_in: bfloat16 [8, 1024, 16, 128], P(None, 'cp')
- value: bfloat16 [8, 1024, 16, 128], P(None, 'cp')
- bias_u: bfloat16 [16, 128], replicated
- bias_w: bfloat16 [16, 128], replicated
- rel_k: bfloat16 [1024, 16, 128], replicated
- d_out: bfloat16 [8, 1024, 16, 128], P(None, 'cp')
Outputs:
- output 1: bfloat16 [8, 1024, 16, 128], P(None, 'cp')
- output 2: bfloat16 [8, 1024, 16, 128], P(None, 'cp')
- output 3: bfloat16 [8, 1024, 16, 128], P(None, 'cp')
- output 4: bfloat16 [8, 1024, 16, 128], P(None, 'cp')
- output 5: float32 [16, 128], replicated
- output 6: float32 [16, 128], replicated
- output 7: float32 [1024, 16, 128], replicated
All inputs are finite; a program needn't handle non-finite values.
Results may differ from a plain program's by a relative error of at most 0.00858762.
Values are sent between devices in bfloat16 or wider.
A program may use at most 1 GiB of HBM per device.

v0:
```python
import jax
import jax.numpy as jnp
from jax import lax
from jax.sharding import PartitionSpec as P


def skew_rel(by_win, rows):
    lead_dims = by_win.shape[:-2]
    flattened = by_win.reshape(lead_dims + (2 * rows * rows,))
    flattened = flattened[..., rows - 1:rows - 1 + rows * (2 * rows - 1)]
    return flattened.reshape(lead_dims + (rows, 2 * rows - 1))[..., :rows]


def unskew_rel(d_rel, rows):
    lead_dims = d_rel.shape[:-2]
    pad_cfg = [(0, 0)] * len(lead_dims)
    widened = jnp.pad(d_rel, pad_cfg + [(0, 0), (0, rows - 1)])
    flattened = widened.reshape(lead_dims + (rows * (2 * rows - 1),))
    flattened = jnp.pad(flattened, pad_cfg + [(rows - 1, 1)])
    return flattened.reshape(lead_dims + (rows, 2 * rows))


def block_logits(q_u, q_w, key_blk, window, delta):
    rows = q_u.shape[1]
    inv_sqrt = q_u.shape[-1] ** -0.5
    content = jnp.einsum('bihd,bjhd->bhij', q_u, key_blk, preferred_element_type=jnp.float32)
    by_win = jnp.einsum('bihd,chd->bhic', q_w, window, preferred_element_type=jnp.float32)
    logits = (content + skew_rel(by_win, rows)) * inv_sqrt
    row_id = jnp.arange(rows)[:, None]
    col_id = jnp.arange(rows)[None, :]
    keep = (col_id <= row_id) | (delta > 0)
    return jnp.where(keep, logits, -jnp.inf)


def fwd_update(state, q_u, q_w, key_blk, val_blk, window, delta):
    row_max, row_sum, out_acc = state
    logits = block_logits(q_u, q_w, key_blk, window, delta)
    new_max = jnp.maximum(row_max, jnp.max(logits, axis=-1))
    rescale = jnp.exp(row_max - new_max)
    weights = jnp.exp(logits - new_max[..., None])
    row_sum = row_sum * rescale + jnp.sum(weights, axis=-1)
    out_acc = out_acc * jnp.swapaxes(rescale, 1, 2)[..., None] + jnp.einsum('bhij,bjhd->bihd', weights.astype(jnp.bfloat16), val_blk, preferred_element_type=jnp.float32)
    return new_max, row_sum, out_acc


def bwd_update(q_u, q_w, d_out, log_norm, row_dot, key_blk, val_blk, window, delta):
    rows = q_u.shape[1]
    inv_sqrt = q_u.shape[-1] ** -0.5
    logits = block_logits(q_u, q_w, key_blk, window, delta)
    weights = jnp.exp(logits - log_norm[..., None])
    weights_b = weights.astype(jnp.bfloat16)
    dv_new = jnp.einsum('bhij,bihd->bjhd', weights_b, d_out, preferred_element_type=jnp.float32)
    d_weights = jnp.einsum('bihd,bjhd->bhij', d_out, val_blk, preferred_element_type=jnp.float32)
    d_logit = (weights * (d_weights - row_dot[..., None]) * inv_sqrt).astype(jnp.bfloat16)
    dk_new = jnp.einsum('bhij,bihd->bjhd', d_logit, q_u, preferred_element_type=jnp.float32)
    dqc_new = jnp.einsum('bhij,bjhd->bihd', d_logit, key_blk, preferred_element_type=jnp.float32)
    d_wide = unskew_rel(d_logit, rows)
    dqr_new = jnp.einsum('bhic,chd->bihd', d_wide, window, preferred_element_type=jnp.float32)
    d_win = jnp.einsum('bhic,bihd->chd', d_wide, q_w, preferred_element_type=jnp.float32)
    return dk_new, dv_new, dqc_new, dqr_new, d_win


def solution(mesh):
    n_dev = mesh.shape['cp']
    shift_pairs = [(sender, (sender + 1) % n_dev) for sender in range(n_dev)]
    seq_spec = P(None, 'cp', None, None)

    def local(query, key_in, value, bias_u, bias_w, rel_k, d_out):
        n_batch, rows, n_heads, head_dim = query.shape
        my_idx = lax.axis_index('cp')
        q_u = (query.astype(jnp.float32) + bias_u.astype(jnp.float32)).astype(jnp.bfloat16)
        q_w = (query.astype(jnp.float32) + bias_w.astype(jnp.float32)).astype(jnp.bfloat16)
        rk_rev = jnp.concatenate([jnp.flip(rel_k, axis=0), jnp.zeros((rows, n_heads, head_dim), jnp.bfloat16)], axis=0)

        def window_at(delta):
            return lax.dynamic_slice_in_dim(rk_rev, (n_dev - 1 - delta) * rows, 2 * rows, 0)

        def fwd_visit(step, key_blk, val_blk, state):
            src_blk = (my_idx - step) % n_dev
            delta = my_idx - src_blk
            return lax.cond(src_blk <= my_idx,
                            lambda prev_state: fwd_update(prev_state, q_u, q_w, key_blk, val_blk, window_at(delta), delta),
                            lambda prev_state: prev_state, state)

        stat_shape = (n_batch, n_heads, rows)
        start_state = (jnp.full(stat_shape, -jnp.inf, jnp.float32), jnp.zeros(stat_shape, jnp.float32), jnp.zeros(query.shape, jnp.float32))
        first_state = fwd_visit(0, key_in, value, start_state)

        def fwd_body(step, carry):
            key_blk, val_blk, state = carry
            key_blk = lax.ppermute(key_blk, 'cp', shift_pairs)
            val_blk = lax.ppermute(val_blk, 'cp', shift_pairs)
            return key_blk, val_blk, fwd_visit(step, key_blk, val_blk, state)

        row_max, row_sum, out_acc = lax.fori_loop(1, n_dev, fwd_body, (key_in, value, first_state))[2]
        out_f32 = out_acc / jnp.swapaxes(row_sum, 1, 2)[..., None]
        log_norm = row_max + jnp.log(row_sum)
        row_dot = jnp.swapaxes(jnp.sum(d_out.astype(jnp.float32) * out_f32, axis=-1), 1, 2)

        def bwd_visit(step, grads):
            key_blk, val_blk, dk_blk, dv_blk, dq_cont, dq_rel, drk_rev = grads
            src_blk = (my_idx - step) % n_dev
            delta = my_idx - src_blk

            def visit(prev):
                dk_prev, dv_prev, dqc_prev, dqr_prev, drk_prev = prev
                dk_new, dv_new, dqc_new, dqr_new, d_win = bwd_update(q_u, q_w, d_out, log_norm, row_dot, key_blk, val_blk, window_at(delta), delta)
                start = (n_dev - 1 - delta) * rows
                win_old = lax.dynamic_slice_in_dim(drk_prev, start, 2 * rows, 0)
                drk_prev = lax.dynamic_update_slice_in_dim(drk_prev, win_old + d_win, start, 0)
                return (dk_prev + dk_new, dv_prev + dv_new, dqc_prev + dqc_new, dqr_prev + dqr_new, drk_prev)

            updated = lax.cond(src_blk <= my_idx, visit, lambda prev: prev, (dk_blk, dv_blk, dq_cont, dq_rel, drk_rev))
            return (key_blk, val_blk) + updated

        zeros_blk = jnp.zeros(query.shape, jnp.float32)
        grads = bwd_visit(0, (key_in, value, zeros_blk, zeros_blk, zeros_blk, zeros_blk, jnp.zeros(rk_rev.shape, jnp.float32)))

        def bwd_body(step, grads):
            moved = tuple(lax.ppermute(travel, 'cp', shift_pairs) for travel in grads[:4])
            return bwd_visit(step, moved + grads[4:])

        grads = lax.fori_loop(1, n_dev, bwd_body, grads)
        dk_home = lax.ppermute(grads[2], 'cp', shift_pairs)
        dv_home = lax.ppermute(grads[3], 'cp', shift_pairs)
        dq_cont, dq_rel, drk_rev = grads[4:]
        d_query = (dq_cont + dq_rel).astype(jnp.bfloat16)
        d_bias_u = lax.psum(jnp.sum(dq_cont, axis=(0, 1)), 'cp')
        d_bias_w = lax.psum(jnp.sum(dq_rel, axis=(0, 1)), 'cp')
        d_rel_k = lax.psum(jnp.flip(drk_rev[:rel_k.shape[0]], axis=0), 'cp')
        return (out_f32.astype(jnp.bfloat16), d_query, dk_home.astype(jnp.bfloat16), dv_home.astype(jnp.bfloat16), d_bias_u, d_bias_w, d_rel_k)

    return jax.shard_map(local, mesh=mesh,
                         in_specs=(seq_spec, seq_spec, seq_spec, P(), P(), P(), seq_spec),
                         out_specs=(seq_spec, seq_spec, seq_spec, seq_spec, P(), P(), P()),
                         check_vma=False)
```

profile of v0, /device:TPU:0, one launch (start us, length us, event | category | flops | bytes accessed | tf_op | source)
XLA Modules:
  0.0 5042.9 jit_solution(16327380720322295036)
XLA Ops:
  23.9 59.4 %rev.8 = bf16[1024,16,128]{2,0,1:T(8,128)(2,1)} reverse(bf16[1024,16,128]{2,0,1:T(8,128)(2,1)} %copy.102), dimensions={0} | reverse | bytes 8388608 | tf_op jit(solution)/shard_map/jit(_flip)/rev | solution.py:73
  132.0 1391.3 %while.50 = (s32[]{:T(128)}, bf16[8,64,16,128]{3,1,2,0:T(8,128)(2,1)}, bf16[8,64,16,128]{3,1,2,0:T(8,128)(2,1)}, f32[8,16,64]{2,1,0:T(8,128)}, f32[8,16,64]{2,1,...) while((s32[]{:T(128)}, ...), condition=%wide.region_9.10_spmd, body=%wide.region_4.9_spmd.sunk | while | flops 543195136 | bytes 84812328 | solution.py:95
  385.1 61.2 %collective-permute-done.1 = bf16[8,64,16,128]{3,1,2,0:T(8,128)(2,1)} collective-permute-done((bf16[8,64,16,128]{3,1,2,0:T(8,128)(2,1)}, bf16[8,64,16,128]{3,1,2,0:T(8,128)(2,1)}, u32[]{:S(2)}, u32[]{:S(2)}) %collective-permute-start.1) | collective-permute-done | bytes 2097184 | tf_op jit(solution)/shard_map/while/body/eval_jaxpr/ppermute | solution.py:92
  475.0 66.7 %collective-permute-done.1 = bf16[8,64,16,128]{3,1,2,0:T(8,128)(2,1)} collective-permute-done((bf16[8,64,16,128]{3,1,2,0:T(8,128)(2,1)}, bf16[8,64,16,128]{3,1,2,0:T(8,128)(2,1)}, u32[]{:S(2)}, u32[]{:S(2)}) %collective-permute-start.1) | collective-permute-done | bytes 2097184 | tf_op jit(solution)/shard_map/while/body/eval_jaxpr/ppermute | solution.py:92
  570.3 66.7 %collective-permute-done.1 = bf16[8,64,16,128]{3,1,2,0:T(8,128)(2,1)} collective-permute-done((bf16[8,64,16,128]{3,1,2,0:T(8,128)(2,1)}, bf16[8,64,16,128]{3,1,2,0:T(8,128)(2,1)}, u32[]{:S(2)}, u32[]{:S(2)}) %collective-permute-start.1) | collective-permute-done | bytes 2097184 | tf_op jit(solution)/shard_map/while/body/eval_jaxpr/ppermute | solution.py:92
  665.6 66.7 %collective-permute-done.1 = bf16[8,64,16,128]{3,1,2,0:T(8,128)(2,1)} collective-permute-done((bf16[8,64,16,128]{3,1,2,0:T(8,128)(2,1)}, bf16[8,64,16,128]{3,1,2,0:T(8,128)(2,1)}, u32[]{:S(2)}, u32[]{:S(2)}) %collective-permute-start.1) | collective-permute-done | bytes 2097184 | tf_op jit(solution)/shard_map/while/body/eval_jaxpr/ppermute | solution.py:92
  760.9 66.7 %collective-permute-done.1 = bf16[8,64,16,128]{3,1,2,0:T(8,128)(2,1)} collective-permute-done((bf16[8,64,16,128]{3,1,2,0:T(8,128)(2,1)}, bf16[8,64,16,128]{3,1,2,0:T(8,128)(2,1)}, u32[]{:S(2)}, u32[]{:S(2)}) %collective-permute-start.1) | collective-permute-done | bytes 2097184 | tf_op jit(solution)/shard_map/while/body/eval_jaxpr/ppermute | solution.py:92
  856.2 66.7 %collective-permute-done.1 = bf16[8,64,16,128]{3,1,2,0:T(8,128)(2,1)} collective-permute-done((bf16[8,64,16,128]{3,1,2,0:T(8,128)(2,1)}, bf16[8,64,16,128]{3,1,2,0:T(8,128)(2,1)}, u32[]{:S(2)}, u32[]{:S(2)}) %collective-permute-start.1) | collective-permute-done | bytes 2097184 | tf_op jit(solution)/shard_map/while/body/eval_jaxpr/ppermute | solution.py:92
  951.5 66.7 %collective-permute-done.1 = bf16[8,64,16,128]{3,1,2,0:T(8,128)(2,1)} collective-permute-done((bf16[8,64,16,128]{3,1,2,0:T(8,128)(2,1)}, bf16[8,64,16,128]{3,1,2,0:T(8,128)(2,1)}, u32[]{:S(2)}, u32[]{:S(2)}) %collective-permute-start.1) | collective-permute-done | bytes 2097184 | tf_op jit(solution)/shard_map/while/body/eval_jaxpr/ppermute | solution.py:92
  1046.8 66.7 %collective-permute-done.1 = bf16[8,64,16,128]{3,1,2,0:T(8,128)(2,1)} collective-permute-done((bf16[8,64,16,128]{3,1,2,0:T(8,128)(2,1)}, bf16[8,64,16,128]{3,1,2,0:T(8,128)(2,1)}, u32[]{:S(2)}, u32[]{:S(2)}) %collective-permute-start.1) | collective-permute-done | bytes 2097184 | tf_op jit(solution)/shard_map/while/body/eval_jaxpr/ppermute | solution.py:92
  1142.1 66.7 %collective-permute-done.1 = bf16[8,64,16,128]{3,1,2,0:T(8,128)(2,1)} collective-permute-done((bf16[8,64,16,128]{3,1,2,0:T(8,128)(2,1)}, bf16[8,64,16,128]{3,1,2,0:T(8,128)(2,1)}, u32[]{:S(2)}, u32[]{:S(2)}) %collective-permute-start.1) | collective-permute-done | bytes 2097184 | tf_op jit(solution)/shard_map/while/body/eval_jaxpr/ppermute | solution.py:92
  1237.4 66.7 %collective-permute-done.1 = bf16[8,64,16,128]{3,1,2,0:T(8,128)(2,1)} collective-permute-done((bf16[8,64,16,128]{3,1,2,0:T(8,128)(2,1)}, bf16[8,64,16,128]{3,1,2,0:T(8,128)(2,1)}, u32[]{:S(2)}, u32[]{:S(2)}) %collective-permute-start.1) | collective-permute-done | bytes 2097184 | tf_op jit(solution)/shard_map/while/body/eval_jaxpr/ppermute | solution.py:92
  1332.7 66.7 %collective-permute-done.1 = bf16[8,64,16,128]{3,1,2,0:T(8,128)(2,1)} collective-permute-done((bf16[8,64,16,128]{3,1,2,0:T(8,128)(2,1)}, bf16[8,64,16,128]{3,1,2,0:T(8,128)(2,1)}, u32[]{:S(2)}, u32[]{:S(2)}) %collective-permute-start.1) | collective-permute-done | bytes 2097184 | tf_op jit(solution)/shard_map/while/body/eval_jaxpr/ppermute | solution.py:92
  1428.0 66.7 %collective-permute-done.1 = bf16[8,64,16,128]{3,1,2,0:T(8,128)(2,1)} collective-permute-done((bf16[8,64,16,128]{3,1,2,0:T(8,128)(2,1)}, bf16[8,64,16,128]{3,1,2,0:T(8,128)(2,1)}, u32[]{:S(2)}, u32[]{:S(2)}) %collective-permute-start.1) | collective-permute-done | bytes 2097184 | tf_op jit(solution)/shard_map/while/body/eval_jaxpr/ppermute | solution.py:92
  1531.5 61.8 %conditional.5 = (f32[8,64,16,128]{3,1,2,0:T(8,128)}, f32[8,64,16,128]{3,1,2,0:T(8,128)}, f32[8,64,16,128]{3,1,2,0:T(8,128)}, f32[8,64,16,128]{3,1,0,2:T(8,128)}, f32[1088,16,128]{2,0,1:T(8,128)}) conditional(s32[]{:T(128)} %convert_element_type.79, () %tuple.85, (s32[]{:T(128)}, bf16[8,64,16,128]{3,1,0,2:T(8,128)(2,1)}, ...), branch_computations={%region_11.12_spmd, %region_12.13_spmd} | conditional | flops 1481121792 | bytes 159818048 | solution.py:113
  1593.4 3210.4 %while.51 = (s32[]{:T(128)}, bf16[8,64,16,128]{3,1,2,0:T(8,128)(2,1)}, bf16[8,64,16,128]{3,1,2,0:T(8,128)(2,1)}, f32[8,64,16,128]{3,1,2,0:T(8,128)}, f32[8,64,16...) while((s32[]{:T(128)}, ...), condition=%wide.region_16.17_spmd, body=%wide.region_13.16_spmd.sunk | while | flops 1485578240 | bytes 210608944 | solution.py:123
  1593.8 156.3 %collective-permute-done.3 = bf16[8,64,16,128]{3,1,2,0:T(8,128)(2,1)} collective-permute-done((bf16[8,64,16,128]{3,1,2,0:T(8,128)(2,1)}, bf16[8,64,16,128]{3,1,2,0:T(8,128)(2,1)}, u32[]{:S(2)}, u32[]{:S(2)}) %collective-permute-start.3) | collective-permute-done | bytes 2097184 | tf_op jit(solution)/shard_map/while/body/eval_jaxpr/ppermute | solution.py:120
  1785.4 180.3 %collective-permute-done.3 = bf16[8,64,16,128]{3,1,2,0:T(8,128)(2,1)} collective-permute-done((bf16[8,64,16,128]{3,1,2,0:T(8,128)(2,1)}, bf16[8,64,16,128]{3,1,2,0:T(8,128)(2,1)}, u32[]{:S(2)}, u32[]{:S(2)}) %collective-permute-start.3) | collective-permute-done | bytes 2097184 | tf_op jit(solution)/shard_map/while/body/eval_jaxpr/ppermute | solution.py:120
  2001.0 180.3 %collective-permute-done.3 = bf16[8,64,16,128]{3,1,2,0:T(8,128)(2,1)} collective-permute-done((bf16[8,64,16,128]{3,1,2,0:T(8,128)(2,1)}, bf16[8,64,16,128]{3,1,2,0:T(8,128)(2,1)}, u32[]{:S(2)}, u32[]{:S(2)}) %collective-permute-start.3) | collective-permute-done | bytes 2097184 | tf_op jit(solution)/shard_map/while/body/eval_jaxpr/ppermute | solution.py:120
  2216.5 180.3 %collective-permute-done.3 = bf16[8,64,16,128]{3,1,2,0:T(8,128)(2,1)} collective-permute-done((bf16[8,64,16,128]{3,1,2,0:T(8,128)(2,1)}, bf16[8,64,16,128]{3,1,2,0:T(8,128)(2,1)}, u32[]{:S(2)}, u32[]{:S(2)}) %collective-permute-start.3) | collective-permute-done | bytes 2097184 | tf_op jit(solution)/shard_map/while/body/eval_jaxpr/ppermute | solution.py:120
  2432.1 180.3 %collective-permute-done.3 = bf16[8,64,16,128]{3,1,2,0:T(8,128)(2,1)} collective-permute-done((bf16[8,64,16,128]{3,1,2,0:T(8,128)(2,1)}, bf16[8,64,16,128]{3,1,2,0:T(8,128)(2,1)}, u32[]{:S(2)}, u32[]{:S(2)}) %collective-permute-start.3) | collective-permute-done | bytes 2097184 | tf_op jit(solution)/shard_map/while/body/eval_jaxpr/ppermute | solution.py:120
  2647.7 180.3 %collective-permute-done.3 = bf16[8,64,16,128]{3,1,2,0:T(8,128)(2,1)} collective-permute-done((bf16[8,64,16,128]{3,1,2,0:T(8,128)(2,1)}, bf16[8,64,16,128]{3,1,2,0:T(8,128)(2,1)}, u32[]{:S(2)}, u32[]{:S(2)}) %collective-permute-start.3) | collective-permute-done | bytes 2097184 | tf_op jit(solution)/shard_map/while/body/eval_jaxpr/ppermute | solution.py:120
  2863.3 180.3 %collective-permute-done.3 = bf16[8,64,16,128]{3,1,2,0:T(8,128)(2,1)} collective-permute-done((bf16[8,64,16,128]{3,1,2,0:T(8,128)(2,1)}, bf16[8,64,16,128]{3,1,2,0:T(8,128)(2,1)}, u32[]{:S(2)}, u32[]{:S(2)}) %collective-permute-start.3) | collective-permute-done | bytes 2097184 | tf_op jit(solution)/shard_map/while/body/eval_jaxpr/ppermute | solution.py:120
  3078.9 180.3 %collective-permute-done.3 = bf16[8,64,16,128]{3,1,2,0:T(8,128)(2,1)} collective-permute-done((bf16[8,64,16,128]{3,1,2,0:T(8,128)(2,1)}, bf16[8,64,16,128]{3,1,2,0:T(8,128)(2,1)}, u32[]{:S(2)}, u32[]{:S(2)}) %collective-permute-start.3) | collective-permute-done | bytes 2097184 | tf_op jit(solution)/shard_map/while/body/eval_jaxpr/ppermute | solution.py:120
  3294.5 180.3 %collective-permute-done.3 = bf16[8,64,16,128]{3,1,2,0:T(8,128)(2,1)} collective-permute-done((bf16[8,64,16,128]{3,1,2,0:T(8,128)(2,1)}, bf16[8,64,16,128]{3,1,2,0:T(8,128)(2,1)}, u32[]{:S(2)}, u32[]{:S(2)}) %collective-permute-start.3) | collective-permute-done | bytes 2097184 | tf_op jit(solution)/shard_map/while/body/eval_jaxpr/ppermute | solution.py:120
  3510.1 180.3 %collective-permute-done.3 = bf16[8,64,16,128]{3,1,2,0:T(8,128)(2,1)} collective-permute-done((bf16[8,64,16,128]{3,1,2,0:T(8,128)(2,1)}, bf16[8,64,16,128]{3,1,2,0:T(8,128)(2,1)}, u32[]{:S(2)}, u32[]{:S(2)}) %collective-permute-start.3) | collective-permute-done | bytes 2097184 | tf_op jit(solution)/shard_map/while/body/eval_jaxpr/ppermute | solution.py:120
  3725.6 180.3 %collective-permute-done.3 = bf16[8,64,16,128]{3,1,2,0:T(8,128)(2,1)} collective-permute-done((bf16[8,64,16,128]{3,1,2,0:T(8,128)(2,1)}, bf16[8,64,16,128]{3,1,2,0:T(8,128)(2,1)}, u32[]{:S(2)}, u32[]{:S(2)}) %collective-permute-start.3) | collective-permute-done | bytes 2097184 | tf_op jit(solution)/shard_map/while/body/eval_jaxpr/ppermute | solution.py:120
  3941.2 180.4 %collective-permute-done.3 = bf16[8,64,16,128]{3,1,2,0:T(8,128)(2,1)} collective-permute-done((bf16[8,64,16,128]{3,1,2,0:T(8,128)(2,1)}, bf16[8,64,16,128]{3,1,2,0:T(8,128)(2,1)}, u32[]{:S(2)}, u32[]{:S(2)}) %collective-permute-start.3) | collective-permute-done | bytes 2097184 | tf_op jit(solution)/shard_map/while/body/eval_jaxpr/ppermute | solution.py:120
  4156.9 180.3 %collective-permute-done.3 = bf16[8,64,16,128]{3,1,2,0:T(8,128)(2,1)} collective-permute-done((bf16[8,64,16,128]{3,1,2,0:T(8,128)(2,1)}, bf16[8,64,16,128]{3,1,2,0:T(8,128)(2,1)}, u32[]{:S(2)}, u32[]{:S(2)}) %collective-permute-start.3) | collective-permute-done | bytes 2097184 | tf_op jit(solution)/shard_map/while/body/eval_jaxpr/ppermute | solution.py:120
  4372.4 180.4 %collective-permute-done.3 = bf16[8,64,16,128]{3,1,2,0:T(8,128)(2,1)} collective-permute-done((bf16[8,64,16,128]{3,1,2,0:T(8,128)(2,1)}, bf16[8,64,16,128]{3,1,2,0:T(8,128)(2,1)}, u32[]{:S(2)}, u32[]{:S(2)}) %collective-permute-start.3) | collective-permute-done | bytes 2097184 | tf_op jit(solution)/shard_map/while/body/eval_jaxpr/ppermute | solution.py:120
  4588.1 180.4 %collective-permute-done.3 = bf16[8,64,16,128]{3,1,2,0:T(8,128)(2,1)} collective-permute-done((bf16[8,64,16,128]{3,1,2,0:T(8,128)(2,1)}, bf16[8,64,16,128]{3,1,2,0:T(8,128)(2,1)}, u32[]{:S(2)}, u32[]{:S(2)}) %collective-permute-start.3) | collective-permute-done | bytes 2097184 | tf_op jit(solution)/shard_map/while/body/eval_jaxpr/ppermute | solution.py:120
  4843.1 161.5 %all-reduce.5 = (f32[16,128]{1,0:T(8,128)}, f32[16,128]{1,0:T(8,128)}) all-reduce(f32[16,128]{1,0:T(8,128)S(1)} %reduce_sum.46, f32[16,128]{1,0:T(8,128)S(1)} %reduce_sum.47), channel_id=1, replica_groups=mesh['cp'=16] {'cp'}, use_global_device_ids=true, to_apply=%region_18.19 | all-reduce | flops 4096 | bytes 32768 | tf_op jit(solution)/shard_map/psum | solution.py:128
  (367 shorter events, 1374.1 us)
Async XLA Ops:
  7.2 5018.0 %all-reduce.8.cloned.1.call-start = ((), (), s32[]{:S(2)}) async-start(), calls=%async_computation | async-start | bytes 16777216 | tf_op jit(solution)/shard_map/psum | solution.py:130
  1785.3 206.0 %collective-permute-start.5 = (f32[8,64,16,128]{3,1,2,0:T(8,128)}, f32[8,64,16,128]{3,1,2,0:T(8,128)}, u32[]{:S(2)}, u32[]{:S(2)}) collective-permute-start(f32[8,64,16,128]{3,1,2,0:T(8,128)} %get-tuple-element.1283), channel_id=1, source_target_pairs={{0,1},{1,2},{2,3},{3,4},{4,5},{5,6},{6,7},{7,8},{8,9},{9,10},{10,1... | collective-permute-start | bytes 12582920 | tf_op jit(solution)/shard_map/while/body/eval_jaxpr/ppermute | solution.py:120
  1785.3 206.0 %collective-permute-start.4 = (f32[8,64,16,128]{3,1,2,0:T(8,128)}, f32[8,64,16,128]{3,1,2,0:T(8,128)}, u32[]{:S(2)}, u32[]{:S(2)}) collective-permute-start(f32[8,64,16,128]{3,1,2,0:T(8,128)} %get-tuple-element.1282), channel_id=1, source_target_pairs={{0,1},{1,2},{2,3},{3,4},{4,5},{5,6},{6,7},{7,8},{8,9},{9,10},{10,1... | collective-permute-start | bytes 12582920 | tf_op jit(solution)/shard_map/while/body/eval_jaxpr/ppermute | solution.py:120
  2000.9 206.0 %collective-permute-start.5 = (f32[8,64,16,128]{3,1,2,0:T(8,128)}, f32[8,64,16,128]{3,1,2,0:T(8,128)}, u32[]{:S(2)}, u32[]{:S(2)}) collective-permute-start(f32[8,64,16,128]{3,1,2,0:T(8,128)} %get-tuple-element.1283), channel_id=1, source_target_pairs={{0,1},{1,2},{2,3},{3,4},{4,5},{5,6},{6,7},{7,8},{8,9},{9,10},{10,1... | collective-permute-start | bytes 12582920 | tf_op jit(solution)/shard_map/while/body/eval_jaxpr/ppermute | solution.py:120
  2000.9 206.0 %collective-permute-start.4 = (f32[8,64,16,128]{3,1,2,0:T(8,128)}, f32[8,64,16,128]{3,1,2,0:T(8,128)}, u32[]{:S(2)}, u32[]{:S(2)}) collective-permute-start(f32[8,64,16,128]{3,1,2,0:T(8,128)} %get-tuple-element.1282), channel_id=1, source_target_pairs={{0,1},{1,2},{2,3},{3,4},{4,5},{5,6},{6,7},{7,8},{8,9},{9,10},{10,1... | collective-permute-start | bytes 12582920 | tf_op jit(solution)/shard_map/while/body/eval_jaxpr/ppermute | solution.py:120
  2216.4 206.0 %collective-permute-start.5 = (f32[8,64,16,128]{3,1,2,0:T(8,128)}, f32[8,64,16,128]{3,1,2,0:T(8,128)}, u32[]{:S(2)}, u32[]{:S(2)}) collective-permute-start(f32[8,64,16,128]{3,1,2,0:T(8,128)} %get-tuple-element.1283), channel_id=1, source_target_pairs={{0,1},{1,2},{2,3},{3,4},{4,5},{5,6},{6,7},{7,8},{8,9},{9,10},{10,1... | collective-permute-start | bytes 12582920 | tf_op jit(solution)/shard_map/while/body/eval_jaxpr/ppermute | solution.py:120
  2216.4 206.0 %collective-permute-start.4 = (f32[8,64,16,128]{3,1,2,0:T(8,128)}, f32[8,64,16,128]{3,1,2,0:T(8,128)}, u32[]{:S(2)}, u32[]{:S(2)}) collective-permute-start(f32[8,64,16,128]{3,1,2,0:T(8,128)} %get-tuple-element.1282), channel_id=1, source_target_pairs={{0,1},{1,2},{2,3},{3,4},{4,5},{5,6},{6,7},{7,8},{8,9},{9,10},{10,1... | collective-permute-start | bytes 12582920 | tf_op jit(solution)/shard_map/while/body/eval_jaxpr/ppermute | solution.py:120
  2432.0 206.1 %collective-permute-start.5 = (f32[8,64,16,128]{3,1,2,0:T(8,128)}, f32[8,64,16,128]{3,1,2,0:T(8,128)}, u32[]{:S(2)}, u32[]{:S(2)}) collective-permute-start(f32[8,64,16,128]{3,1,2,0:T(8,128)} %get-tuple-element.1283), channel_id=1, source_target_pairs={{0,1},{1,2},{2,3},{3,4},{4,5},{5,6},{6,7},{7,8},{8,9},{9,10},{10,1... | collective-permute-start | bytes 12582920 | tf_op jit(solution)/shard_map/while/body/eval_jaxpr/ppermute | solution.py:120
  2432.0 206.1 %collective-permute-start.4 = (f32[8,64,16,128]{3,1,2,0:T(8,128)}, f32[8,64,16,128]{3,1,2,0:T(8,128)}, u32[]{:S(2)}, u32[]{:S(2)}) collective-permute-start(f32[8,64,16,128]{3,1,2,0:T(8,128)} %get-tuple-element.1282), channel_id=1, source_target_pairs={{0,1},{1,2},{2,3},{3,4},{4,5},{5,6},{6,7},{7,8},{8,9},{9,10},{10,1... | collective-permute-start | bytes 12582920 | tf_op jit(solution)/shard_map/while/body/eval_jaxpr/ppermute | solution.py:120
  2647.6 206.0 %collective-permute-start.5 = (f32[8,64,16,128]{3,1,2,0:T(8,128)}, f32[8,64,16,128]{3,1,2,0:T(8,128)}, u32[]{:S(2)}, u32[]{:S(2)}) collective-permute-start(f32[8,64,16,128]{3,1,2,0:T(8,128)} %get-tuple-element.1283), channel_id=1, source_target_pairs={{0,1},{1,2},{2,3},{3,4},{4,5},{5,6},{6,7},{7,8},{8,9},{9,10},{10,1... | collective-permute-start | bytes 12582920 | tf_op jit(solution)/shard_map/while/body/eval_jaxpr/ppermute | solution.py:120
  2647.6 206.0 %collective-permute-start.4 = (f32[8,64,16,128]{3,1,2,0:T(8,128)}, f32[8,64,16,128]{3,1,2,0:T(8,128)}, u32[]{:S(2)}, u32[]{:S(2)}) collective-permute-start(f32[8,64,16,128]{3,1,2,0:T(8,128)} %get-tuple-element.1282), channel_id=1, source_target_pairs={{0,1},{1,2},{2,3},{3,4},{4,5},{5,6},{6,7},{7,8},{8,9},{9,10},{10,1... | collective-permute-start | bytes 12582920 | tf_op jit(solution)/shard_map/while/body/eval_jaxpr/ppermute | solution.py:120
  2863.2 206.1 %collective-permute-start.5 = (f32[8,64,16,128]{3,1,2,0:T(8,128)}, f32[8,64,16,128]{3,1,2,0:T(8,128)}, u32[]{:S(2)}, u32[]{:S(2)}) collective-permute-start(f32[8,64,16,128]{3,1,2,0:T(8,128)} %get-tuple-element.1283), channel_id=1, source_target_pairs={{0,1},{1,2},{2,3},{3,4},{4,5},{5,6},{6,7},{7,8},{8,9},{9,10},{10,1... | collective-permute-start | bytes 12582920 | tf_op jit(solution)/shard_map/while/body/eval_jaxpr/ppermute | solution.py:120
  2863.2 206.1 %collective-permute-start.4 = (f32[8,64,16,128]{3,1,2,0:T(8,128)}, f32[8,64,16,128]{3,1,2,0:T(8,128)}, u32[]{:S(2)}, u32[]{:S(2)}) collective-permute-start(f32[8,64,16,128]{3,1,2,0:T(8,128)} %get-tuple-element.1282), channel_id=1, source_target_pairs={{0,1},{1,2},{2,3},{3,4},{4,5},{5,6},{6,7},{7,8},{8,9},{9,10},{10,1... | collective-permute-start | bytes 12582920 | tf_op jit(solution)/shard_map/while/body/eval_jaxpr/ppermute | solution.py:120
  3078.8 206.0 %collective-permute-start.5 = (f32[8,64,16,128]{3,1,2,0:T(8,128)}, f32[8,64,16,128]{3,1,2,0:T(8,128)}, u32[]{:S(2)}, u32[]{:S(2)}) collective-permute-start(f32[8,64,16,128]{3,1,2,0:T(8,128)} %get-tuple-element.1283), channel_id=1, source_target_pairs={{0,1},{1,2},{2,3},{3,4},{4,5},{5,6},{6,7},{7,8},{8,9},{9,10},{10,1... | collective-permute-start | bytes 12582920 | tf_op jit(solution)/shard_map/while/body/eval_jaxpr/ppermute | solution.py:120
  3078.8 206.0 %collective-permute-start.4 = (f32[8,64,16,128]{3,1,2,0:T(8,128)}, f32[8,64,16,128]{3,1,2,0:T(8,128)}, u32[]{:S(2)}, u32[]{:S(2)}) collective-permute-start(f32[8,64,16,128]{3,1,2,0:T(8,128)} %get-tuple-element.1282), channel_id=1, source_target_pairs={{0,1},{1,2},{2,3},{3,4},{4,5},{5,6},{6,7},{7,8},{8,9},{9,10},{10,1... | collective-permute-start | bytes 12582920 | tf_op jit(solution)/shard_map/while/body/eval_jaxpr/ppermute | solution.py:120
  3294.4 206.0 %collective-permute-start.5 = (f32[8,64,16,128]{3,1,2,0:T(8,128)}, f32[8,64,16,128]{3,1,2,0:T(8,128)}, u32[]{:S(2)}, u32[]{:S(2)}) collective-permute-start(f32[8,64,16,128]{3,1,2,0:T(8,128)} %get-tuple-element.1283), channel_id=1, source_target_pairs={{0,1},{1,2},{2,3},{3,4},{4,5},{5,6},{6,7},{7,8},{8,9},{9,10},{10,1... | collective-permute-start | bytes 12582920 | tf_op jit(solution)/shard_map/while/body/eval_jaxpr/ppermute | solution.py:120
  3294.4 206.0 %collective-permute-start.4 = (f32[8,64,16,128]{3,1,2,0:T(8,128)}, f32[8,64,16,128]{3,1,2,0:T(8,128)}, u32[]{:S(2)}, u32[]{:S(2)}) collective-permute-start(f32[8,64,16,128]{3,1,2,0:T(8,128)} %get-tuple-element.1282), channel_id=1, source_target_pairs={{0,1},{1,2},{2,3},{3,4},{4,5},{5,6},{6,7},{7,8},{8,9},{9,10},{10,1... | collective-permute-start | bytes 12582920 | tf_op jit(solution)/shard_map/while/body/eval_jaxpr/ppermute | solution.py:120
  3510.0 206.0 %collective-permute-start.5 = (f32[8,64,16,128]{3,1,2,0:T(8,128)}, f32[8,64,16,128]{3,1,2,0:T(8,128)}, u32[]{:S(2)}, u32[]{:S(2)}) collective-permute-start(f32[8,64,16,128]{3,1,2,0:T(8,128)} %get-tuple-element.1283), channel_id=1, source_target_pairs={{0,1},{1,2},{2,3},{3,4},{4,5},{5,6},{6,7},{7,8},{8,9},{9,10},{10,1... | collective-permute-start | bytes 12582920 | tf_op jit(solution)/shard_map/while/body/eval_jaxpr/ppermute | solution.py:120
  3510.0 206.0 %collective-permute-start.4 = (f32[8,64,16,128]{3,1,2,0:T(8,128)}, f32[8,64,16,128]{3,1,2,0:T(8,128)}, u32[]{:S(2)}, u32[]{:S(2)}) collective-permute-start(f32[8,64,16,128]{3,1,2,0:T(8,128)} %get-tuple-element.1282), channel_id=1, source_target_pairs={{0,1},{1,2},{2,3},{3,4},{4,5},{5,6},{6,7},{7,8},{8,9},{9,10},{10,1... | collective-permute-start | bytes 12582920 | tf_op jit(solution)/shard_map/while/body/eval_jaxpr/ppermute | solution.py:120
  3725.5 206.0 %collective-permute-start.5 = (f32[8,64,16,128]{3,1,2,0:T(8,128)}, f32[8,64,16,128]{3,1,2,0:T(8,128)}, u32[]{:S(2)}, u32[]{:S(2)}) collective-permute-start(f32[8,64,16,128]{3,1,2,0:T(8,128)} %get-tuple-element.1283), channel_id=1, source_target_pairs={{0,1},{1,2},{2,3},{3,4},{4,5},{5,6},{6,7},{7,8},{8,9},{9,10},{10,1... | collective-permute-start | bytes 12582920 | tf_op jit(solution)/shard_map/while/body/eval_jaxpr/ppermute | solution.py:120
  3725.5 206.0 %collective-permute-start.4 = (f32[8,64,16,128]{3,1,2,0:T(8,128)}, f32[8,64,16,128]{3,1,2,0:T(8,128)}, u32[]{:S(2)}, u32[]{:S(2)}) collective-permute-start(f32[8,64,16,128]{3,1,2,0:T(8,128)} %get-tuple-element.1282), channel_id=1, source_target_pairs={{0,1},{1,2},{2,3},{3,4},{4,5},{5,6},{6,7},{7,8},{8,9},{9,10},{10,1... | collective-permute-start | bytes 12582920 | tf_op jit(solution)/shard_map/while/body/eval_jaxpr/ppermute | solution.py:120
  3941.1 206.1 %collective-permute-start.5 = (f32[8,64,16,128]{3,1,2,0:T(8,128)}, f32[8,64,16,128]{3,1,2,0:T(8,128)}, u32[]{:S(2)}, u32[]{:S(2)}) collective-permute-start(f32[8,64,16,128]{3,1,2,0:T(8,128)} %get-tuple-element.1283), channel_id=1, source_target_pairs={{0,1},{1,2},{2,3},{3,4},{4,5},{5,6},{6,7},{7,8},{8,9},{9,10},{10,1... | collective-permute-start | bytes 12582920 | tf_op jit(solution)/shard_map/while/body/eval_jaxpr/ppermute | solution.py:120
  3941.1 206.1 %collective-permute-start.4 = (f32[8,64,16,128]{3,1,2,0:T(8,128)}, f32[8,64,16,128]{3,1,2,0:T(8,128)}, u32[]{:S(2)}, u32[]{:S(2)}) collective-permute-start(f32[8,64,16,128]{3,1,2,0:T(8,128)} %get-tuple-element.1282), channel_id=1, source_target_pairs={{0,1},{1,2},{2,3},{3,4},{4,5},{5,6},{6,7},{7,8},{8,9},{9,10},{10,1... | collective-permute-start | bytes 12582920 | tf_op jit(solution)/shard_map/while/body/eval_jaxpr/ppermute | solution.py:120
  3941.1 202.9 %collective-permute-start.2 = (bf16[8,64,16,128]{3,1,2,0:T(8,128)(2,1)}, bf16[8,64,16,128]{3,1,2,0:T(8,128)(2,1)}, u32[]{:S(2)}, u32[]{:S(2)}) collective-permute-start(bf16[8,64,16,128]{3,1,2,0:T(8,128)(2,1)} %get-tuple-element.1280), channel_id=1, source_target_pairs={{0,1},{1,2},{2,3},{3,4},{4,5},{5,6},{6,7},{7,8},{8,9},{9,10},{10,1... | collective-permute-start | bytes 6291464 | tf_op jit(solution)/shard_map/while/body/eval_jaxpr/ppermute | solution.py:120
  4156.8 206.0 %collective-permute-start.5 = (f32[8,64,16,128]{3,1,2,0:T(8,128)}, f32[8,64,16,128]{3,1,2,0:T(8,128)}, u32[]{:S(2)}, u32[]{:S(2)}) collective-permute-start(f32[8,64,16,128]{3,1,2,0:T(8,128)} %get-tuple-element.1283), channel_id=1, source_target_pairs={{0,1},{1,2},{2,3},{3,4},{4,5},{5,6},{6,7},{7,8},{8,9},{9,10},{10,1... | collective-permute-start | bytes 12582920 | tf_op jit(solution)/shard_map/while/body/eval_jaxpr/ppermute | solution.py:120
  4156.8 206.0 %collective-permute-start.4 = (f32[8,64,16,128]{3,1,2,0:T(8,128)}, f32[8,64,16,128]{3,1,2,0:T(8,128)}, u32[]{:S(2)}, u32[]{:S(2)}) collective-permute-start(f32[8,64,16,128]{3,1,2,0:T(8,128)} %get-tuple-element.1282), channel_id=1, source_target_pairs={{0,1},{1,2},{2,3},{3,4},{4,5},{5,6},{6,7},{7,8},{8,9},{9,10},{10,1... | collective-permute-start | bytes 12582920 | tf_op jit(solution)/shard_map/while/body/eval_jaxpr/ppermute | solution.py:120
  4372.3 206.1 %collective-permute-start.5 = (f32[8,64,16,128]{3,1,2,0:T(8,128)}, f32[8,64,16,128]{3,1,2,0:T(8,128)}, u32[]{:S(2)}, u32[]{:S(2)}) collective-permute-start(f32[8,64,16,128]{3,1,2,0:T(8,128)} %get-tuple-element.1283), channel_id=1, source_target_pairs={{0,1},{1,2},{2,3},{3,4},{4,5},{5,6},{6,7},{7,8},{8,9},{9,10},{10,1... | collective-permute-start | bytes 12582920 | tf_op jit(solution)/shard_map/while/body/eval_jaxpr/ppermute | solution.py:120
  4372.4 206.1 %collective-permute-start.4 = (f32[8,64,16,128]{3,1,2,0:T(8,128)}, f32[8,64,16,128]{3,1,2,0:T(8,128)}, u32[]{:S(2)}, u32[]{:S(2)}) collective-permute-start(f32[8,64,16,128]{3,1,2,0:T(8,128)} %get-tuple-element.1282), channel_id=1, source_target_pairs={{0,1},{1,2},{2,3},{3,4},{4,5},{5,6},{6,7},{7,8},{8,9},{9,10},{10,1... | collective-permute-start | bytes 12582920 | tf_op jit(solution)/shard_map/while/body/eval_jaxpr/ppermute | solution.py:120
  4372.4 202.9 %collective-permute-start.2 = (bf16[8,64,16,128]{3,1,2,0:T(8,128)(2,1)}, bf16[8,64,16,128]{3,1,2,0:T(8,128)(2,1)}, u32[]{:S(2)}, u32[]{:S(2)}) collective-permute-start(bf16[8,64,16,128]{3,1,2,0:T(8,128)(2,1)} %get-tuple-element.1280), channel_id=1, source_target_pairs={{0,1},{1,2},{2,3},{3,4},{4,5},{5,6},{6,7},{7,8},{8,9},{9,10},{10,1... | collective-permute-start | bytes 6291464 | tf_op jit(solution)/shard_map/while/body/eval_jaxpr/ppermute | solution.py:120
  4588.0 206.1 %collective-permute-start.5 = (f32[8,64,16,128]{3,1,2,0:T(8,128)}, f32[8,64,16,128]{3,1,2,0:T(8,128)}, u32[]{:S(2)}, u32[]{:S(2)}) collective-permute-start(f32[8,64,16,128]{3,1,2,0:T(8,128)} %get-tuple-element.1283), channel_id=1, source_target_pairs={{0,1},{1,2},{2,3},{3,4},{4,5},{5,6},{6,7},{7,8},{8,9},{9,10},{10,1... | collective-permute-start | bytes 12582920 | tf_op jit(solution)/shard_map/while/body/eval_jaxpr/ppermute | solution.py:120
  4588.0 206.1 %collective-permute-start.4 = (f32[8,64,16,128]{3,1,2,0:T(8,128)}, f32[8,64,16,128]{3,1,2,0:T(8,128)}, u32[]{:S(2)}, u32[]{:S(2)}) collective-permute-start(f32[8,64,16,128]{3,1,2,0:T(8,128)} %get-tuple-element.1282), channel_id=1, source_target_pairs={{0,1},{1,2},{2,3},{3,4},{4,5},{5,6},{6,7},{7,8},{8,9},{9,10},{10,1... | collective-permute-start | bytes 12582920 | tf_op jit(solution)/shard_map/while/body/eval_jaxpr/ppermute | solution.py:120
  4588.0 202.9 %collective-permute-start.2 = (bf16[8,64,16,128]{3,1,2,0:T(8,128)(2,1)}, bf16[8,64,16,128]{3,1,2,0:T(8,128)(2,1)}, u32[]{:S(2)}, u32[]{:S(2)}) collective-permute-start(bf16[8,64,16,128]{3,1,2,0:T(8,128)(2,1)} %get-tuple-element.1280), channel_id=1, source_target_pairs={{0,1},{1,2},{2,3},{3,4},{4,5},{5,6},{6,7},{7,8},{8,9},{9,10},{10,1... | collective-permute-start | bytes 6291464 | tf_op jit(solution)/shard_map/while/body/eval_jaxpr/ppermute | solution.py:120
  (77 other events, 8095.4 us)
Sparse Core Ops, SparseCore 0:
  4827.4 197.7 all-reduce.7
where the time goes:
time: 5070 us; the launch traced here: 5040 us
  waiting for transfers between devices  4180 us (82%)
  local copies, waits for them, and re-layouts  512 us (10%)
  blocking collectives  161 us (3%)
  starting transfers between devices  101 us (2%)
    ppermute x60, waiting for transfers between devices, bwd_body(): lax.ppermute(travel, 'cp', shift_pairs)  2970 us
    ppermute x15, waiting for transfers between devices, fwd_body(): val_blk = lax.ppermute(val_blk, 'cp', shift_pairs)  862 us
    ppermute x15, waiting for transfers between devices, fwd_body(): key_blk = lax.ppermute(key_blk, 'cp', shift_pairs)  337 us
    while x90, local copies, waits for them, and re-layouts  329 us
    psum x1, blocking collectives, local(): d_bias_u = lax.psum(jnp.sum(dq_cont, axis=(0, 1)), 'cp')  161 us
  transfers between devices with their start and end apart: 93, of which 61 were waited for; matrix products, arithmetic and copies ran while one was open for 2% of the time, Pallas kernels for 0%

commit v1 on v0

v1 whole, which is shorter than its diff:
```python
import functools

import jax
import jax.numpy as jnp
from jax import lax
from jax.experimental import pallas as pl
from jax.experimental.pallas import tpu as pltpu
from jax.sharding import PartitionSpec as P

MESH = pl.DeviceIdType.MESH
BF16, F32 = jnp.bfloat16, jnp.float32
LOG2E = 1.4426950408889634

N_DEV = 16
PAIR = 2
N_PAIR = 8
SLOTS = 4
ROWS = 64
SEQ = N_DEV * ROWS
HEAD = 128
QB = 256
N_QB = SEQ // QB
PARTS = ((0, 171), (171, 171), (342, 171), (513, 171), (684, 170), (854, 170))
HOPS = ((1, 2, 4), (2, 4, 1), (4, 1, 2)) * 2
N_PART = len(PARTS)


def dot(lhs, rhs):
    return jnp.dot(lhs, rhs, preferred_element_type=F32)


def flip8(x):
    rows, cols = x.shape
    idx = 7 - lax.broadcasted_iota(jnp.int32, (rows // 8, 8, cols), 1)
    return jnp.take_along_axis(x.reshape(rows // 8, 8, cols), idx, axis=1).reshape(rows, cols)


def eye_rev(dtype):
    total = lax.broadcasted_iota(jnp.int32, (HEAD, HEAD), 0) + lax.broadcasted_iota(jnp.int32, (HEAD, HEAD), 1)
    return jnp.where(total == HEAD - 1, 1.0, 0.0).astype(dtype)


def kernel(q_in, k_in, v_in, g_in, r_in, u_in, w_in,
           o_out, dq_out, dk_out, dv_out, dr0_out, dr1_out, dr2_out, dr3_out, dr4_out, dr5_out, du_out, dw_out,
           buf, r_buf, dr_rx, dr_fin, dr_acc,
           s_ref, e_ref, dp_ref, pb_ref, ds_ref, dd_ref,
           a_s, c_s, g_s, k_s, v_s, rev_s, kt_s, vt_s, rt_s, at_s, ct_s, gt_s,
           dkt, dvt, stage,
           in_send, in_recv, out_send, out_recv, own_sem, r_sem, x_send, x_recv, ring_send, ring_recv, fw_send, fw_recv, b_send, b_recv):
    me = lax.axis_index("cp")
    core = me % 2
    chip = me // 2
    partner = me + 1 - 2 * core
    scale = HEAD ** -0.5

    r_copy = pltpu.make_async_copy(r_in.at[:, chip], r_buf, r_sem)
    r_copy.start()

    barrier = pltpu.get_barrier_semaphore()

    def say(step, carry):
        pl.semaphore_signal(barrier, inc=1, device_id=((me + step) % N_DEV,), device_id_type=MESH)
        return carry

    lax.fori_loop(1, N_DEV, say, 0)
    pl.semaphore_wait(barrier, N_DEV - 1)

    ins = (q_in, k_in, g_in, v_in)
    my_rows = pl.ds(pl.multiple_of(me * ROWS, ROWS), ROWS)

    def send_in(slot):
        for t, src in enumerate(ins):
            pltpu.make_async_copy(src.at[core * SLOTS + slot, :, chip], buf.at[t, slot, my_rows], in_recv.at[t, slot]).start()

        def to(step, carry):
            peer = me ^ step
            for t, src in enumerate(ins):
                pltpu.make_async_remote_copy(
                    src_ref=src.at[(peer % 2) * SLOTS + slot, :, peer // 2], dst_ref=buf.at[t, slot, my_rows],
                    send_sem=in_send, recv_sem=in_recv.at[t, slot], device_id=(peer,), device_id_type=MESH).start()
            return carry
        lax.fori_loop(1, N_DEV, to, 0)

    for slot in range(SLOTS):
        send_in(slot)

    r_copy.wait()
    pair_tab = pltpu.einshape("abc->bac", r_buf[...])
    rev = eye_rev(BF16)
    for hh in range(PAIR):
        for blk in range(SEQ // HEAD):
            part = pair_tab[hh, SEQ - HEAD * (blk + 1):SEQ - HEAD * blk]
            flipped = dot(rev, part).astype(BF16)
            rev_s[hh, HEAD * blk:HEAD * (blk + 1), :] = flipped
            rt_s[hh, :, HEAD * blk:HEAD * (blk + 1)] = flipped.T
    dr_acc[...] = jnp.zeros_like(dr_acc)

    u_all = u_in[chip].astype(F32)
    w_all = w_in[chip].astype(F32)

    acts = (o_out, dq_out, dk_out, dv_out)

    def send_out(slot, which):
        for t in which:
            pltpu.make_async_copy(buf.at[t, slot, my_rows], acts[t].at[core * SLOTS + slot, :, chip], out_recv.at[t]).start()

        def to(step, carry):
            peer = me ^ step
            peer_rows = pl.ds(pl.multiple_of(peer * ROWS, ROWS), ROWS)
            for t in which:
                pltpu.make_async_remote_copy(
                    src_ref=buf.at[t, slot, peer_rows], dst_ref=acts[t].at[core * SLOTS + slot, :, chip],
                    send_sem=out_send, recv_sem=out_recv.at[t], device_id=(peer,), device_id_type=MESH).start()
            return carry
        lax.fori_loop(1, N_DEV, to, 0)

    def slot_body(slot, carry):
        for t in range(4):
            pltpu.make_async_copy(buf.at[t, slot], buf.at[t, slot], in_recv.at[t, slot]).wait()
        q2 = pltpu.einshape("abc->bac", buf[0, slot])
        for hh in range(PAIR):
            q32 = q2[hh].astype(F32)
            a = (q32 + u_all[hh:hh + 1]).astype(BF16)
            c = (q32 + w_all[hh:hh + 1]).astype(BF16)
            a_s[hh] = a
            c_s[hh] = c
            at_s[hh] = a.T
            ct_s[hh] = flip8(c.astype(F32)).astype(BF16).T
        k2 = pltpu.einshape("abc->bac", buf[1, slot])
        k_s[...] = k2
        g2 = pltpu.einshape("abc->bac", buf[2, slot])
        g_s[...] = g2
        v2 = pltpu.einshape("abc->bac", buf[3, slot])
        v_s[...] = v2
        for hh in range(PAIR):
            kt_s[hh] = k2[hh].T
            gt_s[hh] = g2[hh].T
            vt_s[hh] = v2[hh].T

        def head_body(hh, carry):
            for qb in reversed(range(N_QB)):
                i0 = QB * qb
                width = i0 + QB
                rows = slice(i0, i0 + QB)
                s_ref[:, :width] = dot(a_s[hh, rows, :], kt_s[hh, :, :width])
                e_ref[:, :width] = dot(c_s[hh, rows, :], rt_s[hh, :, SEQ - width:])
                dp_ref[:, :width] = dot(g_s[hh, rows, :], vt_s[hh, :, :width])
                for g in range(QB // 16):
                    r0 = 16 * g
                    group = slice(r0, r0 + 16)
                    rel = pltpu.roll(e_ref[group, :width], i0 + 1 + r0, 1, stride=1, stride_axis=0)
                    s = s_ref[group, :width] + rel
                    ahead = lax.broadcasted_iota(jnp.int32, (16, width), 1) - lax.broadcasted_iota(jnp.int32, (16, width), 0)
                    s = jnp.where(ahead <= i0 + r0, s, -jnp.inf)
                    top = jnp.max(s, axis=1, keepdims=True)
                    p = jnp.exp2((s - top) * (scale * LOG2E))
                    p = p * (1.0 / jnp.sum(p, axis=1, keepdims=True))
                    pb_ref[group, :width] = p.astype(BF16)
                    dp = dp_ref[group, :width]
                    row_dot = jnp.sum(p * dp, axis=1, keepdims=True)
                    ds = (p * (dp - row_dot) * scale).astype(BF16)
                    ds_ref[group, :width] = ds
                    flipped = flip8(ds.astype(F32))
                    half = [pltpu.roll(flipped[8 * j:8 * j + 8], QB - 8 - r0 - 8 * j, 1, stride=1, stride_axis=0) for j in range(2)]
                    dd_ref[group, :width] = jnp.concatenate(half, axis=0).astype(BF16)
                pb = pb_ref[:, :width]
                ds = ds_ref[:, :width]
                dd = dd_ref[:, :width]
                stage[0, hh, rows, :] = dot(pb, v_s[hh, :width, :]).astype(BF16)
                dqc = dot(ds, k_s[hh, :width, :])
                dqr = flip8(dot(dd, rev_s[hh, SEQ - width:, :]))
                stage[1, hh, rows, :] = (dqc + dqr).astype(BF16)
                dr_acc[hh, HEAD:HEAD + 1, :HEAD] += jnp.sum(dqc, axis=0, keepdims=True)
                dr_acc[hh, HEAD + 1:HEAD + 2, :HEAD] += jnp.sum(dqr, axis=0, keepdims=True)
                dk_new = dot(at_s[hh, :, rows], ds)
                dv_new = dot(gt_s[hh, :, rows], pb)
                if qb == N_QB - 1:
                    dkt[...] = dk_new
                    dvt[...] = dv_new
                else:
                    dkt[:, :width] += dk_new
                    dvt[:, :width] += dv_new
                dr_acc[hh, :HEAD, SEQ - width:] += dot(ct_s[hh, :, rows], dd)
            stage[2, hh] = dkt[...].astype(BF16).T
            stage[3, hh] = dvt[...].astype(BF16).T
            return carry

        lax.fori_loop(0, PAIR, head_body, 0)
        for t in range(4):
            buf[t, slot] = pltpu.einshape("abc->bac", stage[t])

        @pl.when(slot < SLOTS - 1)
        def _():
            send_out(slot, range(4))
        return carry

    lax.fori_loop(0, SLOTS, slot_body, 0)

    swap = pltpu.make_async_remote_copy(
        src_ref=dr_acc.at[1 - core], dst_ref=dr_rx, send_sem=x_send, recv_sem=x_recv, device_id=(partner,), device_id_type=MESH)
    swap.start()
    swap.wait()
    head = 2 * chip + core
    total = dr_acc[core] + dr_rx[...]
    rev32 = eye_rev(F32)
    for blk in range(SEQ // HEAD):
        part = total[:HEAD, SEQ - HEAD * (blk + 1):SEQ - HEAD * blk]
        turned = lax.dot_general(rev32, part, (((1,), (1,)), ((), ())), precision=lax.Precision.HIGHEST, preferred_element_type=F32)
        dr_fin[HEAD * blk:HEAD * (blk + 1)] = turned.reshape(HEAD, 1, HEAD)
    dr_fin[SEQ] = total[HEAD:HEAD + 1, :HEAD]
    dr_fin[SEQ + 1] = total[HEAD + 1:HEAD + 2, :HEAD]

    def wait_for(ref, sem):
        pltpu.make_async_copy(ref, ref, sem).wait()

    parts = (dr0_out, dr1_out, dr2_out, dr3_out, dr4_out, dr5_out)

    def block(m, bits):
        if bits == 0:
            start, rows = PARTS[m]
            return dr_fin.at[start:start + rows]
        return parts[m].at[:, 2 * (chip ^ bits) + core]

    def forward(m, bits):
        dst = parts[m].at[:, 2 * (chip ^ bits) + core]
        pltpu.make_async_remote_copy(src_ref=block(m, bits), dst_ref=dst, send_sem=fw_send.at[m], recv_sem=fw_recv.at[m],
                                     device_id=(partner,), device_id_type=MESH).start()

    held = [[0] for _ in range(N_PART)]
    for m in range(N_PART):
        pltpu.make_async_copy(block(m, 0), parts[m].at[:, head], own_sem.at[m]).start()
    for hop in range(3):
        for m in range(N_PART):
            bit = HOPS[m][hop]
            peer = me ^ (2 * bit)
            for bits in held[m]:
                pltpu.make_async_remote_copy(
                    src_ref=block(m, bits), dst_ref=parts[m].at[:, 2 * (chip ^ bits) + core], send_sem=ring_send.at[m],
                    recv_sem=ring_recv.at[hop, m], device_id=(peer,), device_id_type=MESH).start()
        for m in range(N_PART):
            for bits in (held[m] if hop == 0 else held[m][len(held[m]) // 2:]):
                forward(m, bits)
        if hop == 0:
            for j, dst in enumerate((du_out, dw_out)):
                pltpu.make_async_copy(dr_fin.at[SEQ + j], dst.at[head], b_recv.at[j]).start()
                for step in range(1, N_DEV):
                    pltpu.make_async_remote_copy(
                        src_ref=dr_fin.at[SEQ + j], dst_ref=dst.at[head], send_sem=b_send.at[j], recv_sem=b_recv.at[j],
                        device_id=(me ^ step,), device_id_type=MESH).start()
        send_out(SLOTS - 1, ((0, 1), (2,), (3,))[hop])
        for m in range(N_PART):
            count = len(held[m])
            wait_for(parts[m].at[:, :count], ring_recv.at[hop, m])
            held[m] = held[m] + [bits ^ HOPS[m][hop] for bits in held[m]]
    for m in range(N_PART):
        for bits in held[m][4:]:
            forward(m, bits)

    for t, dst in enumerate(acts):
        wait_for(dst, out_recv.at[t])
    for j, dst in enumerate((du_out, dw_out)):
        wait_for(dst, b_recv.at[j])
        wait_for(dst.at[:N_DEV - 1], b_send.at[j])
    wait_for(buf.at[:, :, :SEQ - ROWS], in_send)
    wait_for(buf.at[:, :, :SEQ - ROWS], out_send)
    for m in range(N_PART):
        wait_for(parts[m].at[:, head], own_sem.at[m])
        wait_for(parts[m].at[:, :N_PAIR - 1], ring_send.at[m])
        wait_for(parts[m].at[:, :N_PAIR], fw_send.at[m])
        wait_for(parts[m].at[:, :N_PAIR], fw_recv.at[m])


def writer(*refs):
    ins, (o, dq, dk, dv, dr, du, dw, sem) = refs[:6 + N_PART], refs[6 + N_PART:]
    pairs = list(zip(ins[:4] + ins[-2:], (o, dq, dk, dv, du, dw)))
    for part, (start, rows) in zip(ins[4:-2], PARTS):
        pairs.append((part, dr.at[start:start + rows]))
    copies = [pltpu.make_async_copy(src, dst, sem.at[j]) for j, (src, dst) in enumerate(pairs)]
    for copy in copies:
        copy.start()
    for copy in copies:
        copy.wait()


def solution(mesh):
    n_dev = mesh.shape["cp"]
    seq_spec = P(None, "cp", None, None)

    def local(query, key_in, value, bias_u, bias_w, rel_k, d_out):
        n_batch, rows, n_heads, head_dim = query.shape
        pairs = (n_batch, rows, N_PAIR, PAIR, head_dim)
        vm = pltpu.VMEM
        dma = pltpu.SemaphoreType.DMA
        whole = pl.BlockSpec(memory_space=pl.ANY)
        near = pl.BlockSpec(memory_space=pltpu.VMEM)
        act = jax.ShapeDtypeStruct(pairs, BF16)
        vec = jax.ShapeDtypeStruct((n_heads, 1, head_dim), F32)
        tok = (PAIR, SEQ, HEAD)
        tok_t = (PAIR, HEAD, SEQ)
        outs = pl.pallas_call(
            kernel,
            name="rel_attn",
            out_shape=(act, act, act, act,
                       *[jax.ShapeDtypeStruct((rows, n_heads, 1, head_dim), F32) for _, rows in PARTS],
                       vec, vec),
            in_specs=[whole] * 5 + [near] * 2,
            out_specs=[whole] * (6 + N_PART),
            scratch_shapes=[
                vm((4, SLOTS, SEQ, PAIR, HEAD), BF16),
                vm((SEQ, PAIR, HEAD), BF16), vm((HEAD + 8, SEQ), F32), vm((SEQ + 2, 1, HEAD), F32), vm((PAIR, HEAD + 8, SEQ), F32),
                vm((QB, SEQ), F32), vm((QB, SEQ), F32), vm((QB, SEQ), F32),
                vm((QB, SEQ), BF16), vm((QB, SEQ), BF16), vm((QB, SEQ), BF16),
                vm(tok, BF16), vm(tok, BF16), vm(tok, BF16), vm(tok, BF16), vm(tok, BF16), vm(tok, BF16),
                vm(tok_t, BF16), vm(tok_t, BF16), vm(tok_t, BF16), vm(tok_t, BF16), vm(tok_t, BF16), vm(tok_t, BF16),
                vm((HEAD, SEQ), F32), vm((HEAD, SEQ), F32), vm((4, PAIR, SEQ, HEAD), BF16),
                dma, dma((4, SLOTS)), dma, dma((4,)), dma((N_PART,)), dma, dma, dma, dma((N_PART,)), dma((3, N_PART)), dma((N_PART,)), dma((N_PART,)), dma((2,)), dma((2,)),
            ],
            compiler_params=pltpu.CompilerParams(collective_id=0, has_side_effects=True, vmem_limit_bytes=36 * 1024 * 1024),
        )(query.reshape(pairs), key_in.reshape(pairs), value.reshape(pairs), d_out.reshape(pairs),
          rel_k.reshape(SEQ, N_PAIR, PAIR, head_dim), bias_u.reshape(N_PAIR, PAIR, head_dim), bias_w.reshape(N_PAIR, PAIR, head_dim))
        o, dq, dk, dv, dr, du, dw = pl.pallas_call(
            writer,
            name="writer",
            out_shape=(act, act, act, act, jax.ShapeDtypeStruct((SEQ, n_heads, 1, head_dim), F32), vec, vec),
            in_specs=[whole] * (6 + N_PART),
            out_specs=[whole] * 7,
            scratch_shapes=[dma((6 + N_PART,))],
            compiler_params=pltpu.CompilerParams(vmem_limit_bytes=1024 * 1024),
        )(*outs)
        full = query.shape
        return (o.reshape(full), dq.reshape(full), dk.reshape(full), dv.reshape(full),
                du.reshape(bias_u.shape), dw.reshape(bias_w.shape), dr.reshape(rel_k.shape))

    return jax.shard_map(local, mesh=mesh,
                         in_specs=(seq_spec, seq_spec, seq_spec, P(), P(), P(), seq_spec),
                         out_specs=(seq_spec, seq_spec, seq_spec, seq_spec, P(), P(), P()),
                         check_vma=False)
```

time: 5070 us -> 243 us (0.05)
  waiting for transfers between devices: 4180 us -> 0 us
  local copies, waits for them, and re-layouts: 512 us -> 1.37 us
  Pallas kernels: 0 us -> 241 us
  blocking collectives: 161 us -> 0 us
  starting transfers between devices: 101 us -> 0 us
    ppermute x92 -> x0, waiting for transfers between devices: 4170 us -> none  [the longest x60 2970 us: bwd_body(): lax.ppermute(travel, 'cp', shift_pairs)]
    while x98 -> x0, local copies, waits for them, and re-layouts: 357 us -> none
    pallas_call x0 -> x2, Pallas kernels: none -> 241 us  [the longest x1 235 us: local(): pl.pallas_call(kernel, name='rel_attn', out_shape=(act, act, act, act, *[...]
    psum x1 -> x0, blocking collectives: 161 us -> none  [local(): d_bias_u = lax.psum(jnp.sum(dq_cont, axis=(0, 1)), 'cp')]
    ppermute x92 -> x0, starting transfers between devices: 101 us -> none  [the longest x15 53.8 us: fwd_body(): key_blk = lax.ppermute(key_blk, 'cp', shift_pairs)]
    rev x2 -> x0, local copies, waits for them, and re-layouts: 66.5 us -> none  [the longest x1 59.4 us: local(): jnp.flip(rel_k, axis=0)]
  transfers between devices with their start and end apart: 93 -> 0, of which waited for: 61 -> 0; matrix products, arithmetic and copies ran while one was open for 2% -> 0% of each run, Pallas kernels for 0% -> 0%
where the time goes in v1:
time: 243 us
  Pallas kernels  241 us (99%)
    pallas_call x1, Pallas kernels, local(): pl.pallas_call(kernel, name='rel_attn', out_shape=(act, act, act, act, *[...  235 us
    pallas_call x1, Pallas kernels, local(): pl.pallas_call(writer, name='writer', out_shape=(act, act, act, act, jax....  5.95 us

profile of v1, /device:TPU:0, one launch (start us, length us, event | category | flops | bytes accessed | tf_op | source)
XLA Modules:
  0.0 243.3 jit_solution(17819241814267806007)
XLA Ops:
  0.6 0.0 copy-start
  0.6 0.7 copy-done
  1.3 0.0 copy-start.1
  1.3 0.7 copy-done.1
  2.0 235.3 %rel_attn.1 = (bf16[8,64,8,2,128]{4,3,2,1,0:T(2,128)(2,1)S(1)}, bf16[8,64,8,2,128]{4,3,2,1,0:T(2,128)(2,1)S(1)}, bf16[8,64,8,2,128]{4,3,2,1,0:T(2,128)(2,1)S(1)}...) custom-call(bf16[8,64,8,2,128]{4,3,2,1,0:T(2,128)(2,1)} %bitcast.17,, ...), custom_call_target="tpu_custom_call" | custom-call | tf_op jit(solution)/shard_map/rel_attn/pallas_call | solution.py:300
  237.3 6.0 %writer.1 = (bf16[8,64,8,2,128]{4,3,2,1,0:T(2,128)(2,1)}, bf16[8,64,8,2,128]{4,3,2,1,0:T(2,128)(2,1)}, bf16[8,64,8,2,128]{4,3,2,1,0:T(2,128)(2,1)}, bf16[8,64,8,...) custom-call(bf16[8,64,8,2,128]{4,3,2,1,0:T(2,128)(2,1)S(1)} %get-tuple-el, ...), custom_call_target="tpu_custom_call" | custom-call | tf_op jit(solution)/shard_map/writer/pallas_call | solution.py:321
Async XLA Ops:
  0.6 0.7 copy-start
  1.3 0.7 copy-start.1

commit v2 on v1

--- a/solution.py
+++ b/solution.py
@@ -23,6 +23,7 @@
 PARTS = ((0, 171), (171, 171), (342, 171), (513, 171), (684, 170), (854, 170))
 HOPS = ((1, 2, 4), (2, 4, 1), (4, 1, 2)) * 2
 N_PART = len(PARTS)
+TURNS = ((1, 3, 5, 7, 6, 2, 4), (7, 5, 3, 1, 2, 6, 4))
 
 
 def dot(lhs, rhs):
@@ -68,21 +69,28 @@
     ins = (q_in, k_in, g_in, v_in)
     my_rows = pl.ds(pl.multiple_of(me * ROWS, ROWS), ROWS)
 
+    def peers():
+        for near_turn, far_turn in zip(*TURNS):
+            turn = jnp.where(core == 0, near_turn, far_turn)
+            yield me ^ (2 * turn)
+            yield me ^ (2 * turn + 1)
+        yield partner
+
     def send_in(slot):
         for t, src in enumerate(ins):
             pltpu.make_async_copy(src.at[core * SLOTS + slot, :, chip], buf.at[t, slot, my_rows], in_recv.at[t, slot]).start()
 
-        def to(step, carry):
-            peer = me ^ step
+        for peer in peers():
             for t, src in enumerate(ins):
                 pltpu.make_async_remote_copy(
                     src_ref=src.at[(peer % 2) * SLOTS + slot, :, peer // 2], dst_ref=buf.at[t, slot, my_rows],
                     send_sem=in_send, recv_sem=in_recv.at[t, slot], device_id=(peer,), device_id_type=MESH).start()
-            return carry
-        lax.fori_loop(1, N_DEV, to, 0)
-
-    for slot in range(SLOTS):
+
+    def send_slot(slot, carry):
         send_in(slot)
+        return carry
+
+    lax.fori_loop(0, SLOTS, send_slot, 0)
 
     r_copy.wait()
     pair_tab = pltpu.einshape("abc->bac", r_buf[...])
@@ -104,15 +112,12 @@
         for t in which:
             pltpu.make_async_copy(buf.at[t, slot, my_rows], acts[t].at[core * SLOTS + slot, :, chip], out_recv.at[t]).start()
 
-        def to(step, carry):
-            peer = me ^ step
+        for peer in peers():
             peer_rows = pl.ds(pl.multiple_of(peer * ROWS, ROWS), ROWS)
             for t in which:
                 pltpu.make_async_remote_copy(
                     src_ref=buf.at[t, slot, peer_rows], dst_ref=acts[t].at[core * SLOTS + slot, :, chip],
                     send_sem=out_send, recv_sem=out_recv.at[t], device_id=(peer,), device_id_type=MESH).start()
-            return carry
-        lax.fori_loop(1, N_DEV, to, 0)
 
     def slot_body(slot, carry):
         for t in range(4):

time: 243 us -> 222 us (0.914)
  Pallas kernels: 241 us -> 220 us
    pallas_call x1, Pallas kernels: 235 us -> 214 us  [local(): pl.pallas_call(kernel, name='rel_attn', out_shape=(act, act, act, act, *[...]
where the time goes in v2:
time: 222 us
  Pallas kernels  220 us (99%)
    pallas_call x1, Pallas kernels, local(): pl.pallas_call(kernel, name='rel_attn', out_shape=(act, act, act, act, *[...  214 us
    pallas_call x1, Pallas kernels, local(): pl.pallas_call(writer, name='writer', out_shape=(act, act, act, act, jax....  5.95 us

profile of v2, /device:TPU:0, one launch (start us, length us, event | category | flops | bytes accessed | tf_op | source)
XLA Modules:
  0.0 221.8 jit_solution(7623419749168501321)
XLA Ops:
  0.6 0.0 copy-start
  0.6 0.7 copy-done
  1.3 0.0 copy-start.1
  1.3 0.7 copy-done.1
  2.0 213.8 %rel_attn.1 = (bf16[8,64,8,2,128]{4,3,2,1,0:T(2,128)(2,1)S(1)}, bf16[8,64,8,2,128]{4,3,2,1,0:T(2,128)(2,1)S(1)}, bf16[8,64,8,2,128]{4,3,2,1,0:T(2,128)(2,1)S(1)}...) custom-call(bf16[8,64,8,2,128]{4,3,2,1,0:T(2,128)(2,1)} %bitcast.17,, ...), custom_call_target="tpu_custom_call" | custom-call | tf_op jit(solution)/shard_map/rel_attn/pallas_call | solution.py:305
  215.9 6.0 %writer.1 = (bf16[8,64,8,2,128]{4,3,2,1,0:T(2,128)(2,1)}, bf16[8,64,8,2,128]{4,3,2,1,0:T(2,128)(2,1)}, bf16[8,64,8,2,128]{4,3,2,1,0:T(2,128)(2,1)}, bf16[8,64,8,...) custom-call(bf16[8,64,8,2,128]{4,3,2,1,0:T(2,128)(2,1)S(1)} %get-tuple-el, ...), custom_call_target="tpu_custom_call" | custom-call | tf_op jit(solution)/shard_map/writer/pallas_call | solution.py:326
Async XLA Ops:
  0.6 0.7 copy-start
  1.3 0.7 copy-start.1

commit v3 on v2

--- a/solution.py
+++ b/solution.py
@@ -43,7 +43,7 @@
 
 def kernel(q_in, k_in, v_in, g_in, r_in, u_in, w_in,
            o_out, dq_out, dk_out, dv_out, dr0_out, dr1_out, dr2_out, dr3_out, dr4_out, dr5_out, du_out, dw_out,
-           buf, r_buf, dr_rx, dr_fin, dr_acc,
+           buf, r_buf, u_buf, w_buf, dr_rx, dr_fin, dr_acc,
            s_ref, e_ref, dp_ref, pb_ref, ds_ref, dd_ref,
            a_s, c_s, g_s, k_s, v_s, rev_s, kt_s, vt_s, rt_s, at_s, ct_s, gt_s,
            dkt, dvt, stage,
@@ -54,8 +54,10 @@
     partner = me + 1 - 2 * core
     scale = HEAD ** -0.5
 
-    r_copy = pltpu.make_async_copy(r_in.at[:, chip], r_buf, r_sem)
-    r_copy.start()
+    tables = [pltpu.make_async_copy(src, dst, r_sem.at[j]) for j, (src, dst) in enumerate(
+        ((r_in.at[:, chip], r_buf), (u_in.at[chip], u_buf), (w_in.at[chip], w_buf)))]
+    for copy in tables:
+        copy.start()
 
     barrier = pltpu.get_barrier_semaphore()
 
@@ -92,7 +94,8 @@
 
     lax.fori_loop(0, SLOTS, send_slot, 0)
 
-    r_copy.wait()
+    for copy in tables:
+        copy.wait()
     pair_tab = pltpu.einshape("abc->bac", r_buf[...])
     rev = eye_rev(BF16)
     for hh in range(PAIR):
@@ -103,8 +106,8 @@
             rt_s[hh, :, HEAD * blk:HEAD * (blk + 1)] = flipped.T
     dr_acc[...] = jnp.zeros_like(dr_acc)
 
-    u_all = u_in[chip].astype(F32)
-    w_all = w_in[chip].astype(F32)
+    u_all = u_buf[...].astype(F32)
+    w_all = w_buf[...].astype(F32)
 
     acts = (o_out, dq_out, dk_out, dv_out)
 
@@ -252,14 +255,14 @@
                     pltpu.make_async_remote_copy(
                         src_ref=dr_fin.at[SEQ + j], dst_ref=dst.at[head], send_sem=b_send.at[j], recv_sem=b_recv.at[j],
                         device_id=(me ^ step,), device_id_type=MESH).start()
-        send_out(SLOTS - 1, ((0, 1), (2,), (3,))[hop])
+        send_out(SLOTS - 1, ((0,), (1,), (2, 3))[hop])
         for m in range(N_PART):
             count = len(held[m])
             wait_for(parts[m].at[:, :count], ring_recv.at[hop, m])
             held[m] = held[m] + [bits ^ HOPS[m][hop] for bits in held[m]]
-    for m in range(N_PART):
-        for bits in held[m][4:]:
-            forward(m, bits)
+            if hop == 2:
+                for bits in held[m][4:]:
+                    forward(m, bits)
 
     for t, dst in enumerate(acts):
         wait_for(dst, out_recv.at[t])
@@ -297,7 +300,6 @@
         vm = pltpu.VMEM
         dma = pltpu.SemaphoreType.DMA
         whole = pl.BlockSpec(memory_space=pl.ANY)
-        near = pl.BlockSpec(memory_space=pltpu.VMEM)
         act = jax.ShapeDtypeStruct(pairs, BF16)
         vec = jax.ShapeDtypeStruct((n_heads, 1, head_dim), F32)
         tok = (PAIR, SEQ, HEAD)
@@ -308,21 +310,22 @@
             out_shape=(act, act, act, act,
                        *[jax.ShapeDtypeStruct((rows, n_heads, 1, head_dim), F32) for _, rows in PARTS],
                        vec, vec),
-            in_specs=[whole] * 5 + [near] * 2,
+            in_specs=[pl.BlockSpec(memory_space=pltpu.HBM)] * 7,
             out_specs=[whole] * (6 + N_PART),
             scratch_shapes=[
                 vm((4, SLOTS, SEQ, PAIR, HEAD), BF16),
-                vm((SEQ, PAIR, HEAD), BF16), vm((HEAD + 8, SEQ), F32), vm((SEQ + 2, 1, HEAD), F32), vm((PAIR, HEAD + 8, SEQ), F32),
+                vm((SEQ, PAIR, HEAD), BF16), vm((PAIR, HEAD), BF16), vm((PAIR, HEAD), BF16), vm((HEAD + 8, SEQ), F32), vm((SEQ + 2, 1, HEAD), F32), vm((PAIR, HEAD + 8, SEQ), F32),
                 vm((QB, SEQ), F32), vm((QB, SEQ), F32), vm((QB, SEQ), F32),
                 vm((QB, SEQ), BF16), vm((QB, SEQ), BF16), vm((QB, SEQ), BF16),
                 vm(tok, BF16), vm(tok, BF16), vm(tok, BF16), vm(tok, BF16), vm(tok, BF16), vm(tok, BF16),
                 vm(tok_t, BF16), vm(tok_t, BF16), vm(tok_t, BF16), vm(tok_t, BF16), vm(tok_t, BF16), vm(tok_t, BF16),
                 vm((HEAD, SEQ), F32), vm((HEAD, SEQ), F32), vm((4, PAIR, SEQ, HEAD), BF16),
-                dma, dma((4, SLOTS)), dma, dma((4,)), dma((N_PART,)), dma, dma, dma, dma((N_PART,)), dma((3, N_PART)), dma((N_PART,)), dma((N_PART,)), dma((2,)), dma((2,)),
+                dma, dma((4, SLOTS)), dma, dma((4,)), dma((N_PART,)), dma((3,)), dma, dma, dma((N_PART,)), dma((3, N_PART)), dma((N_PART,)), dma((N_PART,)), dma((2,)), dma((2,)),
             ],
             compiler_params=pltpu.CompilerParams(collective_id=0, has_side_effects=True, vmem_limit_bytes=36 * 1024 * 1024),
-        )(query.reshape(pairs), key_in.reshape(pairs), value.reshape(pairs), d_out.reshape(pairs),
-          rel_k.reshape(SEQ, N_PAIR, PAIR, head_dim), bias_u.reshape(N_PAIR, PAIR, head_dim), bias_w.reshape(N_PAIR, PAIR, head_dim))
+        )(*[pltpu.with_memory_space_constraint(x, pltpu.HBM) for x in (
+            query.reshape(pairs), key_in.reshape(pairs), value.reshape(pairs), d_out.reshape(pairs),
+            rel_k.reshape(SEQ, N_PAIR, PAIR, head_dim), bias_u.reshape(N_PAIR, PAIR, head_dim), bias_w.reshape(N_PAIR, PAIR, head_dim))])
         o, dq, dk, dv, dr, du, dw = pl.pallas_call(
             writer,
             name="writer",

time: 222 us -> 221 us (level)
  no operation moved by 1% of the time
where the time goes in v3:
time: 221 us
  Pallas kernels  220 us (100%)
    pallas_call x1, Pallas kernels, local(): pl.pallas_call(kernel, name='rel_attn', out_shape=(act, act, act, act, *[...  214 us
    pallas_call x1, Pallas kernels, local(): pl.pallas_call(writer, name='writer', out_shape=(act, act, act, act, jax....  5.95 us

profile of v3, /device:TPU:0, one launch (start us, length us, event | category | flops | bytes accessed | tf_op | source)
XLA Modules:
  0.0 220.5 jit_solution(8119094270725189216)
XLA Ops:
  0.6 213.9 %rel_attn.1 = (bf16[8,64,8,2,128]{4,3,2,1,0:T(2,128)(2,1)S(1)}, bf16[8,64,8,2,128]{4,3,2,1,0:T(2,128)(2,1)S(1)}, bf16[8,64,8,2,128]{4,3,2,1,0:T(2,128)(2,1)S(1)}...) custom-call(bf16[8,64,8,2,128]{4,3,2,1,0:T(2,128)(2,1)} %bitcast.15,, ...), custom_call_target="tpu_custom_call" | custom-call | tf_op jit(solution)/shard_map/rel_attn/pallas_call | solution.py:307
  214.6 6.0 %writer.1 = (bf16[8,64,8,2,128]{4,3,2,1,0:T(2,128)(2,1)}, bf16[8,64,8,2,128]{4,3,2,1,0:T(2,128)(2,1)}, bf16[8,64,8,2,128]{4,3,2,1,0:T(2,128)(2,1)}, bf16[8,64,8,...) custom-call(bf16[8,64,8,2,128]{4,3,2,1,0:T(2,128)(2,1)S(1)} %get-tuple-el, ...), custom_call_target="tpu_custom_call" | custom-call | tf_op jit(solution)/shard_map/writer/pallas_call | solution.py:329

commit v4 on v3

v4 whole, which is shorter than its diff:
```python
import jax
import jax.numpy as jnp
from jax import lax
from jax.experimental import pallas as pl
from jax.experimental.pallas import tpu as pltpu
from jax.sharding import PartitionSpec as P

MESH = pl.DeviceIdType.MESH
BF16, F32 = jnp.bfloat16, jnp.float32
LOG2E = 1.4426950408889634

N_DEV = 16
PLANE = 8
PAIR = 2
N_PAIR = 8
SLOTS = 4
ROWS = 64
HALF = PLANE * ROWS
SEQ = 2 * HALF
HEAD = 128
QB = 256
WIN = HALF + QB
PARTS = ((0, 171), (171, 171), (342, 171), (513, 171), (684, 170), (854, 170))
HOPS = ((1, 2, 4), (2, 1, 4), (1, 2, 4), (2, 1, 4), (4, 1, 2), (4, 2, 1))
N_PART = len(PARTS)
TURNS = ((1, 3, 2), (3, 1, 2))


def dot(lhs, rhs):
    return jnp.dot(lhs, rhs, preferred_element_type=F32)


def flip8(x):
    rows, cols = x.shape
    idx = 7 - lax.broadcasted_iota(jnp.int32, (rows // 8, 8, cols), 1)
    return jnp.take_along_axis(x.reshape(rows // 8, 8, cols), idx, axis=1).reshape(rows, cols)


def eye_rev(dtype):
    total = lax.broadcasted_iota(jnp.int32, (HEAD, HEAD), 0) + lax.broadcasted_iota(jnp.int32, (HEAD, HEAD), 1)
    return jnp.where(total == HEAD - 1, 1.0, 0.0).astype(dtype)


def kernel(q_in, k_in, v_in, g_in, r_in, u_in, w_in,
           o_out, dq_out, dk_out, dv_out, dr0_out, dr1_out, dr2_out, dr3_out, dr4_out, dr5_out, du_out, dw_out,
           buf, rbuf, r_buf, u_buf, w_buf, st_tx, st_rx, st_ref, dr_rx, dr_rz, dr_fin, dr_acc,
           s_ref, e_ref, dp_ref, pb_ref, ds_ref, dd_ref,
           a_s, c_s, g_s, k_s, v_s, at_s, ct_s, gt_s, kt_s, vt_s, rev_s, rt_s, dkt, dvt, stage,
           in_send, in_recv, out_send, out_recv, own_sem, r_sem, up_send, up_recv, st_send, st_recv,
           x_send, x_recv, z_send, z_recv, ring_send, ring_recv, fw_send, fw_recv, b_send, b_recv):
    me = lax.axis_index("cp")
    core = me % 2
    chip = me // 2
    col = chip % 4
    z = chip // 4
    partner = me + 1 - 2 * core
    across = me + PLANE * (1 - 2 * z)
    scale = HEAD ** -0.5

    def wait_for(ref, sem):
        pltpu.make_async_copy(ref, ref, sem).wait()

    tables = [pltpu.make_async_copy(src, dst, r_sem.at[j]) for j, (src, dst) in enumerate(
        ((r_in.at[:, pl.ds(2 * col, 2)], r_buf), (u_in.at[pl.ds(2 * col, 2)], u_buf), (w_in.at[pl.ds(2 * col, 2)], w_buf)))]
    for copy in tables:
        copy.start()
    dr_rz[...] = jnp.zeros_like(dr_rz)

    barrier = pltpu.get_barrier_semaphore()

    def say(step, carry):
        pl.semaphore_signal(barrier, inc=1, device_id=((me + step) % N_DEV,), device_id_type=MESH)
        return carry

    lax.fori_loop(1, N_DEV, say, 0)
    pl.semaphore_wait(barrier, N_DEV - 1)

    my_rows = pl.ds(pl.multiple_of((me % PLANE) * ROWS, ROWS), ROWS)

    def peers():
        for near_turn, far_turn in zip(*TURNS):
            turn = jnp.where(core == 0, near_turn, far_turn)
            yield me ^ (2 * turn)
            yield me ^ (2 * turn + 1)
        yield partner

    def send_in(ins, slot):
        for first in (0, 2):
            for t in (first, first + 1):
                pltpu.make_async_copy(ins[t].at[core * SLOTS + slot, :, pl.ds(2 * col, 2)], buf.at[t, slot, my_rows], in_recv.at[t, slot]).start()
            for peer in peers():
                for t in (first, first + 1):
                    pltpu.make_async_remote_copy(
                        src_ref=ins[t].at[(peer % 2) * SLOTS + slot, :, pl.ds(2 * ((peer // 2) % 4), 2)], dst_ref=buf.at[t, slot, my_rows],
                        send_sem=in_send, recv_sem=in_recv.at[t, slot], device_id=(peer,), device_id_type=MESH).start()

    def send_all(ins):
        def send_slot(slot, carry):
            send_in(ins, slot)
            return carry
        lax.fori_loop(0, SLOTS, send_slot, 0)

    @pl.when(z == 0)
    def _():
        send_all((k_in, v_in, q_in, g_in))

    @pl.when(z == 1)
    def _():
        send_all((q_in, g_in, k_in, v_in))

    for copy in tables:
        copy.wait()
    rev = eye_rev(BF16)
    for p in range(2):
        pair_tab = pltpu.einshape("abc->bac", r_buf[:, p])
        for hh in range(PAIR):
            for blk in range(SEQ // HEAD):
                part = pair_tab[hh, SEQ - HEAD * (blk + 1):SEQ - HEAD * blk]
                flipped = dot(rev, part).astype(BF16)
                rev_s[2 * p + hh, HEAD * blk:HEAD * (blk + 1), :] = flipped
                rt_s[2 * p + hh, :, HEAD * blk:HEAD * (blk + 1)] = flipped.T
    dr_acc[...] = jnp.zeros_like(dr_acc)

    acts = (o_out, dq_out, dk_out, dv_out)

    def send_out(slot, which):
        for t in which:
            pltpu.make_async_copy(buf.at[t, slot, my_rows], acts[t].at[core * SLOTS + slot, :, pl.ds(2 * col, 2)], out_recv.at[t]).start()
        for peer in peers():
            peer_rows = pl.ds(pl.multiple_of((peer % PLANE) * ROWS, ROWS), ROWS)
            for t in which:
                pltpu.make_async_remote_copy(
                    src_ref=buf.at[t, slot, peer_rows], dst_ref=acts[t].at[core * SLOTS + slot, :, pl.ds(2 * col, 2)],
                    send_sem=out_send, recv_sem=out_recv.at[t], device_id=(peer,), device_id_type=MESH).start()

    def send_up(slot):
        for j in range(2):
            wait_for(buf.at[j, slot], in_recv.at[j, slot])
            pltpu.make_async_remote_copy(src_ref=buf.at[j, slot], dst_ref=rbuf.at[j, slot], send_sem=up_send.at[slot], recv_sem=up_recv.at[j, slot],
                                         device_id=(across,), device_id_type=MESH).start()

    def unpack(ref, j, slot, p):
        return pltpu.einshape("abc->bac", ref[j, slot, :, p])

    def load_rows(q_ref, q_j, g_ref, g_j, slot, p, start, turned):
        rows = slice(start, start + HALF)
        q2 = unpack(q_ref, q_j, slot, p)
        u = u_buf[p].astype(F32)
        w = w_buf[p].astype(F32)
        for hh in range(PAIR):
            q32 = q2[hh].astype(F32)
            a = (q32 + u[hh:hh + 1]).astype(BF16)
            c = (q32 + w[hh:hh + 1]).astype(BF16)
            a_s[hh, rows, :] = a
            c_s[hh, rows, :] = c
            at_s[hh, :, rows] = a.T
            if turned:
                ct_s[hh, :, rows] = flip8(c.astype(F32)).astype(BF16).T
        g2 = unpack(g_ref, g_j, slot, p)
        g_s[:, rows, :] = g2
        for hh in range(PAIR):
            gt_s[hh, :, rows] = g2[hh].T

    def load_keys(k_ref, k_j, v_ref, v_j, slot, p, start):
        rows = slice(start, start + HALF)
        k2 = unpack(k_ref, k_j, slot, p)
        v2 = unpack(v_ref, v_j, slot, p)
        k_s[:, rows, :] = k2
        v_s[:, rows, :] = v2
        for hh in range(PAIR):
            kt_s[hh, :, rows] = k2[hh].T
            vt_s[hh, :, rows] = v2[hh].T

    def row_block(hh, head, start, i0, lo, fresh, stats):
        width = i0 + QB
        rows = slice(start, start + QB)
        s_ref[:, :width] = dot(a_s[hh, rows, :], kt_s[hh, :, :width])
        e_ref[:, :width] = dot(c_s[hh, rows, :], rt_s[head, :, SEQ - width:])
        dp_ref[:, :width] = dot(g_s[hh, rows, :], vt_s[hh, :, :width])
        for r0 in range(0, QB, 16):
            group = slice(r0, r0 + 16)
            rel = pltpu.roll(e_ref[group, :width], i0 + 1 + r0, 1, stride=1, stride_axis=0)
            s = s_ref[group, :width] + rel
            ahead = lax.broadcasted_iota(jnp.int32, (16, width), 1) - lax.broadcasted_iota(jnp.int32, (16, width), 0)
            s = jnp.where(ahead <= i0 + r0, s, -jnp.inf)
            top = jnp.max(s, axis=1, keepdims=True)
            p = jnp.exp2((s - top) * (scale * LOG2E))
            total = jnp.sum(p, axis=1, keepdims=True)
            p = p * (1.0 / total)
            pb_ref[group, :width] = p.astype(BF16)
            dp = dp_ref[group, :width]
            row_dot = jnp.sum(p * dp, axis=1, keepdims=True)
            ds = (p * (dp - row_dot) * scale).astype(BF16)
            ds_ref[group, :width] = ds
            flipped = flip8(ds.astype(F32))
            half = [pltpu.roll(flipped[8 * j:8 * j + 8], QB - 8 - r0 - 8 * j, 1, stride=1, stride_axis=0) for j in range(2)]
            dd_ref[group, :width] = jnp.concatenate(half, axis=0).astype(BF16)
            if stats:
                lane = lax.broadcasted_iota(jnp.int32, (16, HEAD), 1)
                st_ref[group, :] = jnp.where(lane == 0, top * (scale * LOG2E) + jnp.log2(total), row_dot)
        pb = pb_ref[:, :width]
        ds = ds_ref[:, :width]
        dd = dd_ref[:, :width]
        stage[0, hh, rows, :] = dot(pb, v_s[hh, :width, :]).astype(BF16)
        dqc = dot(ds, k_s[hh, :width, :])
        dqr = flip8(dot(dd, rev_s[head, SEQ - width:, :]))
        stage[1, hh, rows, :] = (dqc + dqr).astype(BF16)
        dr_acc[head, HEAD:HEAD + 1, SEQ - HEAD:] += jnp.sum(dqc, axis=0, keepdims=True)
        dr_acc[head, HEAD + 1:HEAD + 2, SEQ - HEAD:] += jnp.sum(dqr, axis=0, keepdims=True)
        dk_new = dot(at_s[hh, :, rows], ds_ref[:, lo:width])
        dv_new = dot(gt_s[hh, :, rows], pb_ref[:, lo:width])
        if fresh:
            dkt[hh] = dk_new
            dvt[hh] = dv_new
        else:
            dkt[hh, :, :width - lo] += dk_new
            dvt[hh, :, :width - lo] += dv_new
        dr_acc[head, :HEAD, SEQ - width:] += dot(ct_s[hh, :, rows], dd)

    def col_block(hh, head, slot, i0):
        rows = slice(i0, i0 + QB)
        first = WIN - i0
        s_ref[:, :HALF] = dot(a_s[hh, rows, :], kt_s[hh, :, :HALF])
        e_ref[:, :WIN] = dot(c_s[hh, rows, :], rt_s[head, :, first:first + WIN])
        dp_ref[:, :HALF] = dot(g_s[hh, rows, :], vt_s[hh, :, :HALF])
        st_ref[:, :8] = st_rx[slot, head, :, i0 - HALF:i0 - HALF + QB].T
        for r0 in range(0, QB, 16):
            group = slice(r0, r0 + 16)
            rel = pltpu.roll(e_ref[group, :WIN], HALF + 1 + r0, 1, stride=1, stride_axis=0)[:, :HALF]
            log_sum = st_ref[group, 0:1]
            row_dot = st_ref[group, 1:2]
            p = jnp.exp2((s_ref[group, :HALF] + rel) * (scale * LOG2E) - log_sum)
            pb_ref[group, :HALF] = p.astype(BF16)
            ds_ref[group, :HALF] = (p * (dp_ref[group, :HALF] - row_dot) * scale).astype(BF16)
        dkt[hh] += dot(at_s[hh, :, rows], ds_ref[:, :HALF])
        dvt[hh] += dot(gt_s[hh, :, rows], pb_ref[:, :HALF])

    def store_pair(slot, p):
        for hh in range(PAIR):
            stage[2, hh] = dkt[hh].astype(BF16).T
            stage[3, hh] = dvt[hh].astype(BF16).T
        for t in range(4):
            buf[t, slot, :, p] = pltpu.einshape("abc->bac", stage[t])

    def lower_pair(slot, p):
        load_rows(buf, 2, buf, 3, slot, p, 0, True)
        load_rows(rbuf, 0, rbuf, 1, slot, p, HALF, False)
        load_keys(buf, 0, buf, 1, slot, p, 0)

        def own(hh, carry):
            row_block(hh, 2 * p + hh, QB, QB, 0, True, False)
            row_block(hh, 2 * p + hh, 0, 0, 0, False, False)
            return carry

        def theirs(hh, carry):
            head = 2 * p + hh
            wait_for(st_rx.at[slot, head], st_recv.at[slot, head])
            col_block(hh, head, slot, HALF)
            col_block(hh, head, slot, HALF + QB)
            return carry

        lax.fori_loop(0, PAIR, own, 0)
        lax.fori_loop(0, PAIR, theirs, 0)

    def upper_pair(slot, p):
        load_rows(buf, 0, buf, 1, slot, p, 0, True)
        load_keys(rbuf, 0, rbuf, 1, slot, p, 0)
        load_keys(buf, 2, buf, 3, slot, p, HALF)

        def own(hh, carry):
            head = 2 * p + hh
            for blk in (1, 0):
                row_block(hh, head, QB * blk, HALF + QB * blk, HALF, blk == 1, True)
                st_tx[slot, head, :, QB * blk:QB * (blk + 1)] = st_ref[...].T[:8]
            pltpu.make_async_remote_copy(src_ref=st_tx.at[slot, head], dst_ref=st_rx.at[slot, head], send_sem=st_send, recv_sem=st_recv.at[slot, head],
                                         device_id=(across,), device_id_type=MESH).start()
            return carry

        lax.fori_loop(0, PAIR, own, 0)

    send_up(0)

    def slot_body(slot, carry):
        @pl.when(slot < SLOTS - 1)
        def _():
            send_up(slot + 1)
        for j in range(2):
            wait_for(buf.at[2 + j, slot], in_recv.at[2 + j, slot])
            wait_for(rbuf.at[j, slot], up_recv.at[j, slot])
        wait_for(rbuf.at[:, slot], up_send.at[slot])

        def pair_body(p, carry):
            @pl.when(z == 0)
            def _():
                lower_pair(slot, p)

            @pl.when(z == 1)
            def _():
                upper_pair(slot, p)

            store_pair(slot, p)
            return carry

        lax.fori_loop(0, 2, pair_body, 0)

        @pl.when(slot < SLOTS - 2)
        def _():
            send_out(slot, range(4))
        return carry

    lax.fori_loop(0, SLOTS, slot_body, 0)
    send_out(SLOTS - 2, (0,))

    swaps = [pltpu.make_async_remote_copy(
        src_ref=dr_acc.at[2 * p + 1 - core], dst_ref=dr_rx.at[p], send_sem=x_send.at[p], recv_sem=x_recv.at[p],
        device_id=(partner,), device_id_type=MESH) for p in range(2)]
    for swap in swaps:
        swap.start()
    for swap in swaps:
        swap.wait()
    for p in range(2):
        dr_rx[p] = dr_rx[p] + dr_acc[2 * p + core]

    @pl.when(z == 0)
    def _():
        pltpu.make_async_remote_copy(src_ref=dr_rx.at[1, :, HALF:], dst_ref=dr_rz.at[:, HALF:], send_sem=z_send, recv_sem=z_recv,
                                     device_id=(across,), device_id_type=MESH).start()
        wait_for(dr_rz, z_recv)
        wait_for(dr_rz.at[:, HALF:], z_send)

    @pl.when(z == 1)
    def _():
        pltpu.make_async_remote_copy(src_ref=dr_rx.at[0], dst_ref=dr_rz, send_sem=z_send, recv_sem=z_recv,
                                     device_id=(across,), device_id_type=MESH).start()
        wait_for(dr_rz.at[:, HALF:], z_recv)
        wait_for(dr_rz, z_send)

    def head_of(bits):
        other = chip ^ bits
        return 4 * (other % 4) + 2 * (other // 4) + core

    head = head_of(0)
    total = dr_rx[z] + dr_rz[...]
    rev32 = eye_rev(F32)
    for blk in range(SEQ // HEAD):
        part = total[:HEAD, SEQ - HEAD * (blk + 1):SEQ - HEAD * blk]
        turned = lax.dot_general(rev32, part, (((1,), (1,)), ((), ())), precision=lax.Precision.HIGHEST, preferred_element_type=F32)
        dr_fin[HEAD * blk:HEAD * (blk + 1)] = turned.reshape(HEAD, 1, HEAD)
    dr_fin[SEQ] = total[HEAD:HEAD + 1, SEQ - HEAD:]
    dr_fin[SEQ + 1] = total[HEAD + 1:HEAD + 2, SEQ - HEAD:]

    parts = (dr0_out, dr1_out, dr2_out, dr3_out, dr4_out, dr5_out)

    def block(m, bits):
        if bits == 0:
            start, rows = PARTS[m]
            return dr_fin.at[start:start + rows]
        return parts[m].at[:, head_of(bits)]

    def forward(m, bits):
        pltpu.make_async_remote_copy(src_ref=block(m, bits), dst_ref=parts[m].at[:, head_of(bits)], send_sem=fw_send.at[m], recv_sem=fw_recv.at[m],
                                     device_id=(partner,), device_id_type=MESH).start()

    held = [[0] for _ in range(N_PART)]
    for m in range(N_PART):
        pltpu.make_async_copy(block(m, 0), parts[m].at[:, head], own_sem.at[m]).start()
    for hop in range(3):
        for m in range(N_PART):
            bit = HOPS[m][hop]
            for bits in held[m]:
                pltpu.make_async_remote_copy(
                    src_ref=block(m, bits), dst_ref=parts[m].at[:, head_of(bits)], send_sem=ring_send.at[m],
                    recv_sem=ring_recv.at[hop, m], device_id=(me ^ (2 * bit),), device_id_type=MESH).start()
        for m in range(N_PART):
            for bits in (held[m] if hop == 0 else held[m][len(held[m]) // 2:]):
                forward(m, bits)
        if hop == 0:
            for j, dst in enumerate((du_out, dw_out)):
                pltpu.make_async_copy(dr_fin.at[SEQ + j], dst.at[head], b_recv.at[j]).start()
                for step in range(1, N_DEV):
                    pltpu.make_async_remote_copy(
                        src_ref=dr_fin.at[SEQ + j], dst_ref=dst.at[head], send_sem=b_send.at[j], recv_sem=b_recv.at[j],
                        device_id=(me ^ step,), device_id_type=MESH).start()
        if hop == 0:
            send_out(SLOTS - 2, (1,))
        elif hop == 1:
            send_out(SLOTS - 2, (2,))
        else:
            send_out(SLOTS - 2, (3,))
            send_out(SLOTS - 1, range(4))
        for m in range(N_PART):
            count = len(held[m])
            wait_for(parts[m].at[:, :count], ring_recv.at[hop, m])
            held[m] = held[m] + [bits ^ HOPS[m][hop] for bits in held[m]]
            if hop == 2:
                for bits in held[m][4:]:
                    forward(m, bits)

    for t, dst in enumerate(acts):
        wait_for(dst, out_recv.at[t])
    for j, dst in enumerate((du_out, dw_out)):
        wait_for(dst, b_recv.at[j])
        wait_for(dst.at[:N_DEV - 1], b_send.at[j])
    wait_for(buf.at[:, :, :HALF - ROWS], in_send)
    wait_for(buf.at[:, :, :HALF - ROWS], out_send)

    @pl.when(z == 1)
    def _():
        wait_for(st_tx, st_send)

    for m in range(N_PART):
        wait_for(parts[m].at[:, head], own_sem.at[m])
        wait_for(parts[m].at[:, :N_PAIR - 1], ring_send.at[m])
        wait_for(parts[m].at[:, :N_PAIR], fw_send.at[m])
        wait_for(parts[m].at[:, :N_PAIR], fw_recv.at[m])


def writer(*refs):
    ins, (o, dq, dk, dv, dr, du, dw, sem) = refs[:6 + N_PART], refs[6 + N_PART:]
    pairs = list(zip(ins[:4] + ins[-2:], (o, dq, dk, dv, du, dw)))
    for part, (start, rows) in zip(ins[4:-2], PARTS):
        pairs.append((part, dr.at[start:start + rows]))
    copies = [pltpu.make_async_copy(src, dst, sem.at[j]) for j, (src, dst) in enumerate(pairs)]
    for copy in copies:
        copy.start()
    for copy in copies:
        copy.wait()


def solution(mesh):
    seq_spec = P(None, "cp", None, None)

    def local(query, key_in, value, bias_u, bias_w, rel_k, d_out):
        n_batch, rows, n_heads, head_dim = query.shape
        pairs = (n_batch, rows, N_PAIR, PAIR, head_dim)
        vm = pltpu.VMEM
        dma = pltpu.SemaphoreType.DMA
        whole = pl.BlockSpec(memory_space=pl.ANY)
        act = jax.ShapeDtypeStruct(pairs, BF16)
        vec = jax.ShapeDtypeStruct((n_heads, 1, head_dim), F32)
        tok = (PAIR, SEQ, HEAD)
        tok_t = (PAIR, HEAD, SEQ)
        acc = (HEAD + 8, SEQ)
        outs = pl.pallas_call(
            kernel,
            name="rel_attn",
            out_shape=(act, act, act, act,
                       *[jax.ShapeDtypeStruct((part_rows, n_heads, 1, head_dim), F32) for _, part_rows in PARTS],
                       vec, vec),
            in_specs=[pl.BlockSpec(memory_space=pltpu.HBM)] * 7,
            out_specs=[whole] * (6 + N_PART),
            scratch_shapes=[
                vm((4, SLOTS, HALF, 2, PAIR, HEAD), BF16), vm((2, SLOTS, HALF, 2, PAIR, HEAD), BF16),
                vm((SEQ, 2, PAIR, HEAD), BF16), vm((2, PAIR, HEAD), BF16), vm((2, PAIR, HEAD), BF16),
                vm((SLOTS, 4, 8, HALF), F32), vm((SLOTS, 4, 8, HALF), F32), vm((QB, HEAD), F32),
                vm((2,) + acc, F32), vm(acc, F32), vm((SEQ + 2, 1, HEAD), F32), vm((4,) + acc, F32),
                vm((QB, SEQ), F32), vm((QB, SEQ), F32), vm((QB, SEQ), F32),
                vm((QB, SEQ), BF16), vm((QB, SEQ), BF16), vm((QB, SEQ), BF16),
                vm(tok, BF16), vm(tok, BF16), vm(tok, BF16), vm(tok, BF16), vm(tok, BF16),
                vm(tok_t, BF16), vm(tok_t, BF16), vm(tok_t, BF16), vm(tok_t, BF16), vm(tok_t, BF16),
                vm((4, SEQ, HEAD), BF16), vm((4, HEAD, SEQ), BF16),
                vm((PAIR, HEAD, HALF), F32), vm((PAIR, HEAD, HALF), F32), vm((4, PAIR, HALF, HEAD), BF16),
                dma, dma((4, SLOTS)), dma, dma((4,)), dma((N_PART,)), dma((3,)), dma((SLOTS,)), dma((2, SLOTS)), dma, dma((SLOTS, 4)),
                dma((2,)), dma((2,)), dma, dma, dma((N_PART,)), dma((3, N_PART)), dma((N_PART,)), dma((N_PART,)), dma((2,)), dma((2,)),
            ],
            compiler_params=pltpu.CompilerParams(collective_id=0, has_side_effects=True, vmem_limit_bytes=36 * 1024 * 1024),
        )(*[pltpu.with_memory_space_constraint(x, pltpu.HBM) for x in (
            query.reshape(pairs), key_in.reshape(pairs), value.reshape(pairs), d_out.reshape(pairs),
            rel_k.reshape(SEQ, N_PAIR, PAIR, head_dim), bias_u.reshape(N_PAIR, PAIR, head_dim), bias_w.reshape(N_PAIR, PAIR, head_dim))])
        o, dq, dk, dv, dr, du, dw = pl.pallas_call(
            writer,
            name="writer",
            out_shape=(act, act, act, act, jax.ShapeDtypeStruct((SEQ, n_heads, 1, head_dim), F32), vec, vec),
            in_specs=[whole] * (6 + N_PART),
            out_specs=[whole] * 7,
            scratch_shapes=[dma((6 + N_PART,))],
            compiler_params=pltpu.CompilerParams(vmem_limit_bytes=1024 * 1024),
        )(*outs)
        full = query.shape
        return (o.reshape(full), dq.reshape(full), dk.reshape(full), dv.reshape(full),
                du.reshape(bias_u.shape), dw.reshape(bias_w.shape), dr.reshape(rel_k.shape))

    return jax.shard_map(local, mesh=mesh,
                         in_specs=(seq_spec, seq_spec, seq_spec, P(), P(), P(), seq_spec),
                         out_specs=(seq_spec, seq_spec, seq_spec, seq_spec, P(), P(), P()),
                         check_vma=False)
```

time: 221 us -> 235 us (1.063)
  Pallas kernels: 220 us -> 234 us
    pallas_call x1, Pallas kernels: 214 us -> 228 us  [local(): pl.pallas_call(kernel, name='rel_attn', out_shape=(act, act, act, act, *[...]
where the time goes in v4:
time: 235 us
  Pallas kernels  234 us (100%)
    pallas_call x1, Pallas kernels, local(): pl.pallas_call(kernel, name='rel_attn', out_shape=(act, act, act, act, *[...  228 us
    pallas_call x1, Pallas kernels, local(): pl.pallas_call(writer, name='writer', out_shape=(act, act, act, act, jax....  5.95 us

profile of v4, /device:TPU:0, one launch (start us, length us, event | category | flops | bytes accessed | tf_op | source)
XLA Modules:
  0.0 234.9 jit_solution(6750256799821369080)
XLA Ops:
  0.6 228.2 %rel_attn.1 = (bf16[8,64,8,2,128]{4,3,2,1,0:T(2,128)(2,1)S(1)}, bf16[8,64,8,2,128]{4,3,2,1,0:T(2,128)(2,1)S(1)}, bf16[8,64,8,2,128]{4,3,2,1,0:T(2,128)(2,1)S(1)}...) custom-call(bf16[8,64,8,2,128]{4,3,2,1,0:T(2,128)(2,1)} %bitcast.15,, ...), custom_call_target="tpu_custom_call" | custom-call | tf_op jit(solution)/shard_map/rel_attn/pallas_call | solution.py:444
  228.8 6.0 %writer.1 = (bf16[8,64,8,2,128]{4,3,2,1,0:T(2,128)(2,1)}, bf16[8,64,8,2,128]{4,3,2,1,0:T(2,128)(2,1)}, bf16[8,64,8,2,128]{4,3,2,1,0:T(2,128)(2,1)}, bf16[8,64,8,...) custom-call(bf16[8,64,8,2,128]{4,3,2,1,0:T(2,128)(2,1)S(1)} %get-tuple-el, ...), custom_call_target="tpu_custom_call" | custom-call | tf_op jit(solution)/shard_map/writer/pallas_call | solution.py:470

commit v5 on v4

v5 whole, which is shorter than its diff:
```python
import jax
import jax.numpy as jnp
from jax import lax
from jax.experimental import pallas as pl
from jax.experimental.pallas import tpu as pltpu
from jax.sharding import PartitionSpec as P

MESH = pl.DeviceIdType.MESH
BF16, F32 = jnp.bfloat16, jnp.float32
LOG2E = 1.4426950408889634

N_DEV = 16
PLANE = 8
PAIR = 2
N_PAIR = 8
SLOTS = 4
SUBS = 2 * SLOTS
EARLY = 2
ROWS = 64
HALF = PLANE * ROWS
SEQ = 2 * HALF
HEAD = 128
QB = 256
WIN = HALF + QB
N_PART = 4
PART = HALF // N_PART
HOPS = ((1, 2, 4), (2, 1, 4), (1, 2, 4), (2, 1, 4))
TURNS = ((1, 3, 2), (3, 1, 2))


def dot(lhs, rhs):
    return jnp.dot(lhs, rhs, preferred_element_type=F32)


def flip8(x):
    rows, cols = x.shape
    idx = 7 - lax.broadcasted_iota(jnp.int32, (rows // 8, 8, cols), 1)
    return jnp.take_along_axis(x.reshape(rows // 8, 8, cols), idx, axis=1).reshape(rows, cols)


def eye_rev(dtype):
    total = lax.broadcasted_iota(jnp.int32, (HEAD, HEAD), 0) + lax.broadcasted_iota(jnp.int32, (HEAD, HEAD), 1)
    return jnp.where(total == HEAD - 1, 1.0, 0.0).astype(dtype)


def kernel(q_in, k_in, v_in, g_in, r_in, u_in, w_in,
           o_out, dq_out, dk_out, dv_out, dr0_out, dr1_out, dr2_out, dr3_out, du_out, dw_out,
           buf, rbuf, r_buf, u_buf, w_buf, st_tx, st_rx, st_ref, dr_rx, dr_fin, dr_acc,
           s_ref, e_ref, dp_ref, pb_ref, ds_ref, dd_ref,
           a_s, c_s, g_s, k_s, v_s, at_s, ct_s, gt_s, kt_s, vt_s, rev_s, rt_s, dkt, dvt, stage,
           in_send, in_recv, out_send, out_recv, own_sem, r_sem, up_send, up_recv, st_send, st_recv,
           x_send, x_recv, ring_send, ring_recv, fw_send, fw_recv, b_send, b_recv):
    me = lax.axis_index("cp")
    core = me % 2
    chip = me // 2
    col = chip % 4
    z = chip // 4
    partner = me + 1 - 2 * core
    across = me + PLANE * (1 - 2 * z)
    scale = HEAD ** -0.5

    def wait_for(ref, sem):
        pltpu.make_async_copy(ref, ref, sem).wait()

    tables = [pltpu.make_async_copy(src, dst, r_sem.at[j]) for j, (src, dst) in enumerate(
        ((r_in.at[:, pl.ds(2 * col, 2)], r_buf), (u_in.at[pl.ds(2 * col, 2)], u_buf), (w_in.at[pl.ds(2 * col, 2)], w_buf)))]
    for copy in tables:
        copy.start()

    barrier = pltpu.get_barrier_semaphore()

    def say(step, carry):
        pl.semaphore_signal(barrier, inc=1, device_id=((me + step) % N_DEV,), device_id_type=MESH)
        return carry

    lax.fori_loop(1, N_DEV, say, 0)
    pl.semaphore_wait(barrier, N_DEV - 1)

    my_rows = pl.ds(pl.multiple_of((me % PLANE) * ROWS, ROWS), ROWS)

    def peers():
        for near_turn, far_turn in zip(*TURNS):
            turn = jnp.where(core == 0, near_turn, far_turn)
            yield me ^ (2 * turn)
            yield me ^ (2 * turn + 1)
        yield partner

    def send_in(ins, sub):
        pair, row = sub // SLOTS, sub % SLOTS
        for first in (0, 2):
            for t in (first, first + 1):
                pltpu.make_async_copy(ins[t].at[core * SLOTS + row, :, 2 * col + pair], buf.at[t, sub, my_rows], in_recv.at[t, sub]).start()
            for peer in peers():
                for t in (first, first + 1):
                    pltpu.make_async_remote_copy(
                        src_ref=ins[t].at[(peer % 2) * SLOTS + row, :, 2 * ((peer // 2) % 4) + pair], dst_ref=buf.at[t, sub, my_rows],
                        send_sem=in_send, recv_sem=in_recv.at[t, sub], device_id=(peer,), device_id_type=MESH).start()

    def send_all(ins):
        def send_sub(sub, carry):
            send_in(ins, sub)
            return carry
        lax.fori_loop(0, SUBS, send_sub, 0)

    @pl.when(z == 0)
    def _():
        send_all((k_in, v_in, q_in, g_in))

    @pl.when(z == 1)
    def _():
        send_all((q_in, g_in, k_in, v_in))

    for copy in tables:
        copy.wait()
    rev = eye_rev(BF16)
    for p in range(2):
        pair_tab = pltpu.einshape("abc->bac", r_buf[:, p])
        for hh in range(PAIR):
            for blk in range(SEQ // HEAD):
                part = pair_tab[hh, SEQ - HEAD * (blk + 1):SEQ - HEAD * blk]
                flipped = dot(rev, part).astype(BF16)
                rev_s[2 * p + hh, HEAD * blk:HEAD * (blk + 1), :] = flipped
                rt_s[2 * p + hh, :, HEAD * blk:HEAD * (blk + 1)] = flipped.T
    dr_acc[...] = jnp.zeros_like(dr_acc)

    acts = (dk_out, dv_out, o_out, dq_out)

    def send_out(sub, which):
        place = (core * SLOTS + sub % SLOTS, slice(None), 2 * col + sub // SLOTS)
        for t in which:
            pltpu.make_async_copy(buf.at[t, sub, my_rows], acts[t].at[place], out_recv.at[t]).start()
        for peer in peers():
            peer_rows = pl.ds(pl.multiple_of((peer % PLANE) * ROWS, ROWS), ROWS)
            for t in which:
                pltpu.make_async_remote_copy(
                    src_ref=buf.at[t, sub, peer_rows], dst_ref=acts[t].at[place],
                    send_sem=out_send, recv_sem=out_recv.at[t], device_id=(peer,), device_id_type=MESH).start()

    def send_up(sub):
        for j in range(2):
            wait_for(buf.at[j, sub], in_recv.at[j, sub])
            pltpu.make_async_remote_copy(src_ref=buf.at[j, sub], dst_ref=rbuf.at[j, sub], send_sem=up_send.at[sub], recv_sem=up_recv.at[j, sub],
                                         device_id=(across,), device_id_type=MESH).start()

    def unpack(ref, j, sub):
        return pltpu.einshape("abc->bac", ref[j, sub])

    def load_rows(q_ref, q_j, g_ref, g_j, sub, start, turned):
        rows = slice(start, start + HALF)
        p = sub // SLOTS
        q2 = unpack(q_ref, q_j, sub)
        u = u_buf[p].astype(F32)
        w = w_buf[p].astype(F32)
        for hh in range(PAIR):
            q32 = q2[hh].astype(F32)
            a = (q32 + u[hh:hh + 1]).astype(BF16)
            c = (q32 + w[hh:hh + 1]).astype(BF16)
            a_s[hh, rows, :] = a
            c_s[hh, rows, :] = c
            at_s[hh, :, rows] = a.T
            if turned:
                ct_s[hh, :, rows] = flip8(c.astype(F32)).astype(BF16).T
        g2 = unpack(g_ref, g_j, sub)
        g_s[:, rows, :] = g2
        for hh in range(PAIR):
            gt_s[hh, :, rows] = g2[hh].T

    def load_keys(k_ref, k_j, v_ref, v_j, sub, start):
        rows = slice(start, start + HALF)
        k2 = unpack(k_ref, k_j, sub)
        v2 = unpack(v_ref, v_j, sub)
        k_s[:, rows, :] = k2
        v_s[:, rows, :] = v2
        for hh in range(PAIR):
            kt_s[hh, :, rows] = k2[hh].T
            vt_s[hh, :, rows] = v2[hh].T

    def row_block(hh, head, start, i0, lo, fresh, stats):
        width = i0 + QB
        rows = slice(start, start + QB)
        s_ref[:, :width] = dot(a_s[hh, rows, :], kt_s[hh, :, :width])
        e_ref[:, :width] = dot(c_s[hh, rows, :], rt_s[head, :, SEQ - width:])
        dp_ref[:, :width] = dot(g_s[hh, rows, :], vt_s[hh, :, :width])
        for r0 in range(0, QB, 16):
            group = slice(r0, r0 + 16)
            rel = pltpu.roll(e_ref[group, :width], i0 + 1 + r0, 1, stride=1, stride_axis=0)
            s = s_ref[group, :width] + rel
            ahead = lax.broadcasted_iota(jnp.int32, (16, width), 1) - lax.broadcasted_iota(jnp.int32, (16, width), 0)
            s = jnp.where(ahead <= i0 + r0, s, -jnp.inf)
            top = jnp.max(s, axis=1, keepdims=True)
            p = jnp.exp2((s - top) * (scale * LOG2E))
            total = jnp.sum(p, axis=1, keepdims=True)
            p = p * (1.0 / total)
            pb_ref[group, :width] = p.astype(BF16)
            dp = dp_ref[group, :width]
            row_dot = jnp.sum(p * dp, axis=1, keepdims=True)
            ds = (p * (dp - row_dot) * scale).astype(BF16)
            ds_ref[group, :width] = ds
            flipped = flip8(ds.astype(F32))
            half = [pltpu.roll(flipped[8 * j:8 * j + 8], QB - 8 - r0 - 8 * j, 1, stride=1, stride_axis=0) for j in range(2)]
            dd_ref[group, :width] = jnp.concatenate(half, axis=0).astype(BF16)
            if stats:
                lane = lax.broadcasted_iota(jnp.int32, (16, HEAD), 1)
                st_ref[group, :] = jnp.where(lane == 0, top * (scale * LOG2E) + jnp.log2(total), row_dot)
        pb = pb_ref[:, :width]
        ds = ds_ref[:, :width]
        dd = dd_ref[:, :width]
        stage[0, hh, rows, :] = dot(pb, v_s[hh, :width, :]).astype(BF16)
        dqc = dot(ds, k_s[hh, :width, :])
        dqr = flip8(dot(dd, rev_s[head, SEQ - width:, :]))
        stage[1, hh, rows, :] = (dqc + dqr).astype(BF16)
        dr_acc[head, 1, HEAD:HEAD + 1, HALF - HEAD:] += jnp.sum(dqc, axis=0, keepdims=True)
        dr_acc[head, 1, HEAD + 1:HEAD + 2, HALF - HEAD:] += jnp.sum(dqr, axis=0, keepdims=True)
        dk_new = dot(at_s[hh, :, rows], ds_ref[:, lo:width])
        dv_new = dot(gt_s[hh, :, rows], pb_ref[:, lo:width])
        if fresh:
            dkt[hh] = dk_new
            dvt[hh] = dv_new
        else:
            dkt[hh, :, :width - lo] += dk_new
            dvt[hh, :, :width - lo] += dv_new
        dr_new = dot(ct_s[hh, :, rows], dd)
        if width > HALF:
            dr_acc[head, 0, :HEAD, SEQ - width:] += dr_new[:, :width - HALF]
            dr_acc[head, 1, :HEAD, :] += dr_new[:, width - HALF:]
        else:
            dr_acc[head, 1, :HEAD, HALF - width:] += dr_new

    def col_block(hh, head, sub, i0):
        rows = slice(i0, i0 + QB)
        first = WIN - i0
        s_ref[:, :HALF] = dot(a_s[hh, rows, :], kt_s[hh, :, :HALF])
        e_ref[:, :WIN] = dot(c_s[hh, rows, :], rt_s[head, :, first:first + WIN])
        dp_ref[:, :HALF] = dot(g_s[hh, rows, :], vt_s[hh, :, :HALF])
        st_ref[:, :8] = st_rx[sub, hh, :, i0 - HALF:i0 - HALF + QB].T
        for r0 in range(0, QB, 16):
            group = slice(r0, r0 + 16)
            rel = pltpu.roll(e_ref[group, :WIN], HALF + 1 + r0, 1, stride=1, stride_axis=0)[:, :HALF]
            log_sum = st_ref[group, 0:1]
            row_dot = st_ref[group, 1:2]
            p = jnp.exp2((s_ref[group, :HALF] + rel) * (scale * LOG2E) - log_sum)
            pb_ref[group, :HALF] = p.astype(BF16)
            ds_ref[group, :HALF] = (p * (dp_ref[group, :HALF] - row_dot) * scale).astype(BF16)
        dkt[hh] += dot(at_s[hh, :, rows], ds_ref[:, :HALF])
        dvt[hh] += dot(gt_s[hh, :, rows], pb_ref[:, :HALF])

    def store_rows(sub):
        for t in range(2):
            buf[2 + t, sub] = pltpu.einshape("abc->bac", stage[t])

    def store_keys(sub):
        for hh in range(PAIR):
            stage[2, hh] = dkt[hh].astype(BF16).T
            stage[3, hh] = dvt[hh].astype(BF16).T
        for t in range(2):
            buf[t, sub] = pltpu.einshape("abc->bac", stage[2 + t])

    def wait_up(sub):
        for j in range(2):
            wait_for(rbuf.at[j, sub], up_recv.at[j, sub])
        wait_for(rbuf.at[:, sub], up_send.at[sub])

    def wait_in(sub):
        for j in range(2, 4):
            wait_for(buf.at[j, sub], in_recv.at[j, sub])

    def lower_own(sub):
        wait_in(sub)
        load_rows(buf, 2, buf, 3, sub, 0, True)
        load_keys(buf, 0, buf, 1, sub, 0)

        def own(hh, carry):
            head = 2 * (sub // SLOTS) + hh
            row_block(hh, head, QB, QB, 0, True, False)
            row_block(hh, head, 0, 0, 0, False, False)
            return carry

        lax.fori_loop(0, PAIR, own, 0)
        store_rows(sub)

    def lower_theirs(sub):
        wait_up(sub)
        load_rows(rbuf, 0, rbuf, 1, sub, HALF, False)

        def theirs(hh, carry):
            head = 2 * (sub // SLOTS) + hh
            wait_for(st_rx.at[sub, hh], st_recv.at[sub, hh])
            col_block(hh, head, sub, HALF)
            col_block(hh, head, sub, HALF + QB)
            return carry

        lax.fori_loop(0, PAIR, theirs, 0)
        store_keys(sub)

    def upper_own(sub):
        wait_in(sub)
        wait_up(sub)
        load_rows(buf, 0, buf, 1, sub, 0, True)
        load_keys(rbuf, 0, rbuf, 1, sub, 0)
        load_keys(buf, 2, buf, 3, sub, HALF)

        def own(hh, carry):
            head = 2 * (sub // SLOTS) + hh
            for blk in (1, 0):
                row_block(hh, head, QB * blk, HALF + QB * blk, HALF, blk == 1, True)
                st_tx[sub, hh, :, QB * blk:QB * (blk + 1)] = st_ref[...].T[:8]
            pltpu.make_async_remote_copy(src_ref=st_tx.at[sub, hh], dst_ref=st_rx.at[sub, hh], send_sem=st_send, recv_sem=st_recv.at[sub, hh],
                                         device_id=(across,), device_id_type=MESH).start()
            return carry

        lax.fori_loop(0, PAIR, own, 0)
        store_rows(sub)
        store_keys(sub)

    side = 1 - core
    parts = (dr0_out, dr1_out, dr2_out, dr3_out)

    def swap_start(p):
        for n, (device, top, end) in enumerate(((partner, z, 1 - core), (across, 1 - z, core), (across + 1 - 2 * core, 1 - z, 1 - core))):
            pltpu.make_async_remote_copy(src_ref=dr_acc.at[2 * p + top, end], dst_ref=dr_rx.at[p, n], send_sem=x_send.at[p], recv_sem=x_recv.at[p, n],
                                         device_id=(device,), device_id_type=MESH).start()

    def head_of(p, bits):
        other = chip ^ bits
        return 4 * (other % 4) + 2 * p + other // 4

    def block(p, m, bits):
        if bits == 0:
            return dr_fin.at[p, PART * m:PART * (m + 1)]
        return parts[m].at[side, :, head_of(p, bits)]

    def forward(p, m, bits):
        pltpu.make_async_remote_copy(src_ref=block(p, m, bits), dst_ref=parts[m].at[side, :, head_of(p, bits)], send_sem=fw_send.at[p, m],
                                     recv_sem=fw_recv.at[p, m], device_id=(partner,), device_id_type=MESH).start()

    def held(m, hop):
        have = [0]
        for bit in HOPS[m][:hop]:
            have = have + [bits ^ bit for bits in have]
        return have

    def hop_start(p, hop):
        for m in range(N_PART):
            for bits in held(m, hop):
                pltpu.make_async_remote_copy(
                    src_ref=block(p, m, bits), dst_ref=parts[m].at[side, :, head_of(p, bits)], send_sem=ring_send.at[p, m],
                    recv_sem=ring_recv.at[p, hop, m], device_id=(me ^ (2 * HOPS[m][hop]),), device_id_type=MESH).start()

    def hop_wait(p, hop):
        for m in range(N_PART):
            have = held(m, hop + 1)
            wait_for(parts[m].at[0, :, :len(have) // 2], ring_recv.at[p, hop, m])
            for bits in have[len(have) // 2:]:
                forward(p, m, bits)

    def swap_finish(p):
        for n in range(3):
            wait_for(dr_rx.at[p, n], x_recv.at[p, n])
        total = dr_acc[2 * p + z, core] + dr_rx[p, 0] + dr_rx[p, 1] + dr_rx[p, 2]
        rev32 = eye_rev(F32)
        for m in range(N_PART):
            part = total[:HEAD, HALF - HEAD * (m + 1):HALF - HEAD * m]
            turned = lax.dot_general(rev32, part, (((1,), (1,)), ((), ())), precision=lax.Precision.HIGHEST, preferred_element_type=F32)
            dr_fin[p, HEAD * m:HEAD * (m + 1)] = turned.reshape(HEAD, 1, HEAD)
        dr_fin[p, HALF] = total[HEAD:HEAD + 1, HALF - HEAD:]
        dr_fin[p, HALF + 1] = total[HEAD + 1:HEAD + 2, HALF - HEAD:]
        hop_start(p, 0)
        head = head_of(p, 0)
        for m in range(N_PART):
            pltpu.make_async_copy(block(p, m, 0), parts[m].at[side, :, head], own_sem.at[p, m]).start()
            forward(p, m, 0)

        @pl.when(core == 1)
        def _():
            for j, dst in enumerate((du_out, dw_out)):
                pltpu.make_async_copy(dr_fin.at[p, HALF + j], dst.at[head], b_recv.at[j]).start()
                for step in range(1, N_DEV):
                    pltpu.make_async_remote_copy(
                        src_ref=dr_fin.at[p, HALF + j], dst_ref=dst.at[head], send_sem=b_send.at[j], recv_sem=b_recv.at[j],
                        device_id=(me ^ step,), device_id_type=MESH).start()

    send_up(0)

    def sub_body(sub, carry):
        @pl.when(sub < SUBS - 1)
        def _():
            send_up(sub + 1)

        @pl.when(sub == SLOTS)
        def _():
            swap_start(0)

        @pl.when(sub == SLOTS + 2)
        def _():
            swap_finish(0)

        @pl.when((z == 0) & (sub > 0))
        def _():
            lower_theirs(sub - 1)

        @pl.when((z == 0) & (sub < SUBS))
        def _():
            lower_own(sub)

        @pl.when((z == 1) & (sub < SUBS))
        def _():
            upper_own(sub)

        @pl.when(sub < EARLY)
        def _():
            send_out(sub, (2, 3))

        @pl.when((sub > 0) & (sub <= EARLY))
        def _():
            send_out(sub - 1, (0, 1))
        return carry

    lax.fori_loop(0, SUBS + 1, sub_body, 0)

    swap_start(1)
    send_out(EARLY, range(4))
    hop_wait(0, 0)
    hop_start(0, 1)
    swap_finish(1)
    send_out(EARLY + 1, range(4))
    hop_wait(0, 1)
    hop_start(0, 2)
    hop_wait(1, 0)
    hop_start(1, 1)
    send_out(EARLY + 2, range(4))
    hop_wait(1, 1)
    hop_start(1, 2)

    def send_late(sub, carry):
        send_out(sub, range(4))
        return carry

    lax.fori_loop(EARLY + 3, SUBS, send_late, 0)
    hop_wait(0, 2)
    hop_wait(1, 2)

    for t, dst in enumerate(acts):
        wait_for(dst, out_recv.at[t])
    for j, dst in enumerate((du_out, dw_out)):
        wait_for(dst, b_recv.at[j])

        @pl.when(core == 1)
        def _():
            wait_for(dr_fin.at[0, :2 * (N_DEV - 1)], b_send.at[j])
    wait_for(buf.at[:, :, :HALF - ROWS], in_send)
    wait_for(buf.at[:, :, :HALF - ROWS], out_send)

    @pl.when(z == 1)
    def _():
        wait_for(st_tx, st_send)

    for p in range(2):
        wait_for(dr_rx.at[p], x_send.at[p])
        for m in range(N_PART):
            wait_for(dr_fin.at[p, :PART], own_sem.at[p, m])
            wait_for(parts[m].at[0, :, :N_PAIR - 1], ring_send.at[p, m])
            wait_for(parts[m].at[0, :, :N_PAIR], fw_send.at[p, m])
            wait_for(parts[m].at[0, :, :N_PAIR], fw_recv.at[p, m])


def writer(*refs):
    ins, (o, dq, dk, dv, dr, du, dw, sem) = refs[:6 + N_PART], refs[6 + N_PART:]
    pairs = list(zip(ins[:4] + ins[-2:], (o, dq, dk, dv, du, dw)))
    for m, part in enumerate(ins[4:-2]):
        for side in range(2):
            start = HALF * side + PART * m
            pairs.append((part.at[side], dr.at[start:start + PART]))
    copies = [pltpu.make_async_copy(src, dst, sem.at[j]) for j, (src, dst) in enumerate(pairs)]
    for copy in copies:
        copy.start()
    for copy in copies:
        copy.wait()


def solution(mesh):
    seq_spec = P(None, "cp", None, None)

    def local(query, key_in, value, bias_u, bias_w, rel_k, d_out):
        n_batch, rows, n_heads, head_dim = query.shape
        pairs = (n_batch, rows, N_PAIR, PAIR, head_dim)
        vm = pltpu.VMEM
        dma = pltpu.SemaphoreType.DMA
        whole = pl.BlockSpec(memory_space=pl.ANY)
        act = jax.ShapeDtypeStruct(pairs, BF16)
        vec = jax.ShapeDtypeStruct((n_heads, 1, head_dim), F32)
        tok = (PAIR, SEQ, HEAD)
        tok_t = (PAIR, HEAD, SEQ)
        acc = (HEAD + 8, HALF)
        outs = pl.pallas_call(
            kernel,
            name="rel_attn",
            out_shape=(act, act, act, act,
                       *[jax.ShapeDtypeStruct((2, PART, n_heads, 1, head_dim), F32)] * N_PART,
                       vec, vec),
            in_specs=[pl.BlockSpec(memory_space=pltpu.HBM)] * 7,
            out_specs=[whole] * (6 + N_PART),
            scratch_shapes=[
                vm((4, SUBS, HALF, PAIR, HEAD), BF16), vm((2, SUBS, HALF, PAIR, HEAD), BF16),
                vm((SEQ, 2, PAIR, HEAD), BF16), vm((2, PAIR, HEAD), BF16), vm((2, PAIR, HEAD), BF16),
                vm((SUBS, PAIR, 8, HALF), F32), vm((SUBS, PAIR, 8, HALF), F32), vm((QB, HEAD), F32),
                vm((2, 3) + acc, F32), vm((2, HALF + 2, 1, HEAD), F32), vm((4, 2) + acc, F32),
                vm((QB, SEQ), F32), vm((QB, SEQ), F32), vm((QB, SEQ), F32),
                vm((QB, SEQ), BF16), vm((QB, SEQ), BF16), vm((QB, SEQ), BF16),
                vm(tok, BF16), vm(tok, BF16), vm(tok, BF16), vm(tok, BF16), vm(tok, BF16),
                vm(tok_t, BF16), vm(tok_t, BF16), vm(tok_t, BF16), vm(tok_t, BF16), vm(tok_t, BF16),
                vm((4, SEQ, HEAD), BF16), vm((4, HEAD, SEQ), BF16),
                vm((PAIR, HEAD, HALF), F32), vm((PAIR, HEAD, HALF), F32), vm((4, PAIR, HALF, HEAD), BF16),
                dma, dma((4, SUBS)), dma, dma((4,)), dma((2, N_PART)), dma((3,)), dma((SUBS,)), dma((2, SUBS)), dma, dma((SUBS, PAIR)),
                dma((2,)), dma((2, 3)), dma((2, N_PART)), dma((2, 3, N_PART)), dma((2, N_PART)), dma((2, N_PART)), dma((2,)), dma((2,)),
            ],
            compiler_params=pltpu.CompilerParams(collective_id=0, has_side_effects=True, vmem_limit_bytes=36 * 1024 * 1024),
        )(*[pltpu.with_memory_space_constraint(x, pltpu.HBM) for x in (
            query.reshape(pairs), key_in.reshape(pairs), value.reshape(pairs), d_out.reshape(pairs),
            rel_k.reshape(SEQ, N_PAIR, PAIR, head_dim), bias_u.reshape(N_PAIR, PAIR, head_dim), bias_w.reshape(N_PAIR, PAIR, head_dim))])
        o, dq, dk, dv, dr, du, dw = pl.pallas_call(
            writer,
            name="writer",
            out_shape=(act, act, act, act, jax.ShapeDtypeStruct((SEQ, n_heads, 1, head_dim), F32), vec, vec),
            in_specs=[whole] * (6 + N_PART),
            out_specs=[whole] * 7,
            scratch_shapes=[dma((6 + 2 * N_PART,))],
            compiler_params=pltpu.CompilerParams(vmem_limit_bytes=1024 * 1024),
        )(*outs)
        full = query.shape
        return (o.reshape(full), dq.reshape(full), dk.reshape(full), dv.reshape(full),
                du.reshape(bias_u.shape), dw.reshape(bias_w.shape), dr.reshape(rel_k.shape))

    return jax.shard_map(local, mesh=mesh,
                         in_specs=(seq_spec, seq_spec, seq_spec, P(), P(), P(), seq_spec),
                         out_specs=(seq_spec, seq_spec, seq_spec, seq_spec, P(), P(), P()),
                         check_vma=False)
```

time: 235 us -> 225 us (0.957)
  Pallas kernels: 234 us -> 224 us
    pallas_call x1, Pallas kernels: 228 us -> 218 us  [local(): pl.pallas_call(kernel, name='rel_attn', out_shape=(act, act, act, act, *[...]
where the time goes in v5:
time: 225 us
  Pallas kernels  224 us (100%)
    pallas_call x1, Pallas kernels, local(): pl.pallas_call(kernel, name='rel_attn', out_shape=(act, act, act, act, *[...  218 us
    pallas_call x1, Pallas kernels, local(): pl.pallas_call(writer, name='writer', out_shape=(act, act, act, act, jax....  5.96 us

profile of v5, /device:TPU:0, one launch (start us, length us, event | category | flops | bytes accessed | tf_op | source)
XLA Modules:
  0.0 224.6 jit_solution(493320572042834968)
XLA Ops:
  0.6 218.0 %rel_attn.1 = (bf16[8,64,8,2,128]{4,3,2,1,0:T(2,128)(2,1)S(1)}, bf16[8,64,8,2,128]{4,3,2,1,0:T(2,128)(2,1)S(1)}, bf16[8,64,8,2,128]{4,3,2,1,0:T(2,128)(2,1)S(1)}...) custom-call(bf16[8,64,8,2,128]{4,3,2,1,0:T(2,128)(2,1)} %bitcast.15,, ...), custom_call_target="tpu_custom_call" | custom-call | tf_op jit(solution)/shard_map/rel_attn/pallas_call | solution.py:494
  218.6 6.0 %writer.1 = (bf16[8,64,8,2,128]{4,3,2,1,0:T(2,128)(2,1)}, bf16[8,64,8,2,128]{4,3,2,1,0:T(2,128)(2,1)}, bf16[8,64,8,2,128]{4,3,2,1,0:T(2,128)(2,1)}, bf16[8,64,8,...) custom-call(bf16[8,64,8,2,128]{4,3,2,1,0:T(2,128)(2,1)S(1)} %get-tuple-el, ...), custom_call_target="tpu_custom_call" | custom-call | tf_op jit(solution)/shard_map/writer/pallas_call | solution.py:520

commit v6 on v5

--- a/solution.py
+++ b/solution.py
@@ -15,7 +15,7 @@
 N_PAIR = 8
 SLOTS = 4
 SUBS = 2 * SLOTS
-EARLY = 2
+EARLY = 3
 ROWS = 64
 HALF = PLANE * ROWS
 SEQ = 2 * HALF
@@ -45,11 +45,11 @@
 
 def kernel(q_in, k_in, v_in, g_in, r_in, u_in, w_in,
            o_out, dq_out, dk_out, dv_out, dr0_out, dr1_out, dr2_out, dr3_out, du_out, dw_out,
-           buf, rbuf, r_buf, u_buf, w_buf, st_tx, st_rx, st_ref, dr_rx, dr_fin, dr_acc,
+           buf, rbuf, r_buf, u_buf, w_buf, st_tx, st_rx, st_ref, dr_rx, dr_rz, dr_fin, dr_acc,
            s_ref, e_ref, dp_ref, pb_ref, ds_ref, dd_ref,
            a_s, c_s, g_s, k_s, v_s, at_s, ct_s, gt_s, kt_s, vt_s, rev_s, rt_s, dkt, dvt, stage,
            in_send, in_recv, out_send, out_recv, own_sem, r_sem, up_send, up_recv, st_send, st_recv,
-           x_send, x_recv, ring_send, ring_recv, fw_send, fw_recv, b_send, b_recv):
+           x_send, x_recv, z_send, z_recv, ring_send, ring_recv, fw_send, fw_recv, b_send, b_recv):
     me = lax.axis_index("cp")
     core = me % 2
     chip = me // 2
@@ -264,9 +264,11 @@
         for j in range(2, 4):
             wait_for(buf.at[j, sub], in_recv.at[j, sub])
 
-    def lower_own(sub):
+    def lower_rows(sub):
         wait_in(sub)
         load_rows(buf, 2, buf, 3, sub, 0, True)
+
+    def lower_own(sub):
         load_keys(buf, 0, buf, 1, sub, 0)
 
         def own(hh, carry):
@@ -316,9 +318,18 @@
     parts = (dr0_out, dr1_out, dr2_out, dr3_out)
 
     def swap_start(p):
-        for n, (device, top, end) in enumerate(((partner, z, 1 - core), (across, 1 - z, core), (across + 1 - 2 * core, 1 - z, 1 - core))):
-            pltpu.make_async_remote_copy(src_ref=dr_acc.at[2 * p + top, end], dst_ref=dr_rx.at[p, n], send_sem=x_send.at[p], recv_sem=x_recv.at[p, n],
-                                         device_id=(device,), device_id_type=MESH).start()
+        for n in range(2):
+            pltpu.make_async_remote_copy(src_ref=dr_acc.at[2 * p + n, side], dst_ref=dr_rx.at[p, n], send_sem=x_send.at[p], recv_sem=x_recv.at[p, n],
+                                         device_id=(partner,), device_id_type=MESH).start()
+
+    def swap_add(p):
+        for n in range(2):
+            wait_for(dr_rx.at[p, n], x_recv.at[p, n])
+            dr_rx[p, n] = dr_rx[p, n] + dr_acc[2 * p + n, core]
+
+    def cross_start(p):
+        pltpu.make_async_remote_copy(src_ref=dr_rx.at[p, 1 - z], dst_ref=dr_rz.at[p], send_sem=z_send.at[p], recv_sem=z_recv.at[p],
+                                     device_id=(across,), device_id_type=MESH).start()
 
     def head_of(p, bits):
         other = chip ^ bits
@@ -353,10 +364,9 @@
             for bits in have[len(have) // 2:]:
                 forward(p, m, bits)
 
-    def swap_finish(p):
-        for n in range(3):
-            wait_for(dr_rx.at[p, n], x_recv.at[p, n])
-        total = dr_acc[2 * p + z, core] + dr_rx[p, 0] + dr_rx[p, 1] + dr_rx[p, 2]
+    def cross_finish(p):
+        wait_for(dr_rz.at[p], z_recv.at[p])
+        total = dr_rx[p, z] + dr_rz[p]
         rev32 = eye_rev(F32)
         for m in range(N_PART):
             part = total[:HEAD, HALF - HEAD * (m + 1):HALF - HEAD * m]
@@ -390,9 +400,19 @@
         def _():
             swap_start(0)
 
-        @pl.when(sub == SLOTS + 2)
-        def _():
-            swap_finish(0)
+        @pl.when(sub == SUBS - 1)
+        def _():
+            swap_add(0)
+            cross_start(0)
+
+        @pl.when(sub == SUBS)
+        def _():
+            swap_start(1)
+            cross_finish(0)
+
+        @pl.when((z == 0) & (sub < SUBS))
+        def _():
+            lower_rows(sub)
 
         @pl.when((z == 0) & (sub > 0))
         def _():
@@ -417,27 +437,24 @@
 
     lax.fori_loop(0, SUBS + 1, sub_body, 0)
 
-    swap_start(1)
-    send_out(EARLY, range(4))
-    hop_wait(0, 0)
-    hop_start(0, 1)
-    swap_finish(1)
-    send_out(EARLY + 1, range(4))
-    hop_wait(0, 1)
-    hop_start(0, 2)
-    hop_wait(1, 0)
-    hop_start(1, 1)
-    send_out(EARLY + 2, range(4))
-    hop_wait(1, 1)
-    hop_start(1, 2)
+    swap_add(1)
+    cross_start(1)
+    cross_finish(1)
+    for p in range(2):
+        hop_wait(p, 0)
+        hop_start(p, 1)
 
     def send_late(sub, carry):
         send_out(sub, range(4))
         return carry
 
-    lax.fori_loop(EARLY + 3, SUBS, send_late, 0)
-    hop_wait(0, 2)
-    hop_wait(1, 2)
+    lax.fori_loop(EARLY, EARLY + 2, send_late, 0)
+    for p in range(2):
+        hop_wait(p, 1)
+        hop_start(p, 2)
+    lax.fori_loop(EARLY + 2, SUBS, send_late, 0)
+    for p in range(2):
+        hop_wait(p, 2)
 
     for t, dst in enumerate(acts):
         wait_for(dst, out_recv.at[t])
@@ -456,6 +473,7 @@
 
     for p in range(2):
         wait_for(dr_rx.at[p], x_send.at[p])
+        wait_for(dr_rz.at[p], z_send.at[p])
         for m in range(N_PART):
             wait_for(dr_fin.at[p, :PART], own_sem.at[p, m])
             wait_for(parts[m].at[0, :, :N_PAIR - 1], ring_send.at[p, m])
@@ -503,7 +521,7 @@
                 vm((4, SUBS, HALF, PAIR, HEAD), BF16), vm((2, SUBS, HALF, PAIR, HEAD), BF16),
                 vm((SEQ, 2, PAIR, HEAD), BF16), vm((2, PAIR, HEAD), BF16), vm((2, PAIR, HEAD), BF16),
                 vm((SUBS, PAIR, 8, HALF), F32), vm((SUBS, PAIR, 8, HALF), F32), vm((QB, HEAD), F32),
-                vm((2, 3) + acc, F32), vm((2, HALF + 2, 1, HEAD), F32), vm((4, 2) + acc, F32),
+                vm((2, 2) + acc, F32), vm((2,) + acc, F32), vm((2, HALF + 2, 1, HEAD), F32), vm((4, 2) + acc, F32),
                 vm((QB, SEQ), F32), vm((QB, SEQ), F32), vm((QB, SEQ), F32),
                 vm((QB, SEQ), BF16), vm((QB, SEQ), BF16), vm((QB, SEQ), BF16),
                 vm(tok, BF16), vm(tok, BF16), vm(tok, BF16), vm(tok, BF16), vm(tok, BF16),
@@ -511,7 +529,7 @@
                 vm((4, SEQ, HEAD), BF16), vm((4, HEAD, SEQ), BF16),
                 vm((PAIR, HEAD, HALF), F32), vm((PAIR, HEAD, HALF), F32), vm((4, PAIR, HALF, HEAD), BF16),
                 dma, dma((4, SUBS)), dma, dma((4,)), dma((2, N_PART)), dma((3,)), dma((SUBS,)), dma((2, SUBS)), dma, dma((SUBS, PAIR)),
-                dma((2,)), dma((2, 3)), dma((2, N_PART)), dma((2, 3, N_PART)), dma((2, N_PART)), dma((2, N_PART)), dma((2,)), dma((2,)),
+                dma((2,)), dma((2, 2)), dma((2,)), dma((2,)), dma((2, N_PART)), dma((2, 3, N_PART)), dma((2, N_PART)), dma((2, N_PART)), dma((2,)), dma((2,)),
             ],
             compiler_params=pltpu.CompilerParams(collective_id=0, has_side_effects=True, vmem_limit_bytes=36 * 1024 * 1024),
         )(*[pltpu.with_memory_space_constraint(x, pltpu.HBM) for x in (

time: 225 us -> 212 us (0.942)
  Pallas kernels: 224 us -> 211 us
    pallas_call x1, Pallas kernels: 218 us -> 205 us  [local(): pl.pallas_call(kernel, name='rel_attn', out_shape=(act, act, act, act, *[...]
where the time goes in v6:
time: 212 us
  Pallas kernels  211 us (100%)
    pallas_call x1, Pallas kernels, local(): pl.pallas_call(kernel, name='rel_attn', out_shape=(act, act, act, act, *[...  205 us
    pallas_call x1, Pallas kernels, local(): pl.pallas_call(writer, name='writer', out_shape=(act, act, act, act, jax....  5.96 us

profile of v6, /device:TPU:0, one launch (start us, length us, event | category | flops | bytes accessed | tf_op | source)
XLA Modules:
  0.0 211.8 jit_solution(2652347102349720311)
XLA Ops:
  0.6 205.2 %rel_attn.1 = (bf16[8,64,8,2,128]{4,3,2,1,0:T(2,128)(2,1)S(1)}, bf16[8,64,8,2,128]{4,3,2,1,0:T(2,128)(2,1)S(1)}, bf16[8,64,8,2,128]{4,3,2,1,0:T(2,128)(2,1)S(1)}...) custom-call(bf16[8,64,8,2,128]{4,3,2,1,0:T(2,128)(2,1)} %bitcast.15,, ...), custom_call_target="tpu_custom_call" | custom-call | tf_op jit(solution)/shard_map/rel_attn/pallas_call | solution.py:512
  205.8 6.0 %writer.1 = (bf16[8,64,8,2,128]{4,3,2,1,0:T(2,128)(2,1)}, bf16[8,64,8,2,128]{4,3,2,1,0:T(2,128)(2,1)}, bf16[8,64,8,2,128]{4,3,2,1,0:T(2,128)(2,1)}, bf16[8,64,8,...) custom-call(bf16[8,64,8,2,128]{4,3,2,1,0:T(2,128)(2,1)S(1)} %get-tuple-el, ...), custom_call_target="tpu_custom_call" | custom-call | tf_op jit(solution)/shard_map/writer/pallas_call | solution.py:538

commit v7 on v6

--- a/solution.py
+++ b/solution.py
@@ -22,9 +22,10 @@
 HEAD = 128
 QB = 256
 WIN = HALF + QB
-N_PART = 4
-PART = HALF // N_PART
-HOPS = ((1, 2, 4), (2, 1, 4), (1, 2, 4), (2, 1, 4))
+N_PART = 6
+PART = 86
+FIN = N_PART * PART
+HOPS = ((1, 2, 4), (2, 1, 4)) * 3
 TURNS = ((1, 3, 2), (3, 1, 2))
 
 
@@ -44,12 +45,12 @@
 
 
 def kernel(q_in, k_in, v_in, g_in, r_in, u_in, w_in,
-           o_out, dq_out, dk_out, dv_out, dr0_out, dr1_out, dr2_out, dr3_out, du_out, dw_out,
+           o_out, dq_out, dk_out, dv_out, dr0_out, dr1_out, dr2_out, dr3_out, dr4_out, dr5_out,
            buf, rbuf, r_buf, u_buf, w_buf, st_tx, st_rx, st_ref, dr_rx, dr_rz, dr_fin, dr_acc,
            s_ref, e_ref, dp_ref, pb_ref, ds_ref, dd_ref,
            a_s, c_s, g_s, k_s, v_s, at_s, ct_s, gt_s, kt_s, vt_s, rev_s, rt_s, dkt, dvt, stage,
            in_send, in_recv, out_send, out_recv, own_sem, r_sem, up_send, up_recv, st_send, st_recv,
-           x_send, x_recv, z_send, z_recv, ring_send, ring_recv, fw_send, fw_recv, b_send, b_recv):
+           x_send, x_recv, z_send, z_recv, ring_send, ring_recv, fw_send, fw_recv):
     me = lax.axis_index("cp")
     core = me % 2
     chip = me // 2
@@ -69,12 +70,9 @@
 
     barrier = pltpu.get_barrier_semaphore()
 
-    def say(step, carry):
-        pl.semaphore_signal(barrier, inc=1, device_id=((me + step) % N_DEV,), device_id_type=MESH)
-        return carry
-
-    lax.fori_loop(1, N_DEV, say, 0)
-    pl.semaphore_wait(barrier, N_DEV - 1)
+    for peer in [across] + [me ^ step for step in range(PLANE - 1, 0, -1)]:
+        pl.semaphore_signal(barrier, inc=1, device_id=(peer,), device_id_type=MESH)
+    pl.semaphore_wait(barrier, PLANE)
 
     my_rows = pl.ds(pl.multiple_of((me % PLANE) * ROWS, ROWS), ROWS)
 
@@ -89,12 +87,12 @@
         pair, row = sub // SLOTS, sub % SLOTS
         for first in (0, 2):
             for t in (first, first + 1):
-                pltpu.make_async_copy(ins[t].at[core * SLOTS + row, :, 2 * col + pair], buf.at[t, sub, my_rows], in_recv.at[t, sub]).start()
+                pltpu.make_async_copy(ins[t].at[core * SLOTS + row, :, 2 * col + pair], buf.at[t, sub, my_rows], in_recv.at[first // 2, sub]).start()
             for peer in peers():
                 for t in (first, first + 1):
                     pltpu.make_async_remote_copy(
                         src_ref=ins[t].at[(peer % 2) * SLOTS + row, :, 2 * ((peer // 2) % 4) + pair], dst_ref=buf.at[t, sub, my_rows],
-                        send_sem=in_send, recv_sem=in_recv.at[t, sub], device_id=(peer,), device_id_type=MESH).start()
+                        send_sem=in_send, recv_sem=in_recv.at[first // 2, sub], device_id=(peer,), device_id_type=MESH).start()
 
     def send_all(ins):
         def send_sub(sub, carry):
@@ -128,18 +126,18 @@
     def send_out(sub, which):
         place = (core * SLOTS + sub % SLOTS, slice(None), 2 * col + sub // SLOTS)
         for t in which:
-            pltpu.make_async_copy(buf.at[t, sub, my_rows], acts[t].at[place], out_recv.at[t]).start()
+            pltpu.make_async_copy(buf.at[t, sub, my_rows], acts[t].at[place], out_recv).start()
         for peer in peers():
             peer_rows = pl.ds(pl.multiple_of((peer % PLANE) * ROWS, ROWS), ROWS)
             for t in which:
                 pltpu.make_async_remote_copy(
                     src_ref=buf.at[t, sub, peer_rows], dst_ref=acts[t].at[place],
-                    send_sem=out_send, recv_sem=out_recv.at[t], device_id=(peer,), device_id_type=MESH).start()
+                    send_sem=out_send, recv_sem=out_recv, device_id=(peer,), device_id_type=MESH).start()
 
     def send_up(sub):
+        wait_for(buf.at[0:2, sub], in_recv.at[0, sub])
         for j in range(2):
-            wait_for(buf.at[j, sub], in_recv.at[j, sub])
-            pltpu.make_async_remote_copy(src_ref=buf.at[j, sub], dst_ref=rbuf.at[j, sub], send_sem=up_send.at[sub], recv_sem=up_recv.at[j, sub],
+            pltpu.make_async_remote_copy(src_ref=buf.at[j, sub], dst_ref=rbuf.at[j, sub], send_sem=up_send.at[sub % 4], recv_sem=up_recv.at[sub],
                                          device_id=(across,), device_id_type=MESH).start()
 
     def unpack(ref, j, sub):
@@ -256,13 +254,11 @@
             buf[t, sub] = pltpu.einshape("abc->bac", stage[2 + t])
 
     def wait_up(sub):
-        for j in range(2):
-            wait_for(rbuf.at[j, sub], up_recv.at[j, sub])
-        wait_for(rbuf.at[:, sub], up_send.at[sub])
+        wait_for(rbuf.at[:, sub], up_recv.at[sub])
+        wait_for(rbuf.at[:, sub], up_send.at[sub % 4])
 
     def wait_in(sub):
-        for j in range(2, 4):
-            wait_for(buf.at[j, sub], in_recv.at[j, sub])
+        wait_for(buf.at[2:4, sub], in_recv.at[1, sub])
 
     def lower_rows(sub):
         wait_in(sub)
@@ -283,10 +279,10 @@
     def lower_theirs(sub):
         wait_up(sub)
         load_rows(rbuf, 0, rbuf, 1, sub, HALF, False)
+        wait_for(st_rx.at[sub], st_recv.at[sub])
 
         def theirs(hh, carry):
             head = 2 * (sub // SLOTS) + hh
-            wait_for(st_rx.at[sub, hh], st_recv.at[sub, hh])
             col_block(hh, head, sub, HALF)
             col_block(hh, head, sub, HALF + QB)
             return carry
@@ -306,7 +302,7 @@
             for blk in (1, 0):
                 row_block(hh, head, QB * blk, HALF + QB * blk, HALF, blk == 1, True)
                 st_tx[sub, hh, :, QB * blk:QB * (blk + 1)] = st_ref[...].T[:8]
-            pltpu.make_async_remote_copy(src_ref=st_tx.at[sub, hh], dst_ref=st_rx.at[sub, hh], send_sem=st_send, recv_sem=st_recv.at[sub, hh],
+            pltpu.make_async_remote_copy(src_ref=st_tx.at[sub, hh], dst_ref=st_rx.at[sub, hh], send_sem=st_send, recv_sem=st_recv.at[sub],
                                          device_id=(across,), device_id_type=MESH).start()
             return carry
 
@@ -315,16 +311,16 @@
         store_keys(sub)
 
     side = 1 - core
-    parts = (dr0_out, dr1_out, dr2_out, dr3_out)
+    parts = (dr0_out, dr1_out, dr2_out, dr3_out, dr4_out, dr5_out)
 
     def swap_start(p):
         for n in range(2):
-            pltpu.make_async_remote_copy(src_ref=dr_acc.at[2 * p + n, side], dst_ref=dr_rx.at[p, n], send_sem=x_send.at[p], recv_sem=x_recv.at[p, n],
+            pltpu.make_async_remote_copy(src_ref=dr_acc.at[2 * p + n, side], dst_ref=dr_rx.at[p, n], send_sem=x_send.at[p], recv_sem=x_recv.at[p],
                                          device_id=(partner,), device_id_type=MESH).start()
 
     def swap_add(p):
+        wait_for(dr_rx.at[p], x_recv.at[p])
         for n in range(2):
-            wait_for(dr_rx.at[p, n], x_recv.at[p, n])
             dr_rx[p, n] = dr_rx[p, n] + dr_acc[2 * p + n, core]
 
     def cross_start(p):
@@ -341,8 +337,8 @@
         return parts[m].at[side, :, head_of(p, bits)]
 
     def forward(p, m, bits):
-        pltpu.make_async_remote_copy(src_ref=block(p, m, bits), dst_ref=parts[m].at[side, :, head_of(p, bits)], send_sem=fw_send.at[p, m],
-                                     recv_sem=fw_recv.at[p, m], device_id=(partner,), device_id_type=MESH).start()
+        pltpu.make_async_remote_copy(src_ref=block(p, m, bits), dst_ref=parts[m].at[side, :, head_of(p, bits)], send_sem=fw_send.at[p, m // 3],
+                                     recv_sem=fw_recv.at[p, m // 3], device_id=(partner,), device_id_type=MESH).start()
 
     def held(m, hop):
         have = [0]
@@ -350,17 +346,20 @@
             have = have + [bits ^ bit for bits in have]
         return have
 
+    def blocks(count):
+        return parts[0].at[:, :, :count // 2]
+
     def hop_start(p, hop):
         for m in range(N_PART):
             for bits in held(m, hop):
                 pltpu.make_async_remote_copy(
-                    src_ref=block(p, m, bits), dst_ref=parts[m].at[side, :, head_of(p, bits)], send_sem=ring_send.at[p, m],
-                    recv_sem=ring_recv.at[p, hop, m], device_id=(me ^ (2 * HOPS[m][hop]),), device_id_type=MESH).start()
+                    src_ref=block(p, m, bits), dst_ref=parts[m].at[side, :, head_of(p, bits)], send_sem=ring_send.at[p, hop],
+                    recv_sem=ring_recv.at[p, hop], device_id=(me ^ (2 * HOPS[m][hop]),), device_id_type=MESH).start()
 
     def hop_wait(p, hop):
+        wait_for(blocks(N_PART << hop), ring_recv.at[p, hop])
         for m in range(N_PART):
             have = held(m, hop + 1)
-            wait_for(parts[m].at[0, :, :len(have) // 2], ring_recv.at[p, hop, m])
             for bits in have[len(have) // 2:]:
                 forward(p, m, bits)
 
@@ -368,26 +367,17 @@
         wait_for(dr_rz.at[p], z_recv.at[p])
         total = dr_rx[p, z] + dr_rz[p]
         rev32 = eye_rev(F32)
-        for m in range(N_PART):
+        for m in range(HALF // HEAD):
             part = total[:HEAD, HALF - HEAD * (m + 1):HALF - HEAD * m]
             turned = lax.dot_general(rev32, part, (((1,), (1,)), ((), ())), precision=lax.Precision.HIGHEST, preferred_element_type=F32)
             dr_fin[p, HEAD * m:HEAD * (m + 1)] = turned.reshape(HEAD, 1, HEAD)
         dr_fin[p, HALF] = total[HEAD:HEAD + 1, HALF - HEAD:]
         dr_fin[p, HALF + 1] = total[HEAD + 1:HEAD + 2, HALF - HEAD:]
+        dr_fin[p, HALF + 2:] = jnp.zeros((FIN - HALF - 2, 1, HEAD), F32)
         hop_start(p, 0)
-        head = head_of(p, 0)
         for m in range(N_PART):
-            pltpu.make_async_copy(block(p, m, 0), parts[m].at[side, :, head], own_sem.at[p, m]).start()
+            pltpu.make_async_copy(block(p, m, 0), parts[m].at[side, :, head_of(p, 0)], own_sem.at[p]).start()
             forward(p, m, 0)
-
-        @pl.when(core == 1)
-        def _():
-            for j, dst in enumerate((du_out, dw_out)):
-                pltpu.make_async_copy(dr_fin.at[p, HALF + j], dst.at[head], b_recv.at[j]).start()
-                for step in range(1, N_DEV):
-                    pltpu.make_async_remote_copy(
-                        src_ref=dr_fin.at[p, HALF + j], dst_ref=dst.at[head], send_sem=b_send.at[j], recv_sem=b_recv.at[j],
-                        device_id=(me ^ step,), device_id_type=MESH).start()
 
     send_up(0)
 
@@ -456,14 +446,7 @@
     for p in range(2):
         hop_wait(p, 2)
 
-    for t, dst in enumerate(acts):
-        wait_for(dst, out_recv.at[t])
-    for j, dst in enumerate((du_out, dw_out)):
-        wait_for(dst, b_recv.at[j])
-
-        @pl.when(core == 1)
-        def _():
-            wait_for(dr_fin.at[0, :2 * (N_DEV - 1)], b_send.at[j])
+    wait_for(buf, out_recv)
     wait_for(buf.at[:, :, :HALF - ROWS], in_send)
     wait_for(buf.at[:, :, :HALF - ROWS], out_send)
 
@@ -474,20 +457,24 @@
     for p in range(2):
         wait_for(dr_rx.at[p], x_send.at[p])
         wait_for(dr_rz.at[p], z_send.at[p])
-        for m in range(N_PART):
-            wait_for(dr_fin.at[p, :PART], own_sem.at[p, m])
-            wait_for(parts[m].at[0, :, :N_PAIR - 1], ring_send.at[p, m])
-            wait_for(parts[m].at[0, :, :N_PAIR], fw_send.at[p, m])
-            wait_for(parts[m].at[0, :, :N_PAIR], fw_recv.at[p, m])
+        wait_for(blocks(N_PART), own_sem.at[p])
+        for hop in range(3):
+            wait_for(blocks(N_PART << hop), ring_send.at[p, hop])
+        for n in range(2):
+            wait_for(blocks(N_PART // 2 * N_PAIR), fw_send.at[p, n])
+            wait_for(blocks(N_PART // 2 * N_PAIR), fw_recv.at[p, n])
 
 
 def writer(*refs):
-    ins, (o, dq, dk, dv, dr, du, dw, sem) = refs[:6 + N_PART], refs[6 + N_PART:]
-    pairs = list(zip(ins[:4] + ins[-2:], (o, dq, dk, dv, du, dw)))
-    for m, part in enumerate(ins[4:-2]):
+    ins, (o, dq, dk, dv, dr, du, dw, sem) = refs[:4 + N_PART], refs[4 + N_PART:]
+    pairs = list(zip(ins[:4], (o, dq, dk, dv)))
+    for m, part in enumerate(ins[4:]):
+        rows = min(PART, HALF - PART * m)
         for side in range(2):
             start = HALF * side + PART * m
-            pairs.append((part.at[side], dr.at[start:start + PART]))
+            pairs.append((part.at[side, :rows], dr.at[start:start + rows]))
+    last = HALF - PART * (N_PART - 1)
+    pairs += [(ins[-1].at[0, last], du), (ins[-1].at[0, last + 1], dw)]
     copies = [pltpu.make_async_copy(src, dst, sem.at[j]) for j, (src, dst) in enumerate(pairs)]
     for copy in copies:
         copy.start()
@@ -513,23 +500,22 @@
             kernel,
             name="rel_attn",
             out_shape=(act, act, act, act,
-                       *[jax.ShapeDtypeStruct((2, PART, n_heads, 1, head_dim), F32)] * N_PART,
-                       vec, vec),
+                       *[jax.ShapeDtypeStruct((2, PART, n_heads, 1, head_dim), F32)] * N_PART),
             in_specs=[pl.BlockSpec(memory_space=pltpu.HBM)] * 7,
-            out_specs=[whole] * (6 + N_PART),
+            out_specs=[whole] * (4 + N_PART),
             scratch_shapes=[
                 vm((4, SUBS, HALF, PAIR, HEAD), BF16), vm((2, SUBS, HALF, PAIR, HEAD), BF16),
                 vm((SEQ, 2, PAIR, HEAD), BF16), vm((2, PAIR, HEAD), BF16), vm((2, PAIR, HEAD), BF16),
                 vm((SUBS, PAIR, 8, HALF), F32), vm((SUBS, PAIR, 8, HALF), F32), vm((QB, HEAD), F32),
-                vm((2, 2) + acc, F32), vm((2,) + acc, F32), vm((2, HALF + 2, 1, HEAD), F32), vm((4, 2) + acc, F32),
+                vm((2, 2) + acc, F32), vm((2,) + acc, F32), vm((2, FIN, 1, HEAD), F32), vm((4, 2) + acc, F32),
                 vm((QB, SEQ), F32), vm((QB, SEQ), F32), vm((QB, SEQ), F32),
                 vm((QB, SEQ), BF16), vm((QB, SEQ), BF16), vm((QB, SEQ), BF16),
                 vm(tok, BF16), vm(tok, BF16), vm(tok, BF16), vm(tok, BF16), vm(tok, BF16),
                 vm(tok_t, BF16), vm(tok_t, BF16), vm(tok_t, BF16), vm(tok_t, BF16), vm(tok_t, BF16),
                 vm((4, SEQ, HEAD), BF16), vm((4, HEAD, SEQ), BF16),
                 vm((PAIR, HEAD, HALF), F32), vm((PAIR, HEAD, HALF), F32), vm((4, PAIR, HALF, HEAD), BF16),
-                dma, dma((4, SUBS)), dma, dma((4,)), dma((2, N_PART)), dma((3,)), dma((SUBS,)), dma((2, SUBS)), dma, dma((SUBS, PAIR)),
-                dma((2,)), dma((2, 2)), dma((2,)), dma((2,)), dma((2, N_PART)), dma((2, 3, N_PART)), dma((2, N_PART)), dma((2, N_PART)), dma((2,)), dma((2,)),
+                dma, dma((2, SUBS)), dma, dma, dma((2,)), dma((3,)), dma((4,)), dma((SUBS,)), dma, dma((SUBS,)),
+                dma((2,)), dma((2,)), dma((2,)), dma((2,)), dma((2, 3)), dma((2, 3)), dma((2, 2)), dma((2, 2)),
             ],
             compiler_params=pltpu.CompilerParams(collective_id=0, has_side_effects=True, vmem_limit_bytes=36 * 1024 * 1024),
         )(*[pltpu.with_memory_space_constraint(x, pltpu.HBM) for x in (
@@ -539,7 +525,7 @@
             writer,
             name="writer",
             out_shape=(act, act, act, act, jax.ShapeDtypeStruct((SEQ, n_heads, 1, head_dim), F32), vec, vec),
-            in_specs=[whole] * (6 + N_PART),
+            in_specs=[whole] * (4 + N_PART),
             out_specs=[whole] * 7,
             scratch_shapes=[dma((6 + 2 * N_PART,))],
             compiler_params=pltpu.CompilerParams(vmem_limit_bytes=1024 * 1024),

time: 212 us -> 210 us (level)
    pallas_call x1, Pallas kernels: 205 us -> 203 us  [local(): pl.pallas_call(kernel, name='rel_attn', out_shape=(act, act, act, act, *[...]
where the time goes in v7:
time: 210 us; the launch traced here: 209 us
  Pallas kernels  209 us (100%)
    pallas_call x1, Pallas kernels, local(): pl.pallas_call(kernel, name='rel_attn', out_shape=(act, act, act, act, *[...  203 us
    pallas_call x1, Pallas kernels, local(): pl.pallas_call(writer, name='writer', out_shape=(act, act, act, act, jax....  5.97 us

profile of v7, /device:TPU:0, one launch (start us, length us, event | category | flops | bytes accessed | tf_op | source)
XLA Modules:
  0.0 209.2 jit_solution(3749916745220696601)
XLA Ops:
  0.6 202.6 %rel_attn.1 = (bf16[8,64,8,2,128]{4,3,2,1,0:T(2,128)(2,1)S(1)}, bf16[8,64,8,2,128]{4,3,2,1,0:T(2,128)(2,1)S(1)}, bf16[8,64,8,2,128]{4,3,2,1,0:T(2,128)(2,1)S(1)}...) custom-call(bf16[8,64,8,2,128]{4,3,2,1,0:T(2,128)(2,1)} %bitcast.15,, ...), custom_call_target="tpu_custom_call" | custom-call | tf_op jit(solution)/shard_map/rel_attn/pallas_call | solution.py:499
  203.2 6.0 %writer.1 = (bf16[8,64,8,2,128]{4,3,2,1,0:T(2,128)(2,1)}, bf16[8,64,8,2,128]{4,3,2,1,0:T(2,128)(2,1)}, bf16[8,64,8,2,128]{4,3,2,1,0:T(2,128)(2,1)}, bf16[8,64,8,...) custom-call(bf16[8,64,8,2,128]{4,3,2,1,0:T(2,128)(2,1)S(1)} %get-tuple-el, ...), custom_call_target="tpu_custom_call" | custom-call | tf_op jit(solution)/shard_map/writer/pallas_call | solution.py:524

commit v8 on v7

--- a/solution.py
+++ b/solution.py
@@ -476,8 +476,8 @@
     last = HALF - PART * (N_PART - 1)
     pairs += [(ins[-1].at[0, last], du), (ins[-1].at[0, last + 1], dw)]
     copies = [pltpu.make_async_copy(src, dst, sem.at[j]) for j, (src, dst) in enumerate(pairs)]
-    for copy in copies:
-        copy.start()
+    for j, copy in enumerate(copies):
+        copy.start(priority=j % 2)
     for copy in copies:
         copy.wait()
 

time: 210 us -> 210 us (level)
  no operation moved by 1% of the time
where the time goes in v8:
time: 210 us; the launch traced here: 209 us
  Pallas kernels  209 us (100%)
    pallas_call x1, Pallas kernels, local(): pl.pallas_call(kernel, name='rel_attn', out_shape=(act, act, act, act, *[...  203 us
    pallas_call x1, Pallas kernels, local(): pl.pallas_call(writer, name='writer', out_shape=(act, act, act, act, jax....  5.97 us

profile of v8, /device:TPU:0, one launch (start us, length us, event | category | flops | bytes accessed | tf_op | source)
XLA Modules:
  0.0 209.2 jit_solution(3176064221154293337)
XLA Ops:
  0.6 202.6 %rel_attn.1 = (bf16[8,64,8,2,128]{4,3,2,1,0:T(2,128)(2,1)S(1)}, bf16[8,64,8,2,128]{4,3,2,1,0:T(2,128)(2,1)S(1)}, bf16[8,64,8,2,128]{4,3,2,1,0:T(2,128)(2,1)S(1)}...) custom-call(bf16[8,64,8,2,128]{4,3,2,1,0:T(2,128)(2,1)} %bitcast.15,, ...), custom_call_target="tpu_custom_call" | custom-call | tf_op jit(solution)/shard_map/rel_attn/pallas_call | solution.py:499
  203.2 6.0 %writer.1 = (bf16[8,64,8,2,128]{4,3,2,1,0:T(2,128)(2,1)}, bf16[8,64,8,2,128]{4,3,2,1,0:T(2,128)(2,1)}, bf16[8,64,8,2,128]{4,3,2,1,0:T(2,128)(2,1)}, bf16[8,64,8,...) custom-call(bf16[8,64,8,2,128]{4,3,2,1,0:T(2,128)(2,1)S(1)} %get-tuple-el, ...), custom_call_target="tpu_custom_call" | custom-call | tf_op jit(solution)/shard_map/writer/pallas_call | solution.py:524

commit v9 on v7

--- a/solution.py
+++ b/solution.py
@@ -46,11 +46,11 @@
 
 def kernel(q_in, k_in, v_in, g_in, r_in, u_in, w_in,
            o_out, dq_out, dk_out, dv_out, dr0_out, dr1_out, dr2_out, dr3_out, dr4_out, dr5_out,
-           buf, rbuf, r_buf, u_buf, w_buf, st_tx, st_rx, st_ref, dr_rx, dr_rz, dr_fin, dr_acc,
+           buf, rbuf, head_start, r_buf, u_buf, w_buf, st_tx, st_rx, st_ref, dr_rx, dr_rz, dr_fin, dr_acc,
            s_ref, e_ref, dp_ref, pb_ref, ds_ref, dd_ref,
            a_s, c_s, g_s, k_s, v_s, at_s, ct_s, gt_s, kt_s, vt_s, rev_s, rt_s, dkt, dvt, stage,
            in_send, in_recv, out_send, out_recv, own_sem, r_sem, up_send, up_recv, st_send, st_recv,
-           x_send, x_recv, z_send, z_recv, ring_send, ring_recv, fw_send, fw_recv):
+           x_send, x_recv, z_send, z_recv, first_sem, ring_send, ring_recv, fw_send, fw_recv):
     me = lax.axis_index("cp")
     core = me % 2
     chip = me // 2
@@ -68,11 +68,26 @@
     for copy in tables:
         copy.start()
 
+    def bring(ins):
+        for t in range(2):
+            for step in range(1, PLANE):
+                peer = me ^ step
+                pltpu.make_async_copy(ins[t].at[(peer % 2) * SLOTS, :, 2 * ((peer // 2) % 4)], head_start.at[t, step - 1], first_sem).start()
+
+    @pl.when(z == 0)
+    def _():
+        bring((k_in, v_in))
+
+    @pl.when(z == 1)
+    def _():
+        bring((q_in, g_in))
+
     barrier = pltpu.get_barrier_semaphore()
 
     for peer in [across] + [me ^ step for step in range(PLANE - 1, 0, -1)]:
         pl.semaphore_signal(barrier, inc=1, device_id=(peer,), device_id_type=MESH)
     pl.semaphore_wait(barrier, PLANE)
+    wait_for(head_start, first_sem)
 
     my_rows = pl.ds(pl.multiple_of((me % PLANE) * ROWS, ROWS), ROWS)
 
@@ -83,22 +98,27 @@
             yield me ^ (2 * turn + 1)
         yield partner
 
-    def send_in(ins, sub):
+    def send_in(ins, sub, first_ones=False):
         pair, row = sub // SLOTS, sub % SLOTS
         for first in (0, 2):
+            for peer in peers():
+                for t in (first, first + 1):
+                    if first_ones and first == 0:
+                        src = head_start.at[t, (peer ^ me) - 1]
+                    else:
+                        src = ins[t].at[(peer % 2) * SLOTS + row, :, 2 * ((peer // 2) % 4) + pair]
+                    pltpu.make_async_remote_copy(
+                        src_ref=src, dst_ref=buf.at[t, sub, my_rows],
+                        send_sem=in_send, recv_sem=in_recv.at[first // 2, sub], device_id=(peer,), device_id_type=MESH).start()
             for t in (first, first + 1):
                 pltpu.make_async_copy(ins[t].at[core * SLOTS + row, :, 2 * col + pair], buf.at[t, sub, my_rows], in_recv.at[first // 2, sub]).start()
-            for peer in peers():
-                for t in (first, first + 1):
-                    pltpu.make_async_remote_copy(
-                        src_ref=ins[t].at[(peer % 2) * SLOTS + row, :, 2 * ((peer // 2) % 4) + pair], dst_ref=buf.at[t, sub, my_rows],
-                        send_sem=in_send, recv_sem=in_recv.at[first // 2, sub], device_id=(peer,), device_id_type=MESH).start()
 
     def send_all(ins):
         def send_sub(sub, carry):
             send_in(ins, sub)
             return carry
-        lax.fori_loop(0, SUBS, send_sub, 0)
+        send_in(ins, 0, True)
+        lax.fori_loop(1, SUBS, send_sub, 0)
 
     @pl.when(z == 0)
     def _():
@@ -504,7 +524,7 @@
             in_specs=[pl.BlockSpec(memory_space=pltpu.HBM)] * 7,
             out_specs=[whole] * (4 + N_PART),
             scratch_shapes=[
-                vm((4, SUBS, HALF, PAIR, HEAD), BF16), vm((2, SUBS, HALF, PAIR, HEAD), BF16),
+                vm((4, SUBS, HALF, PAIR, HEAD), BF16), vm((2, SUBS, HALF, PAIR, HEAD), BF16), vm((2, PLANE - 1, ROWS, PAIR, HEAD), BF16),
                 vm((SEQ, 2, PAIR, HEAD), BF16), vm((2, PAIR, HEAD), BF16), vm((2, PAIR, HEAD), BF16),
                 vm((SUBS, PAIR, 8, HALF), F32), vm((SUBS, PAIR, 8, HALF), F32), vm((QB, HEAD), F32),
                 vm((2, 2) + acc, F32), vm((2,) + acc, F32), vm((2, FIN, 1, HEAD), F32), vm((4, 2) + acc, F32),
@@ -515,9 +535,9 @@
                 vm((4, SEQ, HEAD), BF16), vm((4, HEAD, SEQ), BF16),
                 vm((PAIR, HEAD, HALF), F32), vm((PAIR, HEAD, HALF), F32), vm((4, PAIR, HALF, HEAD), BF16),
                 dma, dma((2, SUBS)), dma, dma, dma((2,)), dma((3,)), dma((4,)), dma((SUBS,)), dma, dma((SUBS,)),
-                dma((2,)), dma((2,)), dma((2,)), dma((2,)), dma((2, 3)), dma((2, 3)), dma((2, 2)), dma((2, 2)),
+                dma((2,)), dma((2,)), dma((2,)), dma((2,)), dma, dma((2, 3)), dma((2, 3)), dma((2, 2)), dma((2, 2)),
             ],
-            compiler_params=pltpu.CompilerParams(collective_id=0, has_side_effects=True, vmem_limit_bytes=36 * 1024 * 1024),
+            compiler_params=pltpu.CompilerParams(collective_id=0, has_side_effects=True, vmem_limit_bytes=37 * 1024 * 1024),
         )(*[pltpu.with_memory_space_constraint(x, pltpu.HBM) for x in (
             query.reshape(pairs), key_in.reshape(pairs), value.reshape(pairs), d_out.reshape(pairs),
             rel_k.reshape(SEQ, N_PAIR, PAIR, head_dim), bias_u.reshape(N_PAIR, PAIR, head_dim), bias_w.reshape(N_PAIR, PAIR, head_dim))])

time: 210 us -> 210 us (level)
  no operation moved by 1% of the time
where the time goes in v9:
time: 210 us; the launch traced here: 209 us
  Pallas kernels  209 us (100%)
    pallas_call x1, Pallas kernels, local(): pl.pallas_call(kernel, name='rel_attn', out_shape=(act, act, act, act, *[...  203 us
    pallas_call x1, Pallas kernels, local(): pl.pallas_call(writer, name='writer', out_shape=(act, act, act, act, jax....  5.97 us

profile of v9, /device:TPU:0, one launch (start us, length us, event | category | flops | bytes accessed | tf_op | source)
XLA Modules:
  0.0 209.5 jit_solution(7077972176945796808)
XLA Ops:
  0.6 202.7 %rel_attn.1 = (bf16[8,64,8,2,128]{4,3,2,1,0:T(2,128)(2,1)S(1)}, bf16[8,64,8,2,128]{4,3,2,1,0:T(2,128)(2,1)S(1)}, bf16[8,64,8,2,128]{4,3,2,1,0:T(2,128)(2,1)S(1)}...) custom-call(bf16[8,64,8,2,128]{4,3,2,1,0:T(2,128)(2,1)} %bitcast.15,, ...), custom_call_target="tpu_custom_call" | custom-call | tf_op jit(solution)/shard_map/rel_attn/pallas_call | solution.py:519
  203.3 6.0 %writer.1 = (bf16[8,64,8,2,128]{4,3,2,1,0:T(2,128)(2,1)}, bf16[8,64,8,2,128]{4,3,2,1,0:T(2,128)(2,1)}, bf16[8,64,8,2,128]{4,3,2,1,0:T(2,128)(2,1)}, bf16[8,64,8,...) custom-call(bf16[8,64,8,2,128]{4,3,2,1,0:T(2,128)(2,1)S(1)} %get-tuple-el, ...), custom_call_target="tpu_custom_call" | custom-call | tf_op jit(solution)/shard_map/writer/pallas_call | solution.py:544

commit v10 on v7

--- a/solution.py
+++ b/solution.py
@@ -15,7 +15,7 @@
 N_PAIR = 8
 SLOTS = 4
 SUBS = 2 * SLOTS
-EARLY = 3
+EARLY = 4
 ROWS = 64
 HALF = PLANE * ROWS
 SEQ = 2 * HALF

time: 210 us -> 210 us (level)
  no operation moved by 1% of the time
where the time goes in v10:
time: 210 us; the launch traced here: 209 us
  Pallas kernels  209 us (100%)
    pallas_call x1, Pallas kernels, local(): pl.pallas_call(kernel, name='rel_attn', out_shape=(act, act, act, act, *[...  203 us
    pallas_call x1, Pallas kernels, local(): pl.pallas_call(writer, name='writer', out_shape=(act, act, act, act, jax....  5.97 us

profile of v10, /device:TPU:0, one launch (start us, length us, event | category | flops | bytes accessed | tf_op | source)
XLA Modules:
  0.0 209.2 jit_solution(3041558488957845167)
XLA Ops:
  0.6 202.6 %rel_attn.1 = (bf16[8,64,8,2,128]{4,3,2,1,0:T(2,128)(2,1)S(1)}, bf16[8,64,8,2,128]{4,3,2,1,0:T(2,128)(2,1)S(1)}, bf16[8,64,8,2,128]{4,3,2,1,0:T(2,128)(2,1)S(1)}...) custom-call(bf16[8,64,8,2,128]{4,3,2,1,0:T(2,128)(2,1)} %bitcast.15,, ...), custom_call_target="tpu_custom_call" | custom-call | tf_op jit(solution)/shard_map/rel_attn/pallas_call | solution.py:499
  203.2 6.0 %writer.1 = (bf16[8,64,8,2,128]{4,3,2,1,0:T(2,128)(2,1)}, bf16[8,64,8,2,128]{4,3,2,1,0:T(2,128)(2,1)}, bf16[8,64,8,2,128]{4,3,2,1,0:T(2,128)(2,1)}, bf16[8,64,8,...) custom-call(bf16[8,64,8,2,128]{4,3,2,1,0:T(2,128)(2,1)S(1)} %get-tuple-el, ...), custom_call_target="tpu_custom_call" | custom-call | tf_op jit(solution)/shard_map/writer/pallas_call | solution.py:524

commit v11 on v10

--- a/solution.py
+++ b/solution.py
@@ -25,7 +25,7 @@
 N_PART = 6
 PART = 86
 FIN = N_PART * PART
-HOPS = ((1, 2, 4), (2, 1, 4)) * 3
+HOPS = ((2, 1, 4), (2, 1, 4), (1, 2, 4)) * 2
 TURNS = ((1, 3, 2), (3, 1, 2))
 
 

time: 210 us -> 213 us (1.014)
    pallas_call x1, Pallas kernels: 203 us -> 205 us  [local(): pl.pallas_call(kernel, name='rel_attn', out_shape=(act, act, act, act, *[...]
where the time goes in v11:
time: 213 us; the launch traced here: 212 us
  Pallas kernels  211 us (99%)
    pallas_call x1, Pallas kernels, local(): pl.pallas_call(kernel, name='rel_attn', out_shape=(act, act, act, act, *[...  205 us
    pallas_call x1, Pallas kernels, local(): pl.pallas_call(writer, name='writer', out_shape=(act, act, act, act, jax....  5.97 us

profile of v11, /device:TPU:0, one launch (start us, length us, event | category | flops | bytes accessed | tf_op | source)
XLA Modules:
  0.0 211.9 jit_solution(1852572090583649314)
XLA Ops:
  0.6 205.3 %rel_attn.1 = (bf16[8,64,8,2,128]{4,3,2,1,0:T(2,128)(2,1)S(1)}, bf16[8,64,8,2,128]{4,3,2,1,0:T(2,128)(2,1)S(1)}, bf16[8,64,8,2,128]{4,3,2,1,0:T(2,128)(2,1)S(1)}...) custom-call(bf16[8,64,8,2,128]{4,3,2,1,0:T(2,128)(2,1)} %bitcast.15,, ...), custom_call_target="tpu_custom_call" | custom-call | tf_op jit(solution)/shard_map/rel_attn/pallas_call | solution.py:499
  205.9 6.0 %writer.1 = (bf16[8,64,8,2,128]{4,3,2,1,0:T(2,128)(2,1)}, bf16[8,64,8,2,128]{4,3,2,1,0:T(2,128)(2,1)}, bf16[8,64,8,2,128]{4,3,2,1,0:T(2,128)(2,1)}, bf16[8,64,8,...) custom-call(bf16[8,64,8,2,128]{4,3,2,1,0:T(2,128)(2,1)S(1)} %get-tuple-el, ...), custom_call_target="tpu_custom_call" | custom-call | tf_op jit(solution)/shard_map/writer/pallas_call | solution.py:524

commit v12 on v11

--- a/solution.py
+++ b/solution.py
@@ -25,7 +25,7 @@
 N_PART = 6
 PART = 86
 FIN = N_PART * PART
-HOPS = ((2, 1, 4), (2, 1, 4), (1, 2, 4)) * 2
+HOPS = ((1, 2, 4), (1, 2, 4), (2, 1, 4)) * 2
 TURNS = ((1, 3, 2), (3, 1, 2))
 
 

time: 213 us -> 212 us (level)
  no operation moved by 1% of the time
where the time goes in v12:
time: 212 us
  Pallas kernels  211 us (100%)
    pallas_call x1, Pallas kernels, local(): pl.pallas_call(kernel, name='rel_attn', out_shape=(act, act, act, act, *[...  205 us
    pallas_call x1, Pallas kernels, local(): pl.pallas_call(writer, name='writer', out_shape=(act, act, act, act, jax....  5.97 us

profile of v12, /device:TPU:0, one launch (start us, length us, event | category | flops | bytes accessed | tf_op | source)
XLA Modules:
  0.0 211.9 jit_solution(4780417013022368211)
XLA Ops:
  0.6 205.3 %rel_attn.1 = (bf16[8,64,8,2,128]{4,3,2,1,0:T(2,128)(2,1)S(1)}, bf16[8,64,8,2,128]{4,3,2,1,0:T(2,128)(2,1)S(1)}, bf16[8,64,8,2,128]{4,3,2,1,0:T(2,128)(2,1)S(1)}...) custom-call(bf16[8,64,8,2,128]{4,3,2,1,0:T(2,128)(2,1)} %bitcast.15,, ...), custom_call_target="tpu_custom_call" | custom-call | tf_op jit(solution)/shard_map/rel_attn/pallas_call | solution.py:499
  205.9 6.0 %writer.1 = (bf16[8,64,8,2,128]{4,3,2,1,0:T(2,128)(2,1)}, bf16[8,64,8,2,128]{4,3,2,1,0:T(2,128)(2,1)}, bf16[8,64,8,2,128]{4,3,2,1,0:T(2,128)(2,1)}, bf16[8,64,8,...) custom-call(bf16[8,64,8,2,128]{4,3,2,1,0:T(2,128)(2,1)S(1)} %get-tuple-el, ...), custom_call_target="tpu_custom_call" | custom-call | tf_op jit(solution)/shard_map/writer/pallas_call | solution.py:524

commit v13 on v7

--- a/solution.py
+++ b/solution.py
@@ -427,6 +427,7 @@
 
     lax.fori_loop(0, SUBS + 1, sub_body, 0)
 
+    send_out(EARLY, (2, 3))
     swap_add(1)
     cross_start(1)
     cross_finish(1)
@@ -438,7 +439,8 @@
         send_out(sub, range(4))
         return carry
 
-    lax.fori_loop(EARLY, EARLY + 2, send_late, 0)
+    send_out(EARLY, (0, 1))
+    send_out(EARLY + 1, range(4))
     for p in range(2):
         hop_wait(p, 1)
         hop_start(p, 2)

time: 210 us -> 210 us (level)
  no operation moved by 1% of the time
where the time goes in v13:
time: 210 us; the launch traced here: 209 us
  Pallas kernels  209 us (100%)
    pallas_call x1, Pallas kernels, local(): pl.pallas_call(kernel, name='rel_attn', out_shape=(act, act, act, act, *[...  203 us
    pallas_call x1, Pallas kernels, local(): pl.pallas_call(writer, name='writer', out_shape=(act, act, act, act, jax....  5.97 us

profile of v13, /device:TPU:0, one launch (start us, length us, event | category | flops | bytes accessed | tf_op | source)
XLA Modules:
  0.0 209.3 jit_solution(7528720903589527820)
XLA Ops:
  0.6 202.7 %rel_attn.1 = (bf16[8,64,8,2,128]{4,3,2,1,0:T(2,128)(2,1)S(1)}, bf16[8,64,8,2,128]{4,3,2,1,0:T(2,128)(2,1)S(1)}, bf16[8,64,8,2,128]{4,3,2,1,0:T(2,128)(2,1)S(1)}...) custom-call(bf16[8,64,8,2,128]{4,3,2,1,0:T(2,128)(2,1)} %bitcast.15,, ...), custom_call_target="tpu_custom_call" | custom-call | tf_op jit(solution)/shard_map/rel_attn/pallas_call | solution.py:501
  203.4 6.0 %writer.1 = (bf16[8,64,8,2,128]{4,3,2,1,0:T(2,128)(2,1)}, bf16[8,64,8,2,128]{4,3,2,1,0:T(2,128)(2,1)}, bf16[8,64,8,2,128]{4,3,2,1,0:T(2,128)(2,1)}, bf16[8,64,8,...) custom-call(bf16[8,64,8,2,128]{4,3,2,1,0:T(2,128)(2,1)S(1)} %get-tuple-el, ...), custom_call_target="tpu_custom_call" | custom-call | tf_op jit(solution)/shard_map/writer/pallas_call | solution.py:526

commit v14 on v13

--- a/solution.py
+++ b/solution.py
@@ -25,7 +25,9 @@
 N_PART = 6
 PART = 86
 FIN = N_PART * PART
-HOPS = ((1, 2, 4), (2, 1, 4)) * 3
+TIP = 2 * ROWS
+FAR = N_PAIR - 2
+UNITS = FAR * SLOTS
 TURNS = ((1, 3, 2), (3, 1, 2))
 
 
@@ -45,12 +47,13 @@
 
 
 def kernel(q_in, k_in, v_in, g_in, r_in, u_in, w_in,
-           o_out, dq_out, dk_out, dv_out, dr0_out, dr1_out, dr2_out, dr3_out, dr4_out, dr5_out,
-           buf, rbuf, r_buf, u_buf, w_buf, st_tx, st_rx, st_ref, dr_rx, dr_rz, dr_fin, dr_acc,
+           o_out, dq_out, dk_out, dv_out, dr0_out, dr1_out, dr2_out, dr3_out, dr4_out, dr5_out, far_out,
+           buf, rbuf, r_buf, u_buf, w_buf, st_tx, st_rx, tip_st, st_ref, dr_rx, dr_rz, dr_fin, dr_acc,
            s_ref, e_ref, dp_ref, pb_ref, ds_ref, dd_ref,
            a_s, c_s, g_s, k_s, v_s, at_s, ct_s, gt_s, kt_s, vt_s, rev_s, rt_s, dkt, dvt, stage,
            in_send, in_recv, out_send, out_recv, own_sem, r_sem, up_send, up_recv, st_send, st_recv,
-           x_send, x_recv, z_send, z_recv, ring_send, ring_recv, fw_send, fw_recv):
+           x_send, x_recv, z_send, z_recv, ring_send, ring_recv, fw_send, fw_recv,
+           far_send, far_recv, tip_sem, tip_near, tip_send, ts_send, ts_recv):
     me = lax.axis_index("cp")
     core = me % 2
     chip = me // 2
@@ -63,8 +66,13 @@
     def wait_for(ref, sem):
         pltpu.make_async_copy(ref, ref, sem).wait()
 
+    y = col // 2
+    lower, upper = z == 0, z == 1
+    tip = chip == 7 * z
+    tip_base = 2 - 2 * z
+
     tables = [pltpu.make_async_copy(src, dst, r_sem.at[j]) for j, (src, dst) in enumerate(
-        ((r_in.at[:, pl.ds(2 * col, 2)], r_buf), (u_in.at[pl.ds(2 * col, 2)], u_buf), (w_in.at[pl.ds(2 * col, 2)], w_buf)))]
+        ((r_in.at[:, 2 * col], r_buf.at[0]), (r_in.at[:, 2 * col + 1], r_buf.at[1]), (u_in, u_buf), (w_in, w_buf)))]
     for copy in tables:
         copy.start()
 
@@ -100,19 +108,27 @@
             return carry
         lax.fori_loop(0, SUBS, send_sub, 0)
 
-    @pl.when(z == 0)
+    @pl.when(lower)
     def _():
         send_all((k_in, v_in, q_in, g_in))
 
-    @pl.when(z == 1)
+    @pl.when(upper)
     def _():
         send_all((q_in, g_in, k_in, v_in))
+
+    @pl.when(tip)
+    def _():
+        for t, src in enumerate((q_in, k_in, v_in, g_in)):
+            for row in range(SLOTS):
+                pltpu.make_async_remote_copy(
+                    src_ref=src.at[(1 - core) * SLOTS + row, :, pl.ds(tip_base, FAR)], dst_ref=far_out.at[t, row],
+                    send_sem=far_send, recv_sem=far_recv, device_id=(partner,), device_id_type=MESH).start()
 
     for copy in tables:
         copy.wait()
     rev = eye_rev(BF16)
     for p in range(2):
-        pair_tab = pltpu.einshape("abc->bac", r_buf[:, p])
+        pair_tab = pltpu.einshape("abc->bac", r_buf[p])
         for hh in range(PAIR):
             for blk in range(SEQ // HEAD):
                 part = pair_tab[hh, SEQ - HEAD * (blk + 1):SEQ - HEAD * blk]
@@ -129,10 +145,13 @@
             pltpu.make_async_copy(buf.at[t, sub, my_rows], acts[t].at[place], out_recv).start()
         for peer in peers():
             peer_rows = pl.ds(pl.multiple_of((peer % PLANE) * ROWS, ROWS), ROWS)
+            to_tip = (peer // 2 == 7 * z) & jnp.logical_not(tip)
             for t in which:
-                pltpu.make_async_remote_copy(
-                    src_ref=buf.at[t, sub, peer_rows], dst_ref=acts[t].at[place],
-                    send_sem=out_send, recv_sem=out_recv, device_id=(peer,), device_id_type=MESH).start()
+                @pl.when(jnp.logical_not(to_tip & (lower if t >= 2 else upper)))
+                def _():
+                    pltpu.make_async_remote_copy(
+                        src_ref=buf.at[t, sub, peer_rows], dst_ref=acts[t].at[place],
+                        send_sem=out_send, recv_sem=out_recv, device_id=(peer,), device_id_type=MESH).start()
 
     def send_up(sub):
         wait_for(buf.at[0:2, sub], in_recv.at[0, sub])
@@ -147,8 +166,8 @@
         rows = slice(start, start + HALF)
         p = sub // SLOTS
         q2 = unpack(q_ref, q_j, sub)
-        u = u_buf[p].astype(F32)
-        w = w_buf[p].astype(F32)
+        u = u_buf[2 * col + p].astype(F32)
+        w = w_buf[2 * col + p].astype(F32)
         for hh in range(PAIR):
             q32 = q2[hh].astype(F32)
             a = (q32 + u[hh:hh + 1]).astype(BF16)
@@ -304,6 +323,11 @@
                 st_tx[sub, hh, :, QB * blk:QB * (blk + 1)] = st_ref[...].T[:8]
             pltpu.make_async_remote_copy(src_ref=st_tx.at[sub, hh], dst_ref=st_rx.at[sub, hh], send_sem=st_send, recv_sem=st_recv.at[sub],
                                          device_id=(across,), device_id_type=MESH).start()
+
+            @pl.when(jnp.logical_not(tip))
+            def _():
+                pltpu.make_async_remote_copy(src_ref=st_tx.at[sub, hh, :, HALF - TIP:], dst_ref=tip_st.at[col, sub, hh], send_sem=ts_send,
+                                             recv_sem=ts_recv, device_id=(N_DEV - 2 + core,), device_id_type=MESH).start()
             return carry
 
         lax.fori_loop(0, PAIR, own, 0)
@@ -340,28 +364,102 @@
         pltpu.make_async_remote_copy(src_ref=block(p, m, bits), dst_ref=parts[m].at[side, :, head_of(p, bits)], send_sem=fw_send.at[p, m // 3],
                                      recv_sem=fw_recv.at[p, m // 3], device_id=(partner,), device_id_type=MESH).start()
 
-    def held(m, hop):
-        have = [0]
-        for bit in HOPS[m][:hop]:
-            have = have + [bits ^ bit for bits in have]
-        return have
-
     def blocks(count):
-        return parts[0].at[:, :, :count // 2]
+        return parts[0].at[:, :, :N_PART // 2 * count]
+
+    def pass_on(p, bits, hop, device):
+        for m in range(N_PART):
+            pltpu.make_async_remote_copy(
+                src_ref=block(p, m, bits), dst_ref=parts[m].at[side, :, head_of(p, bits)], send_sem=ring_send.at[p, hop],
+                recv_sem=ring_recv.at[p, hop], device_id=(device,), device_id_type=MESH).start()
+
+    def hand_over(p, bits):
+        for m in range(N_PART):
+            forward(p, m, bits)
+
+    even = chip % 2 == z
+    loaded = y != z
+    along_x, along_y = me ^ 2, me ^ 4
 
     def hop_start(p, hop):
-        for m in range(N_PART):
-            for bits in held(m, hop):
-                pltpu.make_async_remote_copy(
-                    src_ref=block(p, m, bits), dst_ref=parts[m].at[side, :, head_of(p, bits)], send_sem=ring_send.at[p, hop],
-                    recv_sem=ring_recv.at[p, hop], device_id=(me ^ (2 * HOPS[m][hop]),), device_id_type=MESH).start()
+        if hop == 0:
+            for device in (along_x, along_y, across):
+                pass_on(p, 0, 0, device)
+        if hop == 1:
+            @pl.when(even & loaded)
+            def _():
+                pass_on(p, 1, 1, along_y)
+
+            @pl.when(jnp.logical_not(even) & loaded)
+            def _():
+                pass_on(p, 2, 1, along_x)
+
+            pass_on(p, 1, 1, across)
+            pass_on(p, 2, 1, across)
+        if hop == 2:
+            @pl.when(even & loaded)
+            def _():
+                pass_on(p, 5, 2, along_y)
+
+            @pl.when(jnp.logical_not(even) & loaded)
+            def _():
+                pass_on(p, 6, 2, along_x)
+
+            @pl.when(even)
+            def _():
+                pass_on(p, 3, 2, across)
+        if hop == 3:
+            @pl.when(even)
+            def _():
+                pass_on(p, 7, 3, across)
 
     def hop_wait(p, hop):
-        wait_for(blocks(N_PART << hop), ring_recv.at[p, hop])
-        for m in range(N_PART):
-            have = held(m, hop + 1)
-            for bits in have[len(have) // 2:]:
-                forward(p, m, bits)
+        if hop == 0:
+            wait_for(blocks(3), ring_recv.at[p, 0])
+            for bits in (1, 2, 4):
+                hand_over(p, bits)
+        if hop == 1:
+            @pl.when(even)
+            def _():
+                wait_for(blocks(3), ring_recv.at[p, 1])
+                hand_over(p, 3)
+
+            @pl.when(jnp.logical_not(even))
+            def _():
+                wait_for(blocks(2), ring_recv.at[p, 1])
+            for bits in (5, 6):
+                hand_over(p, bits)
+        if hop == 2:
+            wait_for(blocks(1), ring_recv.at[p, 2])
+            hand_over(p, 7)
+        if hop == 3:
+            @pl.when(jnp.logical_not(even))
+            def _():
+                wait_for(blocks(1), ring_recv.at[p, 3])
+                hand_over(p, 3)
+
+    def sent_wait(p):
+        wait_for(blocks(3), ring_send.at[p, 0])
+
+        @pl.when(loaded)
+        def _():
+            wait_for(blocks(3), ring_send.at[p, 1])
+
+        @pl.when(jnp.logical_not(loaded))
+        def _():
+            wait_for(blocks(2), ring_send.at[p, 1])
+
+        @pl.when(even & loaded)
+        def _():
+            wait_for(blocks(2), ring_send.at[p, 2])
+
+        @pl.when(even != loaded)
+        def _():
+            wait_for(blocks(1), ring_send.at[p, 2])
+
+        @pl.when(even)
+        def _():
+            wait_for(blocks(1), ring_send.at[p, 3])
 
     def cross_finish(p):
         wait_for(dr_rz.at[p], z_recv.at[p])
@@ -377,7 +475,134 @@
         hop_start(p, 0)
         for m in range(N_PART):
             pltpu.make_async_copy(block(p, m, 0), parts[m].at[side, :, head_of(p, 0)], own_sem.at[p]).start()
-            forward(p, m, 0)
+        hand_over(p, 0)
+
+    def tip_load(unit):
+        slot, row, far = unit % 2, unit // FAR, unit % FAR
+        pair = far + tip_base
+        for t, src in enumerate((q_in, k_in, v_in, g_in)):
+            pltpu.make_async_copy(src.at[core * SLOTS + row, :, pair], r_buf.at[slot, pl.ds(TIP * t + ROWS * core, ROWS)], tip_sem.at[slot]).start()
+            pltpu.make_async_copy(far_out.at[t, row, :, far], r_buf.at[slot, pl.ds(TIP * t + ROWS * (1 - core), ROWS)], tip_sem.at[slot]).start()
+        pltpu.make_async_copy(r_in.at[:TIP, pair], r_buf.at[slot, 4 * TIP:5 * TIP], tip_sem.at[slot]).start()
+
+    def tip_done(slot):
+        wait_for(r_buf.at[slot, :TIP], tip_near.at[slot])
+        wait_for(r_buf.at[slot, :TIP], tip_send.at[slot])
+
+    def tip_group(hh, r0):
+        group = slice(TIP * hh + r0, TIP * hh + r0 + 16)
+        rel = pltpu.roll(e_ref[group, :TIP], 1 + r0, 1, stride=1, stride_axis=0)
+        ahead = lax.broadcasted_iota(jnp.int32, (16, TIP), 1) - lax.broadcasted_iota(jnp.int32, (16, TIP), 0)
+        return group, s_ref[group, :TIP] + rel, ahead <= r0
+
+    def tip_rows(hh):
+        for r0 in range(0, TIP, 16):
+            group, s, seen = tip_group(hh, r0)
+            s = jnp.where(seen, s, -jnp.inf)
+            top = jnp.max(s, axis=1, keepdims=True)
+            p = jnp.exp2((s - top) * (scale * LOG2E))
+            p = p * (1.0 / jnp.sum(p, axis=1, keepdims=True))
+            pb_ref[group, :TIP] = p.astype(BF16)
+            dp = dp_ref[group, :TIP]
+            row_dot = jnp.sum(p * dp, axis=1, keepdims=True)
+            ds = (p * (dp - row_dot) * scale).astype(BF16)
+            ds_ref[group, :TIP] = ds
+            flipped = flip8(ds.astype(F32))
+            half = [pltpu.roll(flipped[8 * j:8 * j + 8], TIP - 8 - r0 - 8 * j, 1, stride=1, stride_axis=0) for j in range(2)]
+            dd_ref[group, :TIP] = jnp.concatenate(half, axis=0).astype(BF16)
+        rows = slice(TIP * hh, TIP * (hh + 1))
+        stage[0, hh, :TIP, :] = dot(pb_ref[rows, :TIP], v_s[hh, :TIP, :]).astype(BF16)
+        dqc = dot(ds_ref[rows, :TIP], k_s[hh, :TIP, :])
+        dqr = flip8(dot(dd_ref[rows, :TIP], c_s[hh, :TIP, :]))
+        stage[1, hh, :TIP, :] = (dqc + dqr).astype(BF16)
+
+    def tip_keys(hh, stats):
+        rows = slice(TIP * hh, TIP * (hh + 1))
+        st_ref[rows, :8] = stats.T
+        for r0 in range(0, TIP, 16):
+            group, s, seen = tip_group(hh, r0)
+            p = jnp.where(seen, jnp.exp2(s * (scale * LOG2E) - st_ref[group, 0:1]), 0.0)
+            pb_ref[group, :TIP] = p.astype(BF16)
+            ds_ref[group, :TIP] = (p * (dp_ref[group, :TIP] - st_ref[group, 1:2]) * scale).astype(BF16)
+        over_rows = (((0,), (0,)), ((), ()))
+        stage[0, hh, :TIP, :] = lax.dot_general(ds_ref[rows, :TIP], a_s[hh, :TIP, :], over_rows, preferred_element_type=F32).astype(BF16)
+        stage[1, hh, :TIP, :] = lax.dot_general(pb_ref[rows, :TIP], g_s[hh, :TIP, :], over_rows, preferred_element_type=F32).astype(BF16)
+
+    def tip_unit(unit, carry):
+        slot, row, far = unit % 2, unit // FAR, unit % FAR
+        pair = far + tip_base
+        wait_for(r_buf.at[slot, :5 * TIP], tip_sem.at[slot])
+
+        @pl.when(unit + 1 < UNITS)
+        def _():
+            tip_load(unit + 1)
+
+        q2, k2, v2, g2, r2 = [pltpu.einshape("abc->bac", r_buf[slot, TIP * t:TIP * (t + 1)]) for t in range(5)]
+        u = u_buf[pair].astype(F32)
+        w = w_buf[pair].astype(F32)
+        for hh in range(PAIR):
+            rows = slice(TIP * hh, TIP * (hh + 1))
+            q32 = q2[hh].astype(F32)
+            a = (q32 + u[hh:hh + 1]).astype(BF16)
+            c = (q32 + w[hh:hh + 1]).astype(BF16)
+            falling = dot(eye_rev(BF16), r2[hh]).astype(BF16)
+            s_ref[rows, :TIP] = dot(a, k2[hh].T)
+            e_ref[rows, :TIP] = dot(c, falling.T)
+            dp_ref[rows, :TIP] = dot(g2[hh], v2[hh].T)
+            a_s[hh, :TIP, :] = a
+            c_s[hh, :TIP, :] = falling
+            g_s[hh, :TIP, :] = g2[hh]
+            k_s[hh, :TIP, :] = k2[hh]
+            v_s[hh, :TIP, :] = v2[hh]
+
+        @pl.when(lower)
+        def _():
+            for hh in range(PAIR):
+                tip_rows(hh)
+
+        @pl.when(upper)
+        def _():
+            for hh in range(PAIR):
+                tip_keys(hh, tip_st[far // 2, (far % 2) * SLOTS + row, hh])
+
+        @pl.when(unit >= 2)
+        def _():
+            tip_done(slot)
+
+        for n in range(2):
+            r_buf[slot, (5 + n) * TIP:(6 + n) * TIP] = pltpu.einshape("abc->bac", stage[n, :, :TIP, :])
+        place = (core * SLOTS + row, slice(None), pair)
+
+        def give(results):
+            for n, dst in enumerate(results):
+                pltpu.make_async_copy(r_buf.at[slot, pl.ds((5 + n) * TIP + ROWS * core, ROWS)], dst.at[place], tip_near.at[slot]).start()
+                pltpu.make_async_remote_copy(
+                    src_ref=r_buf.at[slot, pl.ds((5 + n) * TIP + ROWS * (1 - core), ROWS)], dst_ref=dst.at[place],
+                    send_sem=tip_send.at[slot], recv_sem=out_recv, device_id=(partner,), device_id_type=MESH).start()
+
+        @pl.when(lower)
+        def _():
+            give((o_out, dq_out))
+
+        @pl.when(upper)
+        def _():
+            give((dk_out, dv_out))
+        return carry
+
+    def tips(third):
+        @pl.when(tip)
+        def _():
+            if third == 0:
+                wait_for(far_out, far_recv)
+
+                @pl.when(upper)
+                def _():
+                    wait_for(tip_st, ts_recv)
+                tip_load(0)
+            lax.fori_loop(UNITS // 3 * third, UNITS // 3 * (third + 1), tip_unit, 0)
+            if third == 2:
+                tip_done(0)
+                tip_done(1)
 
     send_up(0)
 
@@ -400,19 +625,19 @@
             swap_start(1)
             cross_finish(0)
 
-        @pl.when((z == 0) & (sub < SUBS))
+        @pl.when(lower & (sub < SUBS))
         def _():
             lower_rows(sub)
 
-        @pl.when((z == 0) & (sub > 0))
+        @pl.when(lower & (sub > 0))
         def _():
             lower_theirs(sub - 1)
 
-        @pl.when((z == 0) & (sub < SUBS))
+        @pl.when(lower & (sub < SUBS))
         def _():
             lower_own(sub)
 
-        @pl.when((z == 1) & (sub < SUBS))
+        @pl.when(upper & (sub < SUBS))
         def _():
             upper_own(sub)
 
@@ -431,40 +656,57 @@
     swap_add(1)
     cross_start(1)
     cross_finish(1)
+    send_out(EARLY, (0, 1))
     for p in range(2):
         hop_wait(p, 0)
         hop_start(p, 1)
+    for p in range(2):
+        send_out(EARLY + 1 + p, range(4))
+        tips(p)
+        hop_wait(p, 1)
+        hop_start(p, 2)
 
     def send_late(sub, carry):
         send_out(sub, range(4))
         return carry
 
-    send_out(EARLY, (0, 1))
-    send_out(EARLY + 1, range(4))
-    for p in range(2):
-        hop_wait(p, 1)
-        hop_start(p, 2)
-    lax.fori_loop(EARLY + 2, SUBS, send_late, 0)
+    lax.fori_loop(EARLY + 3, SUBS, send_late, 0)
+    tips(2)
     for p in range(2):
         hop_wait(p, 2)
-
-    wait_for(buf, out_recv)
+        hop_start(p, 3)
+    for p in range(2):
+        hop_wait(p, 3)
+
     wait_for(buf.at[:, :, :HALF - ROWS], in_send)
-    wait_for(buf.at[:, :, :HALF - ROWS], out_send)
-
-    @pl.when(z == 1)
+
+    @pl.when(tip)
+    def _():
+        wait_for(buf.at[:, :, :HALF - 3 * ROWS // 2], out_recv)
+        wait_for(buf.at[:, :, :HALF - ROWS], out_send)
+        wait_for(far_out, far_send)
+
+    @pl.when(jnp.logical_not(tip))
+    def _():
+        wait_for(buf, out_recv)
+        wait_for(buf.at[:, :, :HALF - 2 * ROWS], out_send)
+
+    @pl.when(upper & jnp.logical_not(tip))
+    def _():
+        wait_for(st_tx.at[:2], ts_send)
+
+    @pl.when(upper)
     def _():
         wait_for(st_tx, st_send)
 
     for p in range(2):
         wait_for(dr_rx.at[p], x_send.at[p])
         wait_for(dr_rz.at[p], z_send.at[p])
-        wait_for(blocks(N_PART), own_sem.at[p])
-        for hop in range(3):
-            wait_for(blocks(N_PART << hop), ring_send.at[p, hop])
+        wait_for(blocks(1), own_sem.at[p])
+        sent_wait(p)
         for n in range(2):
-            wait_for(blocks(N_PART // 2 * N_PAIR), fw_send.at[p, n])
-            wait_for(blocks(N_PART // 2 * N_PAIR), fw_recv.at[p, n])
+            wait_for(blocks(N_PAIR // 2), fw_send.at[p, n])
+            wait_for(blocks(N_PAIR // 2), fw_recv.at[p, n])
 
 
 def writer(*refs):
@@ -502,13 +744,14 @@
             kernel,
             name="rel_attn",
             out_shape=(act, act, act, act,
-                       *[jax.ShapeDtypeStruct((2, PART, n_heads, 1, head_dim), F32)] * N_PART),
+                       *[jax.ShapeDtypeStruct((2, PART, n_heads, 1, head_dim), F32)] * N_PART,
+                       jax.ShapeDtypeStruct((4, SLOTS, ROWS, FAR, PAIR, HEAD), BF16)),
             in_specs=[pl.BlockSpec(memory_space=pltpu.HBM)] * 7,
-            out_specs=[whole] * (4 + N_PART),
+            out_specs=[whole] * (5 + N_PART),
             scratch_shapes=[
                 vm((4, SUBS, HALF, PAIR, HEAD), BF16), vm((2, SUBS, HALF, PAIR, HEAD), BF16),
-                vm((SEQ, 2, PAIR, HEAD), BF16), vm((2, PAIR, HEAD), BF16), vm((2, PAIR, HEAD), BF16),
-                vm((SUBS, PAIR, 8, HALF), F32), vm((SUBS, PAIR, 8, HALF), F32), vm((QB, HEAD), F32),
+                vm((2, SEQ, PAIR, HEAD), BF16), vm((N_PAIR, PAIR, HEAD), BF16), vm((N_PAIR, PAIR, HEAD), BF16),
+                vm((SUBS, PAIR, 8, HALF), F32), vm((SUBS, PAIR, 8, HALF), F32), vm((3, SUBS, PAIR, 8, TIP), F32), vm((QB, HEAD), F32),
                 vm((2, 2) + acc, F32), vm((2,) + acc, F32), vm((2, FIN, 1, HEAD), F32), vm((4, 2) + acc, F32),
                 vm((QB, SEQ), F32), vm((QB, SEQ), F32), vm((QB, SEQ), F32),
                 vm((QB, SEQ), BF16), vm((QB, SEQ), BF16), vm((QB, SEQ), BF16),
@@ -516,10 +759,11 @@
                 vm(tok_t, BF16), vm(tok_t, BF16), vm(tok_t, BF16), vm(tok_t, BF16), vm(tok_t, BF16),
                 vm((4, SEQ, HEAD), BF16), vm((4, HEAD, SEQ), BF16),
                 vm((PAIR, HEAD, HALF), F32), vm((PAIR, HEAD, HALF), F32), vm((4, PAIR, HALF, HEAD), BF16),
-                dma, dma((2, SUBS)), dma, dma, dma((2,)), dma((3,)), dma((4,)), dma((SUBS,)), dma, dma((SUBS,)),
-                dma((2,)), dma((2,)), dma((2,)), dma((2,)), dma((2, 3)), dma((2, 3)), dma((2, 2)), dma((2, 2)),
+                dma, dma((2, SUBS)), dma, dma, dma((2,)), dma((4,)), dma((4,)), dma((SUBS,)), dma, dma((SUBS,)),
+                dma((2,)), dma((2,)), dma((2,)), dma((2,)), dma((2, 4)), dma((2, 4)), dma((2, 2)), dma((2, 2)),
+                dma, dma, dma((2,)), dma((2,)), dma((2,)), dma, dma,
             ],
-            compiler_params=pltpu.CompilerParams(collective_id=0, has_side_effects=True, vmem_limit_bytes=36 * 1024 * 1024),
+            compiler_params=pltpu.CompilerParams(collective_id=0, has_side_effects=True, vmem_limit_bytes=37 * 1024 * 1024),
         )(*[pltpu.with_memory_space_constraint(x, pltpu.HBM) for x in (
             query.reshape(pairs), key_in.reshape(pairs), value.reshape(pairs), d_out.reshape(pairs),
             rel_k.reshape(SEQ, N_PAIR, PAIR, head_dim), bias_u.reshape(N_PAIR, PAIR, head_dim), bias_w.reshape(N_PAIR, PAIR, head_dim))])
@@ -531,7 +775,7 @@
             out_specs=[whole] * 7,
             scratch_shapes=[dma((6 + 2 * N_PART,))],
             compiler_params=pltpu.CompilerParams(vmem_limit_bytes=1024 * 1024),
-        )(*outs)
+        )(*outs[:-1])
         full = query.shape
         return (o.reshape(full), dq.reshape(full), dk.reshape(full), dv.reshape(full),
                 du.reshape(bias_u.shape), dw.reshape(bias_w.shape), dr.reshape(rel_k.shape))

time: 210 us -> 209 us (level)
  no operation moved by 1% of the time
where the time goes in v14:
time: 209 us; the launch traced here: 208 us
  Pallas kernels  208 us (100%)
    pallas_call x1, Pallas kernels, local(): pl.pallas_call(kernel, name='rel_attn', out_shape=(act, act, act, act, *[...  202 us
    pallas_call x1, Pallas kernels, local(): pl.pallas_call(writer, name='writer', out_shape=(act, act, act, act, jax....  5.97 us

profile of v14, /device:TPU:0, one launch (start us, length us, event | category | flops | bytes accessed | tf_op | source)
XLA Modules:
  0.0 208.5 jit_solution(5679115657758607982)
XLA Ops:
  0.6 201.7 %rel_attn.1 = (bf16[8,64,8,2,128]{4,3,2,1,0:T(2,128)(2,1)S(1)}, bf16[8,64,8,2,128]{4,3,2,1,0:T(2,128)(2,1)S(1)}, bf16[8,64,8,2,128]{4,3,2,1,0:T(2,128)(2,1)S(1)}...) custom-call(bf16[8,64,8,2,128]{4,3,2,1,0:T(2,128)(2,1)} %bitcast.15,, ...), custom_call_target="tpu_custom_call" | custom-call | tf_op jit(solution)/shard_map/rel_attn/pallas_call | solution.py:743
  202.3 6.0 %writer.1 = (bf16[8,64,8,2,128]{4,3,2,1,0:T(2,128)(2,1)}, bf16[8,64,8,2,128]{4,3,2,1,0:T(2,128)(2,1)}, bf16[8,64,8,2,128]{4,3,2,1,0:T(2,128)(2,1)}, bf16[8,64,8,...) custom-call(bf16[8,64,8,2,128]{4,3,2,1,0:T(2,128)(2,1)S(1)} %get-tuple-el, ...), custom_call_target="tpu_custom_call" | custom-call | tf_op jit(solution)/shard_map/writer/pallas_call | solution.py:770

commit v15 on v14

--- a/solution.py
+++ b/solution.py
@@ -624,6 +624,8 @@
         def _():
             swap_start(1)
             cross_finish(0)
+            swap_add(1)
+            cross_start(1)
 
         @pl.when(lower & (sub < SUBS))
         def _():
@@ -653,8 +655,6 @@
     lax.fori_loop(0, SUBS + 1, sub_body, 0)
 
     send_out(EARLY, (2, 3))
-    swap_add(1)
-    cross_start(1)
     cross_finish(1)
     send_out(EARLY, (0, 1))
     for p in range(2):

time: 209 us -> 209 us (level)
  no operation moved by 1% of the time
where the time goes in v15:
time: 209 us; the launch traced here: 208 us
  Pallas kernels  208 us (100%)
    pallas_call x1, Pallas kernels, local(): pl.pallas_call(kernel, name='rel_attn', out_shape=(act, act, act, act, *[...  202 us
    pallas_call x1, Pallas kernels, local(): pl.pallas_call(writer, name='writer', out_shape=(act, act, act, act, jax....  5.97 us

profile of v15, /device:TPU:0, one launch (start us, length us, event | category | flops | bytes accessed | tf_op | source)
XLA Modules:
  0.0 208.5 jit_solution(813460043822927446)
XLA Ops:
  0.6 201.7 %rel_attn.1 = (bf16[8,64,8,2,128]{4,3,2,1,0:T(2,128)(2,1)S(1)}, bf16[8,64,8,2,128]{4,3,2,1,0:T(2,128)(2,1)S(1)}, bf16[8,64,8,2,128]{4,3,2,1,0:T(2,128)(2,1)S(1)}...) custom-call(bf16[8,64,8,2,128]{4,3,2,1,0:T(2,128)(2,1)} %bitcast.15,, ...), custom_call_target="tpu_custom_call" | custom-call | tf_op jit(solution)/shard_map/rel_attn/pallas_call | solution.py:743
  202.3 6.0 %writer.1 = (bf16[8,64,8,2,128]{4,3,2,1,0:T(2,128)(2,1)}, bf16[8,64,8,2,128]{4,3,2,1,0:T(2,128)(2,1)}, bf16[8,64,8,2,128]{4,3,2,1,0:T(2,128)(2,1)}, bf16[8,64,8,...) custom-call(bf16[8,64,8,2,128]{4,3,2,1,0:T(2,128)(2,1)S(1)} %get-tuple-el, ...), custom_call_target="tpu_custom_call" | custom-call | tf_op jit(solution)/shard_map/writer/pallas_call | solution.py:770

commit v16 on v15

--- a/solution.py
+++ b/solution.py
@@ -623,9 +623,9 @@
         @pl.when(sub == SUBS)
         def _():
             swap_start(1)
-            cross_finish(0)
             swap_add(1)
             cross_start(1)
+            cross_finish(0)
 
         @pl.when(lower & (sub < SUBS))
         def _():
@@ -643,7 +643,7 @@
         def _():
             upper_own(sub)
 
-        @pl.when(sub < EARLY)
+        @pl.when(sub <= EARLY)
         def _():
             send_out(sub, (2, 3))
 
@@ -654,7 +654,6 @@
 
     lax.fori_loop(0, SUBS + 1, sub_body, 0)
 
-    send_out(EARLY, (2, 3))
     cross_finish(1)
     send_out(EARLY, (0, 1))
     for p in range(2):

time: 209 us -> 206 us (0.986)
  Pallas kernels: 208 us -> 205 us
    pallas_call x1, Pallas kernels: 202 us -> 199 us  [local(): pl.pallas_call(kernel, name='rel_attn', out_shape=(act, act, act, act, *[...]
where the time goes in v16:
time: 206 us
  Pallas kernels  205 us (100%)
    pallas_call x1, Pallas kernels, local(): pl.pallas_call(kernel, name='rel_attn', out_shape=(act, act, act, act, *[...  199 us
    pallas_call x1, Pallas kernels, local(): pl.pallas_call(writer, name='writer', out_shape=(act, act, act, act, jax....  5.97 us

profile of v16, /device:TPU:0, one launch (start us, length us, event | category | flops | bytes accessed | tf_op | source)
XLA Modules:
  0.0 205.8 jit_solution(14525491765874988385)
XLA Ops:
  0.6 199.1 %rel_attn.1 = (bf16[8,64,8,2,128]{4,3,2,1,0:T(2,128)(2,1)S(1)}, bf16[8,64,8,2,128]{4,3,2,1,0:T(2,128)(2,1)S(1)}, bf16[8,64,8,2,128]{4,3,2,1,0:T(2,128)(2,1)S(1)}...) custom-call(bf16[8,64,8,2,128]{4,3,2,1,0:T(2,128)(2,1)} %bitcast.15,, ...), custom_call_target="tpu_custom_call" | custom-call | tf_op jit(solution)/shard_map/rel_attn/pallas_call | solution.py:742
  199.7 6.0 %writer.1 = (bf16[8,64,8,2,128]{4,3,2,1,0:T(2,128)(2,1)}, bf16[8,64,8,2,128]{4,3,2,1,0:T(2,128)(2,1)}, bf16[8,64,8,2,128]{4,3,2,1,0:T(2,128)(2,1)}, bf16[8,64,8,...) custom-call(bf16[8,64,8,2,128]{4,3,2,1,0:T(2,128)(2,1)S(1)} %get-tuple-el, ...), custom_call_target="tpu_custom_call" | custom-call | tf_op jit(solution)/shard_map/writer/pallas_call | solution.py:769

commit v17 on v16

--- a/solution.py
+++ b/solution.py
@@ -298,7 +298,7 @@
     def lower_theirs(sub):
         wait_up(sub)
         load_rows(rbuf, 0, rbuf, 1, sub, HALF, False)
-        wait_for(st_rx.at[sub], st_recv.at[sub])
+        wait_for(st_rx.at[sub], st_recv.at[sub % 4])
 
         def theirs(hh, carry):
             head = 2 * (sub // SLOTS) + hh
@@ -321,7 +321,7 @@
             for blk in (1, 0):
                 row_block(hh, head, QB * blk, HALF + QB * blk, HALF, blk == 1, True)
                 st_tx[sub, hh, :, QB * blk:QB * (blk + 1)] = st_ref[...].T[:8]
-            pltpu.make_async_remote_copy(src_ref=st_tx.at[sub, hh], dst_ref=st_rx.at[sub, hh], send_sem=st_send, recv_sem=st_recv.at[sub],
+            pltpu.make_async_remote_copy(src_ref=st_tx.at[sub, hh], dst_ref=st_rx.at[sub, hh], send_sem=st_send, recv_sem=st_recv.at[sub % 4],
                                          device_id=(across,), device_id_type=MESH).start()
 
             @pl.when(jnp.logical_not(tip))
@@ -339,7 +339,7 @@
 
     def swap_start(p):
         for n in range(2):
-            pltpu.make_async_remote_copy(src_ref=dr_acc.at[2 * p + n, side], dst_ref=dr_rx.at[p, n], send_sem=x_send.at[p], recv_sem=x_recv.at[p],
+            pltpu.make_async_remote_copy(src_ref=dr_acc.at[2 * p + n, side], dst_ref=dr_rx.at[p, n], send_sem=x_send, recv_sem=x_recv.at[p],
                                          device_id=(partner,), device_id_type=MESH).start()
 
     def swap_add(p):
@@ -348,7 +348,7 @@
             dr_rx[p, n] = dr_rx[p, n] + dr_acc[2 * p + n, core]
 
     def cross_start(p):
-        pltpu.make_async_remote_copy(src_ref=dr_rx.at[p, 1 - z], dst_ref=dr_rz.at[p], send_sem=z_send.at[p], recv_sem=z_recv.at[p],
+        pltpu.make_async_remote_copy(src_ref=dr_rx.at[p, 1 - z], dst_ref=dr_rz.at[p], send_sem=z_send, recv_sem=z_recv.at[p],
                                      device_id=(across,), device_id_type=MESH).start()
 
     def head_of(p, bits):
@@ -361,8 +361,8 @@
         return parts[m].at[side, :, head_of(p, bits)]
 
     def forward(p, m, bits):
-        pltpu.make_async_remote_copy(src_ref=block(p, m, bits), dst_ref=parts[m].at[side, :, head_of(p, bits)], send_sem=fw_send.at[p, m // 3],
-                                     recv_sem=fw_recv.at[p, m // 3], device_id=(partner,), device_id_type=MESH).start()
+        pltpu.make_async_remote_copy(src_ref=block(p, m, bits), dst_ref=parts[m].at[side, :, head_of(p, bits)], send_sem=fw_send,
+                                     recv_sem=fw_recv, device_id=(partner,), device_id_type=MESH).start()
 
     def blocks(count):
         return parts[0].at[:, :, :N_PART // 2 * count]
@@ -370,7 +370,7 @@
     def pass_on(p, bits, hop, device):
         for m in range(N_PART):
             pltpu.make_async_remote_copy(
-                src_ref=block(p, m, bits), dst_ref=parts[m].at[side, :, head_of(p, bits)], send_sem=ring_send.at[p, hop],
+                src_ref=block(p, m, bits), dst_ref=parts[m].at[side, :, head_of(p, bits)], send_sem=ring_send,
                 recv_sem=ring_recv.at[p, hop], device_id=(device,), device_id_type=MESH).start()
 
     def hand_over(p, bits):
@@ -438,28 +438,18 @@
                 wait_for(blocks(1), ring_recv.at[p, 3])
                 hand_over(p, 3)
 
-    def sent_wait(p):
-        wait_for(blocks(3), ring_send.at[p, 0])
-
-        @pl.when(loaded)
-        def _():
-            wait_for(blocks(3), ring_send.at[p, 1])
-
-        @pl.when(jnp.logical_not(loaded))
-        def _():
-            wait_for(blocks(2), ring_send.at[p, 1])
-
+    def sent_wait():
         @pl.when(even & loaded)
         def _():
-            wait_for(blocks(2), ring_send.at[p, 2])
+            wait_for(buf.at[:3, :, :FIN * 18 // 24], ring_send)
 
         @pl.when(even != loaded)
         def _():
-            wait_for(blocks(1), ring_send.at[p, 2])
-
-        @pl.when(even)
-        def _():
-            wait_for(blocks(1), ring_send.at[p, 3])
+            wait_for(buf.at[:3, :7, :FIN * 14 // 21], ring_send)
+
+        @pl.when(jnp.logical_not(even | loaded))
+        def _():
+            wait_for(buf.at[:2, :6, :FIN * 10 // 12], ring_send)
 
     def cross_finish(p):
         wait_for(dr_rz.at[p], z_recv.at[p])
@@ -474,7 +464,7 @@
         dr_fin[p, HALF + 2:] = jnp.zeros((FIN - HALF - 2, 1, HEAD), F32)
         hop_start(p, 0)
         for m in range(N_PART):
-            pltpu.make_async_copy(block(p, m, 0), parts[m].at[side, :, head_of(p, 0)], own_sem.at[p]).start()
+            pltpu.make_async_copy(block(p, m, 0), parts[m].at[side, :, head_of(p, 0)], own_sem).start()
         hand_over(p, 0)
 
     def tip_load(unit):
@@ -698,14 +688,12 @@
     def _():
         wait_for(st_tx, st_send)
 
-    for p in range(2):
-        wait_for(dr_rx.at[p], x_send.at[p])
-        wait_for(dr_rz.at[p], z_send.at[p])
-        wait_for(blocks(1), own_sem.at[p])
-        sent_wait(p)
-        for n in range(2):
-            wait_for(blocks(N_PAIR // 2), fw_send.at[p, n])
-            wait_for(blocks(N_PAIR // 2), fw_recv.at[p, n])
+    wait_for(dr_rx, x_send)
+    wait_for(dr_rz, z_send)
+    wait_for(blocks(2), own_sem)
+    sent_wait()
+    for sem in (fw_send, fw_recv):
+        wait_for(buf.at[:3, :, :FIN * 16 // 24], sem)
 
 
 def writer(*refs):
@@ -758,8 +746,8 @@
                 vm(tok_t, BF16), vm(tok_t, BF16), vm(tok_t, BF16), vm(tok_t, BF16), vm(tok_t, BF16),
                 vm((4, SEQ, HEAD), BF16), vm((4, HEAD, SEQ), BF16),
                 vm((PAIR, HEAD, HALF), F32), vm((PAIR, HEAD, HALF), F32), vm((4, PAIR, HALF, HEAD), BF16),
-                dma, dma((2, SUBS)), dma, dma, dma((2,)), dma((4,)), dma((4,)), dma((SUBS,)), dma, dma((SUBS,)),
-                dma((2,)), dma((2,)), dma((2,)), dma((2,)), dma((2, 4)), dma((2, 4)), dma((2, 2)), dma((2, 2)),
+                dma, dma((2, SUBS)), dma, dma, dma, dma((4,)), dma((4,)), dma((SUBS,)), dma, dma((4,)),
+                dma, dma((2,)), dma, dma((2,)), dma, dma((2, 4)), dma, dma,
                 dma, dma, dma((2,)), dma((2,)), dma((2,)), dma, dma,
             ],
             compiler_params=pltpu.CompilerParams(collective_id=0, has_side_effects=True, vmem_limit_bytes=37 * 1024 * 1024),

time: 206 us -> 206 us (level)
  no operation moved by 1% of the time
where the time goes in v17:
time: 206 us
  Pallas kernels  205 us (100%)
    pallas_call x1, Pallas kernels, local(): pl.pallas_call(kernel, name='rel_attn', out_shape=(act, act, act, act, *[...  199 us
    pallas_call x1, Pallas kernels, local(): pl.pallas_call(writer, name='writer', out_shape=(act, act, act, act, jax....  5.97 us

profile of v17, /device:TPU:0, one launch (start us, length us, event | category | flops | bytes accessed | tf_op | source)
XLA Modules:
  0.0 205.6 jit_solution(17686955392854716338)
XLA Ops:
  0.6 198.9 %rel_attn.1 = (bf16[8,64,8,2,128]{4,3,2,1,0:T(2,128)(2,1)S(1)}, bf16[8,64,8,2,128]{4,3,2,1,0:T(2,128)(2,1)S(1)}, bf16[8,64,8,2,128]{4,3,2,1,0:T(2,128)(2,1)S(1)}...) custom-call(bf16[8,64,8,2,128]{4,3,2,1,0:T(2,128)(2,1)} %bitcast.15,, ...), custom_call_target="tpu_custom_call" | custom-call | tf_op jit(solution)/shard_map/rel_attn/pallas_call | solution.py:730
  199.5 6.0 %writer.1 = (bf16[8,64,8,2,128]{4,3,2,1,0:T(2,128)(2,1)}, bf16[8,64,8,2,128]{4,3,2,1,0:T(2,128)(2,1)}, bf16[8,64,8,2,128]{4,3,2,1,0:T(2,128)(2,1)}, bf16[8,64,8,...) custom-call(bf16[8,64,8,2,128]{4,3,2,1,0:T(2,128)(2,1)S(1)} %get-tuple-el, ...), custom_call_target="tpu_custom_call" | custom-call | tf_op jit(solution)/shard_map/writer/pallas_call | solution.py:757

commit v18 on v17

--- a/solution.py
+++ b/solution.py
@@ -75,12 +75,6 @@
         ((r_in.at[:, 2 * col], r_buf.at[0]), (r_in.at[:, 2 * col + 1], r_buf.at[1]), (u_in, u_buf), (w_in, w_buf)))]
     for copy in tables:
         copy.start()
-
-    barrier = pltpu.get_barrier_semaphore()
-
-    for peer in [across] + [me ^ step for step in range(PLANE - 1, 0, -1)]:
-        pl.semaphore_signal(barrier, inc=1, device_id=(peer,), device_id_type=MESH)
-    pl.semaphore_wait(barrier, PLANE)
 
     my_rows = pl.ds(pl.multiple_of((me % PLANE) * ROWS, ROWS), ROWS)
 
@@ -750,7 +744,7 @@
                 dma, dma((2,)), dma, dma((2,)), dma, dma((2, 4)), dma, dma,
                 dma, dma, dma((2,)), dma((2,)), dma((2,)), dma, dma,
             ],
-            compiler_params=pltpu.CompilerParams(collective_id=0, has_side_effects=True, vmem_limit_bytes=37 * 1024 * 1024),
+            compiler_params=pltpu.CompilerParams(has_side_effects=True, vmem_limit_bytes=37 * 1024 * 1024),
         )(*[pltpu.with_memory_space_constraint(x, pltpu.HBM) for x in (
             query.reshape(pairs), key_in.reshape(pairs), value.reshape(pairs), d_out.reshape(pairs),
             rel_k.reshape(SEQ, N_PAIR, PAIR, head_dim), bias_u.reshape(N_PAIR, PAIR, head_dim), bias_w.reshape(N_PAIR, PAIR, head_dim))])

time: 206 us -> 208 us (level)
    pallas_call x1, Pallas kernels: 199 us -> 201 us  [local(): pl.pallas_call(kernel, name='rel_attn', out_shape=(act, act, act, act, *[...]
where the time goes in v18:
time: 208 us
  Pallas kernels  207 us (100%)
    pallas_call x1, Pallas kernels, local(): pl.pallas_call(kernel, name='rel_attn', out_shape=(act, act, act, act, *[...  201 us
    pallas_call x1, Pallas kernels, local(): pl.pallas_call(writer, name='writer', out_shape=(act, act, act, act, jax....  5.97 us

profile of v18, /device:TPU:0, one launch (start us, length us, event | category | flops | bytes accessed | tf_op | source)
XLA Modules:
  0.0 208.1 jit_solution(17102465607632447518)
XLA Ops:
  0.6 201.3 %rel_attn.1 = (bf16[8,64,8,2,128]{4,3,2,1,0:T(2,128)(2,1)S(1)}, bf16[8,64,8,2,128]{4,3,2,1,0:T(2,128)(2,1)S(1)}, bf16[8,64,8,2,128]{4,3,2,1,0:T(2,128)(2,1)S(1)}...) custom-call(bf16[8,64,8,2,128]{4,3,2,1,0:T(2,128)(2,1)} %bitcast.15,, ...), custom_call_target="tpu_custom_call" | custom-call | tf_op jit(solution)/shard_map/rel_attn/pallas_call | solution.py:724
  202.0 6.0 %writer.1 = (bf16[8,64,8,2,128]{4,3,2,1,0:T(2,128)(2,1)}, bf16[8,64,8,2,128]{4,3,2,1,0:T(2,128)(2,1)}, bf16[8,64,8,2,128]{4,3,2,1,0:T(2,128)(2,1)}, bf16[8,64,8,...) custom-call(bf16[8,64,8,2,128]{4,3,2,1,0:T(2,128)(2,1)S(1)} %get-tuple-el, ...), custom_call_target="tpu_custom_call" | custom-call | tf_op jit(solution)/shard_map/writer/pallas_call | solution.py:751

commit v19 on v17

--- a/solution.py
+++ b/solution.py
@@ -85,10 +85,9 @@
     my_rows = pl.ds(pl.multiple_of((me % PLANE) * ROWS, ROWS), ROWS)
 
     def peers():
-        for near_turn, far_turn in zip(*TURNS):
-            turn = jnp.where(core == 0, near_turn, far_turn)
-            yield me ^ (2 * turn)
-            yield me ^ (2 * turn + 1)
+        first, second, third = [jnp.where(core == 0, near_turn, far_turn) for near_turn, far_turn in zip(*TURNS)]
+        for turn, other in ((first, 0), (third, 0), (first, 1), (third, 1), (second, 0), (second, 1)):
+            yield me ^ (2 * turn + other)
         yield partner
 
     def send_in(ins, sub):

time: 206 us -> 206 us (level)
  no operation moved by 1% of the time
where the time goes in v19:
time: 206 us
  Pallas kernels  205 us (100%)
    pallas_call x1, Pallas kernels, local(): pl.pallas_call(kernel, name='rel_attn', out_shape=(act, act, act, act, *[...  199 us
    pallas_call x1, Pallas kernels, local(): pl.pallas_call(writer, name='writer', out_shape=(act, act, act, act, jax....  5.97 us

profile of v19, /device:TPU:0, one launch (start us, length us, event | category | flops | bytes accessed | tf_op | source)
XLA Modules:
  0.0 205.6 jit_solution(8449257546766794096)
XLA Ops:
  0.6 198.9 %rel_attn.1 = (bf16[8,64,8,2,128]{4,3,2,1,0:T(2,128)(2,1)S(1)}, bf16[8,64,8,2,128]{4,3,2,1,0:T(2,128)(2,1)S(1)}, bf16[8,64,8,2,128]{4,3,2,1,0:T(2,128)(2,1)S(1)}...) custom-call(bf16[8,64,8,2,128]{4,3,2,1,0:T(2,128)(2,1)} %bitcast.15,, ...), custom_call_target="tpu_custom_call" | custom-call | tf_op jit(solution)/shard_map/rel_attn/pallas_call | solution.py:729
  199.5 6.0 %writer.1 = (bf16[8,64,8,2,128]{4,3,2,1,0:T(2,128)(2,1)}, bf16[8,64,8,2,128]{4,3,2,1,0:T(2,128)(2,1)}, bf16[8,64,8,2,128]{4,3,2,1,0:T(2,128)(2,1)}, bf16[8,64,8,...) custom-call(bf16[8,64,8,2,128]{4,3,2,1,0:T(2,128)(2,1)S(1)} %get-tuple-el, ...), custom_call_target="tpu_custom_call" | custom-call | tf_op jit(solution)/shard_map/writer/pallas_call | solution.py:756

commit v20 on v19

--- a/solution.py
+++ b/solution.py
@@ -84,8 +84,14 @@
 
     my_rows = pl.ds(pl.multiple_of((me % PLANE) * ROWS, ROWS), ROWS)
 
-    def peers():
-        first, second, third = [jnp.where(core == 0, near_turn, far_turn) for near_turn, far_turn in zip(*TURNS)]
+    even = chip % 2 == z
+    loaded = y != z
+
+    def peers(late=False):
+        near = core == 0
+        if late:
+            near = near & (even | jnp.logical_not(loaded))
+        first, second, third = [jnp.where(near, near_turn, far_turn) for near_turn, far_turn in zip(*TURNS)]
         for turn, other in ((first, 0), (third, 0), (first, 1), (third, 1), (second, 0), (second, 1)):
             yield me ^ (2 * turn + other)
         yield partner
@@ -138,11 +144,11 @@
 
     acts = (dk_out, dv_out, o_out, dq_out)
 
-    def send_out(sub, which):
+    def send_out(sub, which, late=False):
         place = (core * SLOTS + sub % SLOTS, slice(None), 2 * col + sub // SLOTS)
         for t in which:
             pltpu.make_async_copy(buf.at[t, sub, my_rows], acts[t].at[place], out_recv).start()
-        for peer in peers():
+        for peer in peers(late):
             peer_rows = pl.ds(pl.multiple_of((peer % PLANE) * ROWS, ROWS), ROWS)
             to_tip = (peer // 2 == 7 * z) & jnp.logical_not(tip)
             for t in which:
@@ -376,8 +382,6 @@
         for m in range(N_PART):
             forward(p, m, bits)
 
-    even = chip % 2 == z
-    loaded = y != z
     along_x, along_y = me ^ 2, me ^ 4
 
     def hop_start(p, hop):
@@ -655,7 +659,7 @@
         hop_start(p, 2)
 
     def send_late(sub, carry):
-        send_out(sub, range(4))
+        send_out(sub, range(4), True)
         return carry
 
     lax.fori_loop(EARLY + 3, SUBS, send_late, 0)

time: 206 us -> 204 us (level)
  Pallas kernels: 205 us -> 202 us
    pallas_call x1, Pallas kernels: 199 us -> 197 us  [local(): pl.pallas_call(kernel, name='rel_attn', out_shape=(act, act, act, act, *[...]
where the time goes in v20:
time: 204 us; the launch traced here: 203 us
  Pallas kernels  202 us (99%)
    pallas_call x1, Pallas kernels, local(): pl.pallas_call(kernel, name='rel_attn', out_shape=(act, act, act, act, *[...  197 us
    pallas_call x1, Pallas kernels, local(): pl.pallas_call(writer, name='writer', out_shape=(act, act, act, act, jax....  5.97 us

profile of v20, /device:TPU:0, one launch (start us, length us, event | category | flops | bytes accessed | tf_op | source)
XLA Modules:
  0.0 203.3 jit_solution(10805793347590699030)
XLA Ops:
  0.6 196.5 %rel_attn.1 = (bf16[8,64,8,2,128]{4,3,2,1,0:T(2,128)(2,1)S(1)}, bf16[8,64,8,2,128]{4,3,2,1,0:T(2,128)(2,1)S(1)}, bf16[8,64,8,2,128]{4,3,2,1,0:T(2,128)(2,1)S(1)}...) custom-call(bf16[8,64,8,2,128]{4,3,2,1,0:T(2,128)(2,1)} %bitcast.15,, ...), custom_call_target="tpu_custom_call" | custom-call | tf_op jit(solution)/shard_map/rel_attn/pallas_call | solution.py:733
  197.2 6.0 %writer.1 = (bf16[8,64,8,2,128]{4,3,2,1,0:T(2,128)(2,1)}, bf16[8,64,8,2,128]{4,3,2,1,0:T(2,128)(2,1)}, bf16[8,64,8,2,128]{4,3,2,1,0:T(2,128)(2,1)}, bf16[8,64,8,...) custom-call(bf16[8,64,8,2,128]{4,3,2,1,0:T(2,128)(2,1)S(1)} %get-tuple-el, ...), custom_call_target="tpu_custom_call" | custom-call | tf_op jit(solution)/shard_map/writer/pallas_call | solution.py:760

commit v21 on v20

--- a/solution.py
+++ b/solution.py
@@ -90,7 +90,7 @@
     def peers(late=False):
         near = core == 0
         if late:
-            near = near & (even | jnp.logical_not(loaded))
+            near = jnp.logical_not(near) & (even | jnp.logical_not(loaded))
         first, second, third = [jnp.where(near, near_turn, far_turn) for near_turn, far_turn in zip(*TURNS)]
         for turn, other in ((first, 0), (third, 0), (first, 1), (third, 1), (second, 0), (second, 1)):
             yield me ^ (2 * turn + other)

time: 204 us -> 204 us (level)
  no operation moved by 1% of the time
where the time goes in v21:
time: 204 us; the launch traced here: 203 us
  Pallas kernels  202 us (99%)
    pallas_call x1, Pallas kernels, local(): pl.pallas_call(kernel, name='rel_attn', out_shape=(act, act, act, act, *[...  197 us
    pallas_call x1, Pallas kernels, local(): pl.pallas_call(writer, name='writer', out_shape=(act, act, act, act, jax....  5.97 us

profile of v21, /device:TPU:0, one launch (start us, length us, event | category | flops | bytes accessed | tf_op | source)
XLA Modules:
  0.0 203.3 jit_solution(1694472195379092865)
XLA Ops:
  0.6 196.5 %rel_attn.1 = (bf16[8,64,8,2,128]{4,3,2,1,0:T(2,128)(2,1)S(1)}, bf16[8,64,8,2,128]{4,3,2,1,0:T(2,128)(2,1)S(1)}, bf16[8,64,8,2,128]{4,3,2,1,0:T(2,128)(2,1)S(1)}...) custom-call(bf16[8,64,8,2,128]{4,3,2,1,0:T(2,128)(2,1)} %bitcast.15,, ...), custom_call_target="tpu_custom_call" | custom-call | tf_op jit(solution)/shard_map/rel_attn/pallas_call | solution.py:733
  197.2 6.0 %writer.1 = (bf16[8,64,8,2,128]{4,3,2,1,0:T(2,128)(2,1)}, bf16[8,64,8,2,128]{4,3,2,1,0:T(2,128)(2,1)}, bf16[8,64,8,2,128]{4,3,2,1,0:T(2,128)(2,1)}, bf16[8,64,8,...) custom-call(bf16[8,64,8,2,128]{4,3,2,1,0:T(2,128)(2,1)S(1)} %get-tuple-el, ...), custom_call_target="tpu_custom_call" | custom-call | tf_op jit(solution)/shard_map/writer/pallas_call | solution.py:760

commit v22 on v21

--- a/solution.py
+++ b/solution.py
@@ -88,11 +88,12 @@
     loaded = y != z
 
     def peers(late=False):
-        near = core == 0
+        near, last = core == 0, 0
         if late:
+            last = jnp.where(near & loaded & jnp.logical_not(even), 1, 0)
             near = jnp.logical_not(near) & (even | jnp.logical_not(loaded))
         first, second, third = [jnp.where(near, near_turn, far_turn) for near_turn, far_turn in zip(*TURNS)]
-        for turn, other in ((first, 0), (third, 0), (first, 1), (third, 1), (second, 0), (second, 1)):
+        for turn, other in ((first, 0), (third, 0), (first, 1), (third, 1), (second, last), (second, 1 - last)):
             yield me ^ (2 * turn + other)
         yield partner
 

time: 204 us -> 204 us (level)
  no operation moved by 1% of the time
where the time goes in v22:
time: 204 us; the launch traced here: 203 us
  Pallas kernels  202 us (99%)
    pallas_call x1, Pallas kernels, local(): pl.pallas_call(kernel, name='rel_attn', out_shape=(act, act, act, act, *[...  197 us
    pallas_call x1, Pallas kernels, local(): pl.pallas_call(writer, name='writer', out_shape=(act, act, act, act, jax....  5.97 us

profile of v22, /device:TPU:0, one launch (start us, length us, event | category | flops | bytes accessed | tf_op | source)
XLA Modules:
  0.0 203.3 jit_solution(12849499966739717026)
XLA Ops:
  0.6 196.5 %rel_attn.1 = (bf16[8,64,8,2,128]{4,3,2,1,0:T(2,128)(2,1)S(1)}, bf16[8,64,8,2,128]{4,3,2,1,0:T(2,128)(2,1)S(1)}, bf16[8,64,8,2,128]{4,3,2,1,0:T(2,128)(2,1)S(1)}...) custom-call(bf16[8,64,8,2,128]{4,3,2,1,0:T(2,128)(2,1)} %bitcast.15,, ...), custom_call_target="tpu_custom_call" | custom-call | tf_op jit(solution)/shard_map/rel_attn/pallas_call | solution.py:734
  197.2 6.0 %writer.1 = (bf16[8,64,8,2,128]{4,3,2,1,0:T(2,128)(2,1)}, bf16[8,64,8,2,128]{4,3,2,1,0:T(2,128)(2,1)}, bf16[8,64,8,2,128]{4,3,2,1,0:T(2,128)(2,1)}, bf16[8,64,8,...) custom-call(bf16[8,64,8,2,128]{4,3,2,1,0:T(2,128)(2,1)S(1)} %get-tuple-el, ...), custom_call_target="tpu_custom_call" | custom-call | tf_op jit(solution)/shard_map/writer/pallas_call | solution.py:761

commit v23 on v21

--- a/solution.py
+++ b/solution.py
@@ -649,11 +649,12 @@
 
     cross_finish(1)
     send_out(EARLY, (0, 1))
+    send_out(EARLY + 1, (2, 3))
     for p in range(2):
         hop_wait(p, 0)
         hop_start(p, 1)
     for p in range(2):
-        send_out(EARLY + 1 + p, range(4))
+        send_out(EARLY + 1 + p, range(2 * (p + 1)))
         tips(p)
         hop_wait(p, 1)
         hop_start(p, 2)

time: 204 us -> 204 us (level)
  no operation moved by 1% of the time
where the time goes in v23:
time: 204 us
  Pallas kernels  203 us (100%)
    pallas_call x1, Pallas kernels, local(): pl.pallas_call(kernel, name='rel_attn', out_shape=(act, act, act, act, *[...  197 us
    pallas_call x1, Pallas kernels, local(): pl.pallas_call(writer, name='writer', out_shape=(act, act, act, act, jax....  5.97 us

profile of v23, /device:TPU:0, one launch (start us, length us, event | category | flops | bytes accessed | tf_op | source)
XLA Modules:
  0.0 203.9 jit_solution(11245890647540699717)
XLA Ops:
  0.6 197.1 %rel_attn.1 = (bf16[8,64,8,2,128]{4,3,2,1,0:T(2,128)(2,1)S(1)}, bf16[8,64,8,2,128]{4,3,2,1,0:T(2,128)(2,1)S(1)}, bf16[8,64,8,2,128]{4,3,2,1,0:T(2,128)(2,1)S(1)}...) custom-call(bf16[8,64,8,2,128]{4,3,2,1,0:T(2,128)(2,1)} %bitcast.15,, ...), custom_call_target="tpu_custom_call" | custom-call | tf_op jit(solution)/shard_map/rel_attn/pallas_call | solution.py:734
  197.7 6.0 %writer.1 = (bf16[8,64,8,2,128]{4,3,2,1,0:T(2,128)(2,1)}, bf16[8,64,8,2,128]{4,3,2,1,0:T(2,128)(2,1)}, bf16[8,64,8,2,128]{4,3,2,1,0:T(2,128)(2,1)}, bf16[8,64,8,...) custom-call(bf16[8,64,8,2,128]{4,3,2,1,0:T(2,128)(2,1)S(1)} %get-tuple-el, ...), custom_call_target="tpu_custom_call" | custom-call | tf_op jit(solution)/shard_map/writer/pallas_call | solution.py:761

commit v24 on v23

--- a/solution.py
+++ b/solution.py
@@ -87,10 +87,10 @@
     even = chip % 2 == z
     loaded = y != z
 
-    def peers(late=False):
+    def peers(late_sub=None):
         near = core == 0
-        if late:
-            near = jnp.logical_not(near) & (even | jnp.logical_not(loaded))
+        if late_sub is not None:
+            near = jnp.logical_not(near) & (even | jnp.logical_not(loaded) | (late_sub < SUBS - 1))
         first, second, third = [jnp.where(near, near_turn, far_turn) for near_turn, far_turn in zip(*TURNS)]
         for turn, other in ((first, 0), (third, 0), (first, 1), (third, 1), (second, 0), (second, 1)):
             yield me ^ (2 * turn + other)
@@ -144,11 +144,11 @@
 
     acts = (dk_out, dv_out, o_out, dq_out)
 
-    def send_out(sub, which, late=False):
+    def send_out(sub, which, late_sub=None):
         place = (core * SLOTS + sub % SLOTS, slice(None), 2 * col + sub // SLOTS)
         for t in which:
             pltpu.make_async_copy(buf.at[t, sub, my_rows], acts[t].at[place], out_recv).start()
-        for peer in peers(late):
+        for peer in peers(late_sub):
             peer_rows = pl.ds(pl.multiple_of((peer % PLANE) * ROWS, ROWS), ROWS)
             to_tip = (peer // 2 == 7 * z) & jnp.logical_not(tip)
             for t in which:
@@ -660,7 +660,7 @@
         hop_start(p, 2)
 
     def send_late(sub, carry):
-        send_out(sub, range(4), True)
+        send_out(sub, range(4), sub)
         return carry
 
     lax.fori_loop(EARLY + 3, SUBS, send_late, 0)

time: 204 us -> 204 us (level)
  no operation moved by 1% of the time
where the time goes in v24:
time: 204 us
  Pallas kernels  203 us (100%)
    pallas_call x1, Pallas kernels, local(): pl.pallas_call(kernel, name='rel_attn', out_shape=(act, act, act, act, *[...  197 us
    pallas_call x1, Pallas kernels, local(): pl.pallas_call(writer, name='writer', out_shape=(act, act, act, act, jax....  5.97 us

profile of v24, /device:TPU:0, one launch (start us, length us, event | category | flops | bytes accessed | tf_op | source)
XLA Modules:
  0.0 203.9 jit_solution(10074103693199180769)
XLA Ops:
  0.6 197.1 %rel_attn.1 = (bf16[8,64,8,2,128]{4,3,2,1,0:T(2,128)(2,1)S(1)}, bf16[8,64,8,2,128]{4,3,2,1,0:T(2,128)(2,1)S(1)}, bf16[8,64,8,2,128]{4,3,2,1,0:T(2,128)(2,1)S(1)}...) custom-call(bf16[8,64,8,2,128]{4,3,2,1,0:T(2,128)(2,1)} %bitcast.15,, ...), custom_call_target="tpu_custom_call" | custom-call | tf_op jit(solution)/shard_map/rel_attn/pallas_call | solution.py:734
  197.7 6.0 %writer.1 = (bf16[8,64,8,2,128]{4,3,2,1,0:T(2,128)(2,1)}, bf16[8,64,8,2,128]{4,3,2,1,0:T(2,128)(2,1)}, bf16[8,64,8,2,128]{4,3,2,1,0:T(2,128)(2,1)}, bf16[8,64,8,...) custom-call(bf16[8,64,8,2,128]{4,3,2,1,0:T(2,128)(2,1)S(1)} %get-tuple-el, ...), custom_call_target="tpu_custom_call" | custom-call | tf_op jit(solution)/shard_map/writer/pallas_call | solution.py:761

commit v25 on v22

--- a/solution.py
+++ b/solution.py
@@ -90,8 +90,9 @@
     def peers(late=False):
         near, last = core == 0, 0
         if late:
-            last = jnp.where(near & loaded & jnp.logical_not(even), 1, 0)
-            near = jnp.logical_not(near) & (even | jnp.logical_not(loaded))
+            lone = loaded & jnp.logical_not(even)
+            last = jnp.where(near & lone & upper, 1, 0)
+            near = jnp.where(lone, near & upper, jnp.logical_not(near))
         first, second, third = [jnp.where(near, near_turn, far_turn) for near_turn, far_turn in zip(*TURNS)]
         for turn, other in ((first, 0), (third, 0), (first, 1), (third, 1), (second, last), (second, 1 - last)):
             yield me ^ (2 * turn + other)

time: 204 us -> 204 us (level)
  no operation moved by 1% of the time
where the time goes in v25:
time: 204 us; the launch traced here: 203 us
  Pallas kernels  202 us (99%)
    pallas_call x1, Pallas kernels, local(): pl.pallas_call(kernel, name='rel_attn', out_shape=(act, act, act, act, *[...  197 us
    pallas_call x1, Pallas kernels, local(): pl.pallas_call(writer, name='writer', out_shape=(act, act, act, act, jax....  5.97 us

profile of v25, /device:TPU:0, one launch (start us, length us, event | category | flops | bytes accessed | tf_op | source)
XLA Modules:
  0.0 203.3 jit_solution(4603490687670185568)
XLA Ops:
  0.6 196.5 %rel_attn.1 = (bf16[8,64,8,2,128]{4,3,2,1,0:T(2,128)(2,1)S(1)}, bf16[8,64,8,2,128]{4,3,2,1,0:T(2,128)(2,1)S(1)}, bf16[8,64,8,2,128]{4,3,2,1,0:T(2,128)(2,1)S(1)}...) custom-call(bf16[8,64,8,2,128]{4,3,2,1,0:T(2,128)(2,1)} %bitcast.15,, ...), custom_call_target="tpu_custom_call" | custom-call | tf_op jit(solution)/shard_map/rel_attn/pallas_call | solution.py:735
  197.2 6.0 %writer.1 = (bf16[8,64,8,2,128]{4,3,2,1,0:T(2,128)(2,1)}, bf16[8,64,8,2,128]{4,3,2,1,0:T(2,128)(2,1)}, bf16[8,64,8,2,128]{4,3,2,1,0:T(2,128)(2,1)}, bf16[8,64,8,...) custom-call(bf16[8,64,8,2,128]{4,3,2,1,0:T(2,128)(2,1)S(1)} %get-tuple-el, ...), custom_call_target="tpu_custom_call" | custom-call | tf_op jit(solution)/shard_map/writer/pallas_call | solution.py:762

commit v26 on v25

--- a/solution.py
+++ b/solution.py
@@ -10,6 +10,7 @@
 LOG2E = 1.4426950408889634
 
 N_DEV = 16
+BOTH = range(2)
 PLANE = 8
 PAIR = 2
 N_PAIR = 8
@@ -48,7 +49,7 @@
 
 def kernel(q_in, k_in, v_in, g_in, r_in, u_in, w_in,
            o_out, dq_out, dk_out, dv_out, dr0_out, dr1_out, dr2_out, dr3_out, dr4_out, dr5_out, far_out,
-           buf, rbuf, r_buf, u_buf, w_buf, st_tx, st_rx, tip_st, st_ref, dr_rx, dr_rz, dr_fin, dr_acc,
+           buf, rbuf, r_buf, u_buf, w_buf, st_tx, st_rx, tip_tx, tip_st, st_ref, dr_rx, dr_rz, dr_fin, dr_acc,
            s_ref, e_ref, dp_ref, pb_ref, ds_ref, dd_ref,
            a_s, c_s, g_s, k_s, v_s, at_s, ct_s, gt_s, kt_s, vt_s, rev_s, rt_s, dkt, dvt, stage,
            in_send, in_recv, out_send, out_recv, own_sem, r_sem, up_send, up_recv, st_send, st_recv,
@@ -134,9 +135,9 @@
     for copy in tables:
         copy.wait()
     rev = eye_rev(BF16)
-    for p in range(2):
+    for p in BOTH:
         pair_tab = pltpu.einshape("abc->bac", r_buf[p])
-        for hh in range(PAIR):
+        for hh in BOTH:
             for blk in range(SEQ // HEAD):
                 part = pair_tab[hh, SEQ - HEAD * (blk + 1):SEQ - HEAD * blk]
                 flipped = dot(rev, part).astype(BF16)
@@ -162,7 +163,7 @@
 
     def send_up(sub):
         wait_for(buf.at[0:2, sub], in_recv.at[0, sub])
-        for j in range(2):
+        for j in BOTH:
             pltpu.make_async_remote_copy(src_ref=buf.at[j, sub], dst_ref=rbuf.at[j, sub], send_sem=up_send.at[sub % 4], recv_sem=up_recv.at[sub],
                                          device_id=(across,), device_id_type=MESH).start()
 
@@ -175,7 +176,7 @@
         q2 = unpack(q_ref, q_j, sub)
         u = u_buf[2 * col + p].astype(F32)
         w = w_buf[2 * col + p].astype(F32)
-        for hh in range(PAIR):
+        for hh in BOTH:
             q32 = q2[hh].astype(F32)
             a = (q32 + u[hh:hh + 1]).astype(BF16)
             c = (q32 + w[hh:hh + 1]).astype(BF16)
@@ -186,7 +187,7 @@
                 ct_s[hh, :, rows] = flip8(c.astype(F32)).astype(BF16).T
         g2 = unpack(g_ref, g_j, sub)
         g_s[:, rows, :] = g2
-        for hh in range(PAIR):
+        for hh in BOTH:
             gt_s[hh, :, rows] = g2[hh].T
 
     def load_keys(k_ref, k_j, v_ref, v_j, sub, start):
@@ -195,7 +196,7 @@
         v2 = unpack(v_ref, v_j, sub)
         k_s[:, rows, :] = k2
         v_s[:, rows, :] = v2
-        for hh in range(PAIR):
+        for hh in BOTH:
             kt_s[hh, :, rows] = k2[hh].T
             vt_s[hh, :, rows] = v2[hh].T
 
@@ -269,14 +270,14 @@
         dvt[hh] += dot(gt_s[hh, :, rows], pb_ref[:, :HALF])
 
     def store_rows(sub):
-        for t in range(2):
+        for t in BOTH:
             buf[2 + t, sub] = pltpu.einshape("abc->bac", stage[t])
 
     def store_keys(sub):
-        for hh in range(PAIR):
+        for hh in BOTH:
             stage[2, hh] = dkt[hh].astype(BF16).T
             stage[3, hh] = dvt[hh].astype(BF16).T
-        for t in range(2):
+        for t in BOTH:
             buf[t, sub] = pltpu.einshape("abc->bac", stage[2 + t])
 
     def wait_up(sub):
@@ -330,14 +331,20 @@
                 st_tx[sub, hh, :, QB * blk:QB * (blk + 1)] = st_ref[...].T[:8]
             pltpu.make_async_remote_copy(src_ref=st_tx.at[sub, hh], dst_ref=st_rx.at[sub, hh], send_sem=st_send, recv_sem=st_recv.at[sub % 4],
                                          device_id=(across,), device_id_type=MESH).start()
-
-            @pl.when(jnp.logical_not(tip))
-            def _():
-                pltpu.make_async_remote_copy(src_ref=st_tx.at[sub, hh, :, HALF - TIP:], dst_ref=tip_st.at[col, sub, hh], send_sem=ts_send,
-                                             recv_sem=ts_recv, device_id=(N_DEV - 2 + core,), device_id_type=MESH).start()
+            place = 2 * (sub % 2 * PAIR + hh)
+            row_id = lax.broadcasted_iota(jnp.int32, (8, TIP), 0)
+            tile = tip_tx[sub // 2]
+            for j in BOTH:
+                tile = jnp.where(row_id == place + j, st_tx[sub, hh, j:j + 1, HALF - TIP:], tile)
+            tip_tx[sub // 2] = tile
             return carry
 
         lax.fori_loop(0, PAIR, own, 0)
+
+        @pl.when(jnp.logical_not(tip) & (sub % 2 == 1))
+        def _():
+            pltpu.make_async_remote_copy(src_ref=tip_tx.at[sub // 2], dst_ref=tip_st.at[col, sub // 2], send_sem=ts_send, recv_sem=ts_recv,
+                                         device_id=(N_DEV - 2 + core,), device_id_type=MESH).start()
         store_rows(sub)
         store_keys(sub)
 
@@ -345,13 +352,13 @@
     parts = (dr0_out, dr1_out, dr2_out, dr3_out, dr4_out, dr5_out)
 
     def swap_start(p):
-        for n in range(2):
+        for n in BOTH:
             pltpu.make_async_remote_copy(src_ref=dr_acc.at[2 * p + n, side], dst_ref=dr_rx.at[p, n], send_sem=x_send, recv_sem=x_recv.at[p],
                                          device_id=(partner,), device_id_type=MESH).start()
 
     def swap_add(p):
         wait_for(dr_rx.at[p], x_recv.at[p])
-        for n in range(2):
+        for n in BOTH:
             dr_rx[p, n] = dr_rx[p, n] + dr_acc[2 * p + n, core]
 
     def cross_start(p):
@@ -511,9 +518,11 @@
         dqr = flip8(dot(dd_ref[rows, :TIP], c_s[hh, :TIP, :]))
         stage[1, hh, :TIP, :] = (dqc + dqr).astype(BF16)
 
-    def tip_keys(hh, stats):
+    def tip_keys(hh, stats, odd):
         rows = slice(TIP * hh, TIP * (hh + 1))
-        st_ref[rows, :8] = stats.T
+        by_row = stats.T
+        even_row, odd_row = [by_row[:, n:n + 2] for n in (2 * hh, 2 * (hh + PAIR))]
+        st_ref[rows, :2] = jnp.where(odd == 1, odd_row, even_row)
         for r0 in range(0, TIP, 16):
             group, s, seen = tip_group(hh, r0)
             p = jnp.where(seen, jnp.exp2(s * (scale * LOG2E) - st_ref[group, 0:1]), 0.0)
@@ -535,7 +544,7 @@
         q2, k2, v2, g2, r2 = [pltpu.einshape("abc->bac", r_buf[slot, TIP * t:TIP * (t + 1)]) for t in range(5)]
         u = u_buf[pair].astype(F32)
         w = w_buf[pair].astype(F32)
-        for hh in range(PAIR):
+        for hh in BOTH:
             rows = slice(TIP * hh, TIP * (hh + 1))
             q32 = q2[hh].astype(F32)
             a = (q32 + u[hh:hh + 1]).astype(BF16)
@@ -552,19 +561,19 @@
 
         @pl.when(lower)
         def _():
-            for hh in range(PAIR):
+            for hh in BOTH:
                 tip_rows(hh)
 
         @pl.when(upper)
         def _():
-            for hh in range(PAIR):
-                tip_keys(hh, tip_st[far // 2, (far % 2) * SLOTS + row, hh])
+            for hh in BOTH:
+                tip_keys(hh, tip_st[far // 2, (far % 2 * SLOTS + row) // 2], row % 2)
 
         @pl.when(unit >= 2)
         def _():
             tip_done(slot)
 
-        for n in range(2):
+        for n in BOTH:
             r_buf[slot, (5 + n) * TIP:(6 + n) * TIP] = pltpu.einshape("abc->bac", stage[n, :, :TIP, :])
         place = (core * SLOTS + row, slice(None), pair)
 
@@ -651,10 +660,10 @@
 
     cross_finish(1)
     send_out(EARLY, (0, 1))
-    for p in range(2):
+    for p in BOTH:
         hop_wait(p, 0)
         hop_start(p, 1)
-    for p in range(2):
+    for p in BOTH:
         send_out(EARLY + 1 + p, range(4))
         tips(p)
         hop_wait(p, 1)
@@ -666,10 +675,10 @@
 
     lax.fori_loop(EARLY + 3, SUBS, send_late, 0)
     tips(2)
-    for p in range(2):
+    for p in BOTH:
         hop_wait(p, 2)
         hop_start(p, 3)
-    for p in range(2):
+    for p in BOTH:
         hop_wait(p, 3)
 
     wait_for(buf.at[:, :, :HALF - ROWS], in_send)
@@ -687,7 +696,7 @@
 
     @pl.when(upper & jnp.logical_not(tip))
     def _():
-        wait_for(st_tx.at[:2], ts_send)
+        wait_for(tip_tx, ts_send)
 
     @pl.when(upper)
     def _():
@@ -706,7 +715,7 @@
     pairs = list(zip(ins[:4], (o, dq, dk, dv)))
     for m, part in enumerate(ins[4:]):
         rows = min(PART, HALF - PART * m)
-        for side in range(2):
+        for side in BOTH:
             start = HALF * side + PART * m
             pairs.append((part.at[side, :rows], dr.at[start:start + rows]))
     last = HALF - PART * (N_PART - 1)
@@ -743,7 +752,7 @@
             scratch_shapes=[
                 vm((4, SUBS, HALF, PAIR, HEAD), BF16), vm((2, SUBS, HALF, PAIR, HEAD), BF16),
                 vm((2, SEQ, PAIR, HEAD), BF16), vm((N_PAIR, PAIR, HEAD), BF16), vm((N_PAIR, PAIR, HEAD), BF16),
-                vm((SUBS, PAIR, 8, HALF), F32), vm((SUBS, PAIR, 8, HALF), F32), vm((3, SUBS, PAIR, 8, TIP), F32), vm((QB, HEAD), F32),
+                vm((SUBS, PAIR, 8, HALF), F32), vm((SUBS, PAIR, 8, HALF), F32), vm((SUBS // 2, 8, TIP), F32), vm((3, SUBS // 2, 8, TIP), F32), vm((QB, HEAD), F32),
                 vm((2, 2) + acc, F32), vm((2,) + acc, F32), vm((2, FIN, 1, HEAD), F32), vm((4, 2) + acc, F32),
                 vm((QB, SEQ), F32), vm((QB, SEQ), F32), vm((QB, SEQ), F32),
                 vm((QB, SEQ), BF16), vm((QB, SEQ), BF16), vm((QB, SEQ), BF16),

time: 204 us -> 204 us (level)
  no operation moved by 1% of the time
where the time goes in v26:
time: 204 us; the launch traced here: 203 us
  Pallas kernels  202 us (99%)
    pallas_call x1, Pallas kernels, local(): pl.pallas_call(kernel, name='rel_attn', out_shape=(act, act, act, act, *[...  197 us
    pallas_call x1, Pallas kernels, local(): pl.pallas_call(writer, name='writer', out_shape=(act, act, act, act, jax....  5.97 us

profile of v26, /device:TPU:0, one launch (start us, length us, event | category | flops | bytes accessed | tf_op | source)
XLA Modules:
  0.0 203.3 jit_solution(2611661967548603317)
XLA Ops:
  0.6 196.5 %rel_attn.1 = (bf16[8,64,8,2,128]{4,3,2,1,0:T(2,128)(2,1)S(1)}, bf16[8,64,8,2,128]{4,3,2,1,0:T(2,128)(2,1)S(1)}, bf16[8,64,8,2,128]{4,3,2,1,0:T(2,128)(2,1)S(1)}...) custom-call(bf16[8,64,8,2,128]{4,3,2,1,0:T(2,128)(2,1)} %bitcast.15,, ...), custom_call_target="tpu_custom_call" | custom-call | tf_op jit(solution)/shard_map/rel_attn/pallas_call | solution.py:744
  197.2 6.0 %writer.1 = (bf16[8,64,8,2,128]{4,3,2,1,0:T(2,128)(2,1)}, bf16[8,64,8,2,128]{4,3,2,1,0:T(2,128)(2,1)}, bf16[8,64,8,2,128]{4,3,2,1,0:T(2,128)(2,1)}, bf16[8,64,8,...) custom-call(bf16[8,64,8,2,128]{4,3,2,1,0:T(2,128)(2,1)S(1)} %get-tuple-el, ...), custom_call_target="tpu_custom_call" | custom-call | tf_op jit(solution)/shard_map/writer/pallas_call | solution.py:771

commit v27 on v26

--- a/solution.py
+++ b/solution.py
@@ -87,15 +87,14 @@
 
     even = chip % 2 == z
     loaded = y != z
+    lone = loaded & jnp.logical_not(even)
 
     def peers(late=False):
-        near, last = core == 0, 0
+        near = core == 0
         if late:
-            lone = loaded & jnp.logical_not(even)
-            last = jnp.where(near & lone & upper, 1, 0)
-            near = jnp.where(lone, near & upper, jnp.logical_not(near))
+            near = jnp.logical_not(near | lone)
         first, second, third = [jnp.where(near, near_turn, far_turn) for near_turn, far_turn in zip(*TURNS)]
-        for turn, other in ((first, 0), (third, 0), (first, 1), (third, 1), (second, last), (second, 1 - last)):
+        for turn, other in ((first, 0), (third, 0), (first, 1), (third, 1), (second, 0), (second, 1)):
             yield me ^ (2 * turn + other)
         yield partner
 
@@ -660,11 +659,21 @@
 
     cross_finish(1)
     send_out(EARLY, (0, 1))
+
+    @pl.when(lone)
+    def _():
+        send_out(EARLY + 1, (2, 3))
+
     for p in BOTH:
         hop_wait(p, 0)
         hop_start(p, 1)
+
+    @pl.when(jnp.logical_not(lone))
+    def _():
+        send_out(EARLY + 1, (2, 3))
+
     for p in BOTH:
-        send_out(EARLY + 1 + p, range(4))
+        send_out(EARLY + 1 + p, range(2 * (p + 1)))
         tips(p)
         hop_wait(p, 1)
         hop_start(p, 2)

time: 204 us -> 205 us (level)
  no operation moved by 1% of the time
where the time goes in v27:
time: 205 us; the launch traced here: 203 us
  Pallas kernels  202 us (99%)
    pallas_call x1, Pallas kernels, local(): pl.pallas_call(kernel, name='rel_attn', out_shape=(act, act, act, act, *[...  197 us
    pallas_call x1, Pallas kernels, local(): pl.pallas_call(writer, name='writer', out_shape=(act, act, act, act, jax....  5.97 us

profile of v27, /device:TPU:0, one launch (start us, length us, event | category | flops | bytes accessed | tf_op | source)
XLA Modules:
  0.0 203.3 jit_solution(4943077573547752616)
XLA Ops:
  0.6 196.5 %rel_attn.1 = (bf16[8,64,8,2,128]{4,3,2,1,0:T(2,128)(2,1)S(1)}, bf16[8,64,8,2,128]{4,3,2,1,0:T(2,128)(2,1)S(1)}, bf16[8,64,8,2,128]{4,3,2,1,0:T(2,128)(2,1)S(1)}...) custom-call(bf16[8,64,8,2,128]{4,3,2,1,0:T(2,128)(2,1)} %bitcast.15,, ...), custom_call_target="tpu_custom_call" | custom-call | tf_op jit(solution)/shard_map/rel_attn/pallas_call | solution.py:753
  197.2 6.0 %writer.1 = (bf16[8,64,8,2,128]{4,3,2,1,0:T(2,128)(2,1)}, bf16[8,64,8,2,128]{4,3,2,1,0:T(2,128)(2,1)}, bf16[8,64,8,2,128]{4,3,2,1,0:T(2,128)(2,1)}, bf16[8,64,8,...) custom-call(bf16[8,64,8,2,128]{4,3,2,1,0:T(2,128)(2,1)S(1)} %get-tuple-el, ...), custom_call_target="tpu_custom_call" | custom-call | tf_op jit(solution)/shard_map/writer/pallas_call | solution.py:780

commit v28 on v27

--- a/solution.py
+++ b/solution.py
@@ -668,12 +668,17 @@
         hop_wait(p, 0)
         hop_start(p, 1)
 
+    @pl.when(lone)
+    def _():
+        send_out(EARLY + 1, BOTH)
+
     @pl.when(jnp.logical_not(lone))
     def _():
-        send_out(EARLY + 1, (2, 3))
+        send_out(EARLY + 1, range(4))
 
     for p in BOTH:
-        send_out(EARLY + 1 + p, range(2 * (p + 1)))
+        if p:
+            send_out(EARLY + 2, range(4))
         tips(p)
         hop_wait(p, 1)
         hop_start(p, 2)

time: 205 us -> 203 us (level)
  no operation moved by 1% of the time
where the time goes in v28:
time: 203 us
  Pallas kernels  202 us (100%)
    pallas_call x1, Pallas kernels, local(): pl.pallas_call(kernel, name='rel_attn', out_shape=(act, act, act, act, *[...  197 us
    pallas_call x1, Pallas kernels, local(): pl.pallas_call(writer, name='writer', out_shape=(act, act, act, act, jax....  5.97 us

profile of v28, /device:TPU:0, one launch (start us, length us, event | category | flops | bytes accessed | tf_op | source)
XLA Modules:
  0.0 203.3 jit_solution(16561595104281829698)
XLA Ops:
  0.6 196.5 %rel_attn.1 = (bf16[8,64,8,2,128]{4,3,2,1,0:T(2,128)(2,1)S(1)}, bf16[8,64,8,2,128]{4,3,2,1,0:T(2,128)(2,1)S(1)}, bf16[8,64,8,2,128]{4,3,2,1,0:T(2,128)(2,1)S(1)}...) custom-call(bf16[8,64,8,2,128]{4,3,2,1,0:T(2,128)(2,1)} %bitcast.15,, ...), custom_call_target="tpu_custom_call" | custom-call | tf_op jit(solution)/shard_map/rel_attn/pallas_call | solution.py:758
  197.2 6.0 %writer.1 = (bf16[8,64,8,2,128]{4,3,2,1,0:T(2,128)(2,1)}, bf16[8,64,8,2,128]{4,3,2,1,0:T(2,128)(2,1)}, bf16[8,64,8,2,128]{4,3,2,1,0:T(2,128)(2,1)}, bf16[8,64,8,...) custom-call(bf16[8,64,8,2,128]{4,3,2,1,0:T(2,128)(2,1)S(1)} %get-tuple-el, ...), custom_call_target="tpu_custom_call" | custom-call | tf_op jit(solution)/shard_map/writer/pallas_call | solution.py:785

commit v29 on v28

--- a/solution.py
+++ b/solution.py
@@ -11,6 +11,7 @@
 
 N_DEV = 16
 BOTH = range(2)
+ALL = range(4)
 PLANE = 8
 PAIR = 2
 N_PAIR = 8
@@ -53,8 +54,8 @@
            s_ref, e_ref, dp_ref, pb_ref, ds_ref, dd_ref,
            a_s, c_s, g_s, k_s, v_s, at_s, ct_s, gt_s, kt_s, vt_s, rev_s, rt_s, dkt, dvt, stage,
            in_send, in_recv, out_send, out_recv, own_sem, r_sem, up_send, up_recv, st_send, st_recv,
-           x_send, x_recv, z_send, z_recv, ring_send, ring_recv, fw_send, fw_recv,
-           far_send, far_recv, tip_sem, tip_near, tip_send, ts_send, ts_recv):
+           x_recv, z_recv, ring_send, ring_recv, fw_send, fw_recv,
+           far_send, far_recv, tip_sem, tip_send, ts_recv):
     me = lax.axis_index("cp")
     core = me % 2
     chip = me // 2
@@ -342,7 +343,7 @@
 
         @pl.when(jnp.logical_not(tip) & (sub % 2 == 1))
         def _():
-            pltpu.make_async_remote_copy(src_ref=tip_tx.at[sub // 2], dst_ref=tip_st.at[col, sub // 2], send_sem=ts_send, recv_sem=ts_recv,
+            pltpu.make_async_remote_copy(src_ref=tip_tx.at[sub // 2], dst_ref=tip_st.at[col, sub // 2], send_sem=st_send, recv_sem=ts_recv,
                                          device_id=(N_DEV - 2 + core,), device_id_type=MESH).start()
         store_rows(sub)
         store_keys(sub)
@@ -352,7 +353,7 @@
 
     def swap_start(p):
         for n in BOTH:
-            pltpu.make_async_remote_copy(src_ref=dr_acc.at[2 * p + n, side], dst_ref=dr_rx.at[p, n], send_sem=x_send, recv_sem=x_recv.at[p],
+            pltpu.make_async_remote_copy(src_ref=dr_acc.at[2 * p + n, side], dst_ref=dr_rx.at[p, n], send_sem=fw_send, recv_sem=x_recv.at[p],
                                          device_id=(partner,), device_id_type=MESH).start()
 
     def swap_add(p):
@@ -361,7 +362,7 @@
             dr_rx[p, n] = dr_rx[p, n] + dr_acc[2 * p + n, core]
 
     def cross_start(p):
-        pltpu.make_async_remote_copy(src_ref=dr_rx.at[p, 1 - z], dst_ref=dr_rz.at[p], send_sem=z_send, recv_sem=z_recv.at[p],
+        pltpu.make_async_remote_copy(src_ref=dr_rx.at[p, 1 - z], dst_ref=dr_rz.at[p], send_sem=fw_send, recv_sem=z_recv.at[p],
                                      device_id=(across,), device_id_type=MESH).start()
 
     def head_of(p, bits):
@@ -487,8 +488,7 @@
         pltpu.make_async_copy(r_in.at[:TIP, pair], r_buf.at[slot, 4 * TIP:5 * TIP], tip_sem.at[slot]).start()
 
     def tip_done(slot):
-        wait_for(r_buf.at[slot, :TIP], tip_near.at[slot])
-        wait_for(r_buf.at[slot, :TIP], tip_send.at[slot])
+        wait_for(r_buf.at[slot, :2 * TIP], tip_send.at[slot])
 
     def tip_group(hh, r0):
         group = slice(TIP * hh + r0, TIP * hh + r0 + 16)
@@ -578,7 +578,7 @@
 
         def give(results):
             for n, dst in enumerate(results):
-                pltpu.make_async_copy(r_buf.at[slot, pl.ds((5 + n) * TIP + ROWS * core, ROWS)], dst.at[place], tip_near.at[slot]).start()
+                pltpu.make_async_copy(r_buf.at[slot, pl.ds((5 + n) * TIP + ROWS * core, ROWS)], dst.at[place], tip_send.at[slot]).start()
                 pltpu.make_async_remote_copy(
                     src_ref=r_buf.at[slot, pl.ds((5 + n) * TIP + ROWS * (1 - core), ROWS)], dst_ref=dst.at[place],
                     send_sem=tip_send.at[slot], recv_sem=out_recv, device_id=(partner,), device_id_type=MESH).start()
@@ -674,17 +674,17 @@
 
     @pl.when(jnp.logical_not(lone))
     def _():
-        send_out(EARLY + 1, range(4))
+        send_out(EARLY + 1, ALL)
 
     for p in BOTH:
         if p:
-            send_out(EARLY + 2, range(4))
+            send_out(EARLY + 2, ALL)
         tips(p)
         hop_wait(p, 1)
         hop_start(p, 2)
 
     def send_late(sub, carry):
-        send_out(sub, range(4), True)
+        send_out(sub, ALL, True)
         return carry
 
     lax.fori_loop(EARLY + 3, SUBS, send_late, 0)
@@ -708,20 +708,18 @@
         wait_for(buf, out_recv)
         wait_for(buf.at[:, :, :HALF - 2 * ROWS], out_send)
 
+    @pl.when(upper & tip)
+    def _():
+        wait_for(st_tx, st_send)
+
     @pl.when(upper & jnp.logical_not(tip))
     def _():
-        wait_for(tip_tx, ts_send)
-
-    @pl.when(upper)
-    def _():
-        wait_for(st_tx, st_send)
-
-    wait_for(dr_rx, x_send)
-    wait_for(dr_rz, z_send)
+        wait_for(buf.at[0, :2, :272], st_send)
+
     wait_for(blocks(2), own_sem)
     sent_wait()
-    for sem in (fw_send, fw_recv):
-        wait_for(buf.at[:3, :, :FIN * 16 // 24], sem)
+    wait_for(buf.at[:3, :, :480], fw_send)
+    wait_for(buf.at[:3, :, :FIN * 16 // 24], fw_recv)
 
 
 def writer(*refs):
@@ -775,8 +773,8 @@
                 vm((4, SEQ, HEAD), BF16), vm((4, HEAD, SEQ), BF16),
                 vm((PAIR, HEAD, HALF), F32), vm((PAIR, HEAD, HALF), F32), vm((4, PAIR, HALF, HEAD), BF16),
                 dma, dma((2, SUBS)), dma, dma, dma, dma((4,)), dma((4,)), dma((SUBS,)), dma, dma((4,)),
-                dma, dma((2,)), dma, dma((2,)), dma, dma((2, 4)), dma, dma,
-                dma, dma, dma((2,)), dma((2,)), dma((2,)), dma, dma,
+                dma((2,)), dma((2,)), dma, dma((2, 4)), dma, dma,
+                dma, dma, dma((2,)), dma((2,)), dma,
             ],
             compiler_params=pltpu.CompilerParams(collective_id=0, has_side_effects=True, vmem_limit_bytes=37 * 1024 * 1024),
         )(*[pltpu.with_memory_space_constraint(x, pltpu.HBM) for x in (

time: 203 us -> 203 us (level)
  no operation moved by 1% of the time
where the time goes in v29:
time: 203 us
  Pallas kernels  202 us (100%)
    pallas_call x1, Pallas kernels, local(): pl.pallas_call(kernel, name='rel_attn', out_shape=(act, act, act, act, *[...  196 us
    pallas_call x1, Pallas kernels, local(): pl.pallas_call(writer, name='writer', out_shape=(act, act, act, act, jax....  5.97 us

profile of v29, /device:TPU:0, one launch (start us, length us, event | category | flops | bytes accessed | tf_op | source)
XLA Modules:
  0.0 203.2 jit_solution(1099251432998413958)
XLA Ops:
  0.6 196.5 %rel_attn.1 = (bf16[8,64,8,2,128]{4,3,2,1,0:T(2,128)(2,1)S(1)}, bf16[8,64,8,2,128]{4,3,2,1,0:T(2,128)(2,1)S(1)}, bf16[8,64,8,2,128]{4,3,2,1,0:T(2,128)(2,1)S(1)}...) custom-call(bf16[8,64,8,2,128]{4,3,2,1,0:T(2,128)(2,1)} %bitcast.15,, ...), custom_call_target="tpu_custom_call" | custom-call | tf_op jit(solution)/shard_map/rel_attn/pallas_call | solution.py:756
  197.1 6.0 %writer.1 = (bf16[8,64,8,2,128]{4,3,2,1,0:T(2,128)(2,1)}, bf16[8,64,8,2,128]{4,3,2,1,0:T(2,128)(2,1)}, bf16[8,64,8,2,128]{4,3,2,1,0:T(2,128)(2,1)}, bf16[8,64,8,...) custom-call(bf16[8,64,8,2,128]{4,3,2,1,0:T(2,128)(2,1)S(1)} %get-tuple-el, ...), custom_call_target="tpu_custom_call" | custom-call | tf_op jit(solution)/shard_map/writer/pallas_call | solution.py:783

commit v30 on v29

--- a/solution.py
+++ b/solution.py
@@ -164,7 +164,7 @@
     def send_up(sub):
         wait_for(buf.at[0:2, sub], in_recv.at[0, sub])
         for j in BOTH:
-            pltpu.make_async_remote_copy(src_ref=buf.at[j, sub], dst_ref=rbuf.at[j, sub], send_sem=up_send.at[sub % 4], recv_sem=up_recv.at[sub],
+            pltpu.make_async_remote_copy(src_ref=buf.at[j, sub], dst_ref=rbuf.at[j, sub], send_sem=up_send.at[sub % 3], recv_sem=up_recv.at[sub],
                                          device_id=(across,), device_id_type=MESH).start()
 
     def unpack(ref, j, sub):
@@ -282,7 +282,7 @@
 
     def wait_up(sub):
         wait_for(rbuf.at[:, sub], up_recv.at[sub])
-        wait_for(rbuf.at[:, sub], up_send.at[sub % 4])
+        wait_for(rbuf.at[:, sub], up_send.at[sub % 3])
 
     def wait_in(sub):
         wait_for(buf.at[2:4, sub], in_recv.at[1, sub])
@@ -306,7 +306,7 @@
     def lower_theirs(sub):
         wait_up(sub)
         load_rows(rbuf, 0, rbuf, 1, sub, HALF, False)
-        wait_for(st_rx.at[sub], st_recv.at[sub % 4])
+        wait_for(st_rx.at[sub], st_recv.at[sub % 3])
 
         def theirs(hh, carry):
             head = 2 * (sub // SLOTS) + hh
@@ -329,7 +329,7 @@
             for blk in (1, 0):
                 row_block(hh, head, QB * blk, HALF + QB * blk, HALF, blk == 1, True)
                 st_tx[sub, hh, :, QB * blk:QB * (blk + 1)] = st_ref[...].T[:8]
-            pltpu.make_async_remote_copy(src_ref=st_tx.at[sub, hh], dst_ref=st_rx.at[sub, hh], send_sem=st_send, recv_sem=st_recv.at[sub % 4],
+            pltpu.make_async_remote_copy(src_ref=st_tx.at[sub, hh], dst_ref=st_rx.at[sub, hh], send_sem=st_send, recv_sem=st_recv.at[sub % 3],
                                          device_id=(across,), device_id_type=MESH).start()
             place = 2 * (sub % 2 * PAIR + hh)
             row_id = lax.broadcasted_iota(jnp.int32, (8, TIP), 0)
@@ -772,7 +772,7 @@
                 vm(tok_t, BF16), vm(tok_t, BF16), vm(tok_t, BF16), vm(tok_t, BF16), vm(tok_t, BF16),
                 vm((4, SEQ, HEAD), BF16), vm((4, HEAD, SEQ), BF16),
                 vm((PAIR, HEAD, HALF), F32), vm((PAIR, HEAD, HALF), F32), vm((4, PAIR, HALF, HEAD), BF16),
-                dma, dma((2, SUBS)), dma, dma, dma, dma((4,)), dma((4,)), dma((SUBS,)), dma, dma((4,)),
+                dma, dma((2, SUBS)), dma, dma, dma, dma((4,)), dma((3,)), dma((SUBS,)), dma, dma((3,)),
                 dma((2,)), dma((2,)), dma, dma((2, 4)), dma, dma,
                 dma, dma, dma((2,)), dma((2,)), dma,
             ],

time: 203 us -> 203 us (level)
  no operation moved by 1% of the time
where the time goes in v30:
time: 203 us
  Pallas kernels  202 us (100%)
    pallas_call x1, Pallas kernels, local(): pl.pallas_call(kernel, name='rel_attn', out_shape=(act, act, act, act, *[...  196 us
    pallas_call x1, Pallas kernels, local(): pl.pallas_call(writer, name='writer', out_shape=(act, act, act, act, jax....  5.97 us

profile of v30, /device:TPU:0, one launch (start us, length us, event | category | flops | bytes accessed | tf_op | source)
XLA Modules:
  0.0 203.2 jit_solution(16187500739571852644)
XLA Ops:
  0.6 196.4 %rel_attn.1 = (bf16[8,64,8,2,128]{4,3,2,1,0:T(2,128)(2,1)S(1)}, bf16[8,64,8,2,128]{4,3,2,1,0:T(2,128)(2,1)S(1)}, bf16[8,64,8,2,128]{4,3,2,1,0:T(2,128)(2,1)S(1)}...) custom-call(bf16[8,64,8,2,128]{4,3,2,1,0:T(2,128)(2,1)} %bitcast.15,, ...), custom_call_target="tpu_custom_call" | custom-call | tf_op jit(solution)/shard_map/rel_attn/pallas_call | solution.py:756
  197.1 6.0 %writer.1 = (bf16[8,64,8,2,128]{4,3,2,1,0:T(2,128)(2,1)}, bf16[8,64,8,2,128]{4,3,2,1,0:T(2,128)(2,1)}, bf16[8,64,8,2,128]{4,3,2,1,0:T(2,128)(2,1)}, bf16[8,64,8,...) custom-call(bf16[8,64,8,2,128]{4,3,2,1,0:T(2,128)(2,1)S(1)} %get-tuple-el, ...), custom_call_target="tpu_custom_call" | custom-call | tf_op jit(solution)/shard_map/writer/pallas_call | solution.py:783
